TPU v7x, 32 devices: a whole 2x2x4 slice. The times are simulated.
32 devices in a mesh: pages: 8 (over y, x, core), heads: 4 (over z).
Axes of the slice: x: 2, y: 2, z: 4, core: 2. Of those that a mesh axis runs over, the one named last changes fastest.
Arguments:
- queries: bfloat16 [512, 32, 128], P('pages', 'heads'), may hold values from -6 to 6
- keys: bfloat16 [576, 16, 128, 128], P('pages', 'heads'), may hold values from -6 to 6
- values: bfloat16 [576, 16, 128, 128], P('pages', 'heads'), may hold values from -6 to 6
- hot_pages: int32 [64], replicated, may hold values from 0 to 575, as said below
- hot_used: int32 [512], replicated, may hold values from 1 to 64
- user_pages: int32 [512, 1], P('pages'), may hold values from 8 to 71, as said below
- lengths: int32 [512], P('pages'), may hold values from 1 to 128
- o_weight: bfloat16 [4096, 4608], P('heads'), may hold values from -0.09375 to 0.09375
- residual: bfloat16 [512, 4608], P(('pages', 'heads')), may hold values from -6 to 6
- norm_gain: float32 [4608], replicated, may hold values from 0.25 to 1.75
Outputs:
- output: bfloat16 [512, 4608], P(('pages', 'heads'))
Inputs may be any that keep to these rules, and one draw needn't show every extreme that they name: `hot_pages`: 64 distinct pages; each lies among the first 8 pages of its group (page p belongs to group p // 72); one group holds exactly 8 of them and none holds more. `user_pages`: numbers within the sequence's own group (sequence s belongs to group s // 64); all own pages of the sequences of one group are distinct.
All inputs are finite; a program needn't handle non-finite values.
Results may differ from a plain program's by a relative error of at most 0.019.
Values may be sent and summed in bfloat16 or wider, within the bound.
No kernel may reach another device: no remote copies, remote signals or barrier semaphores. Data moves between devices by JAX's collectives and lax.ppermute only.
A program may use at most 128 MiB of HBM per device.

v0:
```python
import jax
import jax.numpy as jnp
from jax import lax
from jax.sharding import PartitionSpec as P

HOT_CAP = 8


score_scale = 1.0 / 12.0
soft_cap = 50.0
epsilon = 1e-06


def shared_terms(grouped, page_keys, page_values, allowed):
    logits = jnp.einsum("skgd,pktd->skgpt", grouped, page_keys, preferred_element_type=jnp.float32)
    weight = jnp.exp(soft_cap * jnp.tanh(logits * (score_scale / soft_cap)))
    weight = jnp.where(allowed[:, None, None, :, None], weight, 0.0)
    numerator = jnp.einsum(
        "skgpt,pktd->skgd",
        weight.astype(jnp.bfloat16),
        page_values,
        preferred_element_type=jnp.float32,
    )
    return (numerator, jnp.sum(weight, axis=(3, 4)))


def own_terms(grouped, owned_keys, owned_values, lengths):
    logits = jnp.einsum(
        "skgd,suktd->skgut", grouped, owned_keys, preferred_element_type=jnp.float32
    )
    page_len = owned_keys.shape[3]
    token_pos = (
        jnp.arange(owned_keys.shape[1], dtype=jnp.int32)[:, None] * page_len
        + jnp.arange(page_len, dtype=jnp.int32)[None, :]
    )
    allowed = token_pos[None, :, :] < lengths[:, None, None]
    weight = jnp.exp(soft_cap * jnp.tanh(logits * (score_scale / soft_cap)))
    weight = jnp.where(allowed[:, None, None, :, :], weight, 0.0)
    numerator = jnp.einsum(
        "skgut,suktd->skgd",
        weight.astype(jnp.bfloat16),
        owned_values,
        preferred_element_type=jnp.float32,
    )
    return (numerator, jnp.sum(weight, axis=(3, 4)))


def slot_places(page_ids, hot_pages):
    hot_order = jnp.arange(hot_pages.shape[0], dtype=jnp.int32)
    matches = page_ids[:, None] == hot_pages[None, :]
    present = jnp.any(matches, axis=1)
    position = jnp.sum(jnp.where(matches, hot_order[None, :], 0), axis=1)
    return (present, position)


def per_device(
    queries, keys, values, hot_pages, hot_used, user_pages, lengths, o_weight, residual, norm_gain
):
    seq_dev, head_count, head_dim = queries.shape
    kv_heads = keys.shape[1]
    group_size = head_count // kv_heads
    page_count = keys.shape[0]
    grouped = queries.reshape(seq_dev, kv_heads, group_size, head_dim)
    myself = lax.axis_index("pages")
    hot_keys = keys[:HOT_CAP]
    hot_values = values[:HOT_CAP]
    everyone = lax.all_gather(queries, "pages", axis=0, tiled=True)
    page_ids = myself * page_count + jnp.arange(HOT_CAP, dtype=jnp.int32)
    present, position = slot_places(page_ids, hot_pages)
    allowed = present[None, :] & (position[None, :] < hot_used[:, None])
    everyone_grouped = everyone.reshape(everyone.shape[0], kv_heads, group_size, head_dim)
    numerator, totals = shared_terms(everyone_grouped, hot_keys, hot_values, allowed)
    numerator, totals = (
        lax.psum_scatter(
            numerator.astype(jnp.bfloat16), "pages", scatter_dimension=0, tiled=True
        ).astype(jnp.float32),
        lax.psum_scatter(
            totals.astype(jnp.bfloat16), "pages", scatter_dimension=0, tiled=True
        ).astype(jnp.float32),
    )
    owned_keys = keys[user_pages]
    owned_values = values[user_pages]
    own_numerator, own_totals = own_terms(grouped, owned_keys, owned_values, lengths)
    attended = ((numerator + own_numerator) / (totals + own_totals)[:, :, :, None]).astype(
        jnp.bfloat16
    )
    attended = attended.reshape(seq_dev, head_count * head_dim)
    projected = lax.psum_scatter(
        jnp.dot(attended, o_weight, preferred_element_type=jnp.float32).astype(jnp.bfloat16),
        "heads",
        scatter_dimension=0,
        tiled=True,
    ).astype(jnp.float32)
    mean_sq = jnp.mean(projected * projected, axis=1, keepdims=True)
    normed = projected / jnp.sqrt(mean_sq + epsilon) * norm_gain[None, :]
    return (residual.astype(jnp.float32) + normed).astype(jnp.bfloat16)


def solution(mesh):
    in_specs = (
        P("pages", "heads", None),
        P("pages", "heads", None, None),
        P("pages", "heads", None, None),
        P(),
        P(),
        P("pages", None),
        P("pages"),
        P("heads", None),
        P(("pages", "heads"), None),
        P(),
    )
    out_specs = P(("pages", "heads"), None)
    return jax.shard_map(
        per_device, mesh=mesh, in_specs=in_specs, out_specs=out_specs, check_vma=False
    )
```

profile of v0, /device:TPU:0, one launch (start us, length us, event | category | flops | bytes accessed | tf_op | source)
XLA Modules:
  0.0 159.2 jit_solution(6237646934203751264)
XLA Ops:
  6.5 0.0 all-gather.2.cloned.1.call-start
  6.5 0.7 all-gather.2.cloned.1.call-update
  7.3 0.0 reduce-scatter.10.cloned.1.call-start
  7.3 0.7 fusion.27
  8.0 9.2 %gather_fusion = bf16[64,4,128,128]{3,2,1,0:T(8,128)(2,1)} fusion(bf16[72,4,128,128]{3,2,1,0:T(8,128)(2,1)} %param.11, s32[1024]{0:T(1024)S(1)} %pad_clamp_fusion), kind=kCustom, calls=%fused_computation | custom fusion | bytes 16777472 | tf_op jit(solution)/shard_map/gather | solution.py:81
  17.2 0.0 copy-start.5
  17.2 0.0 copy-start.3
  17.2 9.4 %gather_fusion.1 = bf16[64,4,128,128]{3,2,1,0:T(8,128)(2,1)} fusion(bf16[72,4,128,128]{3,2,1,0:T(8,128)(2,1)} %param.12, s32[1024]{0:T(1024)S(1)} %pad_clamp_fusion), kind=kCustom, calls=%fused_computation.1 | custom fusion | bytes 16777472 | tf_op jit(solution)/shard_map/gather | solution.py:82
  26.6 0.0 copy-done.5
  26.6 0.2 compare_reduce_fusion
  26.8 0.2 fusion.26
  26.9 0.0 copy-done.3
  26.9 0.1 compare_and_fusion
  27.0 8.3 %all-gather.2.cloned.1.call-done = bf16[512,8,128]{2,1,0:T(8,128)(2,1)} async-done(((bf16[64,8,128]{2,1,0:T(8,128)(2,1)}), bf16[512,8,128]{2,1,0:T(8,128)(2,1)}) %all-gather.2.cloned.1.call-update) | async-done | bytes 1048592 | tf_op jit(solution)/shard_map/all_gather | solution.py:67
  35.3 1.4 copy.39
  36.7 9.5 %fusion = (bf16[512,4,2]{0,2,1:T(2,128)(2,1)S(1)}, f32[4,8,128,512,2]{3,2,4,1,0:T(8,128)}) fusion(pred[512,8]{0,1:T(8,128)(4,1)S(1)} %compare_and_fusion, bf16[512,4,2,128,1]{3,0,2,4,1:T(8,128)(2,1)S(1)} %bitcast.55, bf16[72,4,128,128]{3,2,1,0:T(8,128)(2,1)} %param.11), kind=kOutput, calls=%fused_computation.3 | convolution fusion | flops 1090514944 | bytes 18886656 | tf_op jit(solution)/shard_map/skgd,pktd->skgpt/dot_general | solution.py:15
  46.2 0.8 copy.55
  47.0 0.0 reduce-scatter.10.cloned.1.call-update
  47.0 0.0 reduce-scatter.6.cloned.1.call-start
  47.1 0.0 copy-start.4
  47.1 0.0 copy-start.1
  47.1 10.1 %fusion.7 = bf16[512,4,2,128]{3,0,2,1:T(8,128)(2,1)} fusion(f32[4,8,128,512,2]{3,2,4,1,0:T(8,128)} %get-tuple-element.8, pred[512,8]{0,1:T(8,128)(4,1)S(1)} %compare_and_fusion, bf16[72,4,128,128]{3,2,1,0:T(8,128)(2,1)} %param.12), kind=kOutput, calls=%fused_computation.9 | convolution fusion | flops 1091043328 | bytes 18878464 | tf_op jit(solution)/shard_map/skgpt,pktd->skgd/dot_general | solution.py:18
  57.2 0.0 reduce-scatter.6.cloned.1.call-update
  57.2 0.2 reduce-scatter.8.cloned.1.call-start
  57.5 0.0 copy-done.4
  57.5 0.1 iota_compare_fusion
  57.5 0.0 copy-done.1
  57.5 8.0 %fusion.31 = (f32[64,4,2]{2,1,0:T(4,128)S(1)}, bf16[64,4,2,128]{3,2,1,0:T(2,128)(2,1)S(1)}) fusion(bf16[64,4,128,128]{3,2,1,0:T(8,128)(2,1)} %gather_fusion, bf16[64,4,2,128]{3,2,1,0:T(2,128)(2,1)S(1)} %bitcast.56, pred[64,128]{1,0:T(8,128)(4,1)S(1)} %iota_compare_fusion), kind=kOutput, calls=%fused_computation.45 | convolution fusion | flops 17104384 | bytes 8660992 | tf_op jit(solution)/shard_map/skgd,suktd->skgut/dot_general | solution.py:28
  65.5 0.1 copy.44
  65.6 5.7 %fusion.24 = f32[64,4,2,128]{3,2,1,0:T(2,128)S(1)} fusion(bf16[64,4,128,128]{3,2,1,0:T(8,128)(2,1)} %gather_fusion.1, bf16[64,4,2,128]{3,2,1,0:T(2,128)(2,1)S(1)} %get-tuple-element.6), kind=kOutput, calls=%fused_computation.29 | convolution fusion | flops 16777216 | bytes 8781824 | tf_op jit(solution)/shard_map/skgut,suktd->skgd/dot_general | solution.py:39
  71.3 0.0 copy-start
  71.3 0.0 copy-start.2
  71.3 9.6 %reduce-scatter.10.cloned.1.call-done = bf16[64,8]{1,0:T(8,128)(2,1)} async-done(((bf16[512,8]{1,0:T(8,128)(2,1)}), bf16[64,8]{1,0:T(8,128)(2,1)}) %reduce-scatter.10.cloned.1.call-update) | async-done | bytes 1040
  80.9 0.8 copy.56
  81.7 38.4 %reduce-scatter.6.cloned.1.call-done = bf16[64,4,2,128]{3,0,2,1:T(8,128)(2,1)} async-done(((bf16[512,4,2,128]{3,0,2,1:T(8,128)(2,1)}), bf16[64,4,2,128]{3,0,2,1:T(8,128)(2,1)}) %reduce-scatter.6.cloned.1.call-update) | async-done | bytes 131088 | tf_op jit(solution)/shard_map/reduce_scatter | solution.py:74
  120.1 1.0 fusion.23
  121.1 0.1 copy.46
  121.3 0.1 reshape.104
  121.3 6.2 %convolution_convert_fusion = bf16[64,4608]{1,0:T(8,128)(2,1)} fusion(bf16[64,1024]{1,0:T(8,128)(2,1)S(1)} %reshape.104, bf16[1024,4608]{1,0:T(8,128)(2,1)} %param.17), kind=kOutput, calls=%fused_computation.7 | convolution fusion | flops 604274688 | bytes 10158080 | tf_op jit(solution)/shard_map/dot_general | solution.py:89
  127.6 0.0 reduce-scatter.8.cloned.1.call-update
  127.6 22.3 %reduce-scatter.8.cloned.1.call-done = bf16[16,4608]{1,0:T(8,128)(2,1)} async-done(((bf16[64,4608]{1,0:T(8,128)(2,1)}), bf16[16,4608]{1,0:T(8,128)(2,1)}) %reduce-scatter.8.cloned.1.call-update) | async-done | bytes 147472 | tf_op jit(solution)/shard_map/reduce_scatter | solution.py:88
  149.9 1.1 fusion.18
  151.0 0.0 copy-done
  151.0 0.0 copy-done.2
  151.0 1.7 %fusion.21 = bf16[16,4608]{1,0:T(8,128)(2,1)} fusion(bf16[16,4608]{1,0:T(8,128)(2,1)} %reduce-scatter.8.cloned.1.call-done, bf16[16,4608]{1,0:T(8,128)(2,1)S(1)} %copy-done, f32[4608]{0:T(1024)S(1)} %copy-done.2, f32[16]{0:T(128)S(1)} %add_sqrt_fusion), kind=kLoop, calls=%fused_computation.25 | loop fusion | flops 442368 | bytes 460864 | tf_op jit(solution)/shard_map/convert_element_type | solution.py:96
  (6 shorter events, 0.0 us)
Async XLA Ops:
  6.5 28.8 %all-gather.2.cloned.1.call-start = ((), (), s32[]{:S(2)}) async-start(), calls=%async_computation.3 | async-start | bytes 1179648 | tf_op jit(solution)/shard_map/all_gather | solution.py:67
  7.3 73.7 %reduce-scatter.10.cloned.1.call-start = ((), (), s32[]{:S(2)}) async-start(), calls=%async_computation.6 | async-start | bytes 147456
  17.2 9.4 %copy-start.5 = (s32[64]{0:T(128)S(1)}, s32[64]{0:T(128)}, u32[]{:S(2)}) copy-start(s32[64]{0:T(128)} %param.13) | copy-start | bytes 772
  17.2 9.8 %copy-start.3 = (s32[512]{0:T(512)S(1)}, s32[512]{0:T(512)}, u32[]{:S(2)}) copy-start(s32[512]{0:T(512)} %param.14) | copy-start | bytes 6148
  47.0 73.0 %reduce-scatter.6.cloned.1.call-start = ((), (), s32[]{:S(2)}) async-start(), calls=%async_computation.4 | async-start | bytes 1179648 | tf_op jit(solution)/shard_map/reduce_scatter | solution.py:74
  47.1 10.4 %copy-start.4 = (s32[64]{0:T(128)S(1)}, s32[64]{0:T(128)}, u32[]{:S(2)}) copy-start(s32[64]{0:T(128)} %param.16) | copy-start | bytes 772
  47.1 10.4 %copy-start.1 = (bf16[64,8,128]{2,1,0:T(8,128)(2,1)S(1)}, bf16[64,8,128]{2,1,0:T(8,128)(2,1)}, u32[]{:S(2)}) copy-start(bf16[64,8,128]{2,1,0:T(8,128)(2,1)} %param.10) | copy-start | bytes 393220
  57.2 92.7 %reduce-scatter.8.cloned.1.call-start = ((), (), s32[]{:S(2)}) async-start(), calls=%async_computation.5 | async-start | bytes 737280 | tf_op jit(solution)/shard_map/reduce_scatter | solution.py:88
  71.3 79.7 %copy-start = (bf16[16,4608]{1,0:T(8,128)(2,1)S(1)}, bf16[16,4608]{1,0:T(8,128)(2,1)}, u32[]{:S(2)}) copy-start(bf16[16,4608]{1,0:T(8,128)(2,1)} %param.18) | copy-start | bytes 442372
  71.3 79.7 %copy-start.2 = (f32[4608]{0:T(1024)S(1)}, f32[4608]{0:T(1024)}, u32[]{:S(2)}) copy-start(f32[4608]{0:T(1024)} %param.19) | copy-start | bytes 55300
Sparse Core Ops, SparseCore 0:
  9.2 26.0 all-gather.1
  47.2 33.6 reduce-scatter.9
  84.1 35.9 reduce-scatter.5
  127.7 22.1 reduce-scatter.7
where the time goes:
time: 160 us; the launch traced here: 159 us
  waiting for transfers between devices  79.3 us (50%)
  matrix products  39.5 us (25%)
  local copies, waits for them, and re-layouts  21.9 us (14%)
  between operations  13.2 us (8%)
  other arithmetic  5 us (3%)
    reduce_scatter x1, waiting for transfers between devices, per_device(): lax.psum_scatter(numerator.astype(jnp.bfloat16), 'pages', scatter_dimensi...  38.4 us
    reduce_scatter x1, waiting for transfers between devices, per_device(): lax.psum_scatter(jnp.dot(attended, o_weight, preferred_element_type=jnp.f...  22.3 us
    unnamed x5, waiting for transfers between devices  10.3 us
    dot_general x1, matrix products, shared_terms(): jnp.einsum('skgpt,pktd->skgd', weight.astype(jnp.bfloat16), page_values,...  10.1 us
    dot_general x1, matrix products, shared_terms(): jnp.einsum('skgd,pktd->skgpt', grouped, page_keys, preferred_element_type...  9.5 us
    gather x1, local copies, waits for them, and re-layouts, per_device(): owned_values = values[user_pages]  9.39 us
    gather x1, local copies, waits for them, and re-layouts, per_device(): owned_keys = keys[user_pages]  9.2 us
    all_gather x1, waiting for transfers between devices, per_device(): everyone = lax.all_gather(queries, 'pages', axis=0, tiled=True)  8.32 us
  transfers between devices with their start and end apart: 4, of which 4 were waited for; matrix products, arithmetic and copies ran while one was open for 28% of the time, Pallas kernels for 0%

commit v1 on v0

v1 whole, which is shorter than its diff:
```python
import functools
import math

import jax
import jax.numpy as jnp
from jax import lax
from jax.experimental import pallas as pl
from jax.experimental.pallas import tpu as pltpu
from jax.sharding import PartitionSpec as P

HOT_CAP = 8
score_scale = 1.0 / 12.0
soft_cap = 50.0
epsilon = 1e-06
inner = score_scale / soft_cap
outer = soft_cap * math.log2(math.e)
MIB = 1 << 20


def weights_of(logits):
    return jnp.exp2(outer * jnp.tanh(logits * inner))


def dot_t(a, b):
    return lax.dot_general(a, b, (((1,), (1,)), ((), ())), preferred_element_type=jnp.float32)


def dot_n(a, b):
    return lax.dot_general(a, b, (((1,), (0,)), ((), ())), preferred_element_type=jnp.float32)


def own_kernel(
    seqs, ups, heads, group, kv_heads, unroll,
    pages_ref, lengths_ref, q_ref, keys_ref, values_ref, num_ref, tot_ref, kbuf, vbuf, ksem, vsem,
):
    page_len, head_dim = kbuf.shape[2], kbuf.shape[3]
    width = kv_heads * page_len

    def copies(i):
        page = pages_ref[i]
        return (
            pltpu.make_async_copy(keys_ref.at[page], kbuf.at[i], ksem.at[i]),
            pltpu.make_async_copy(values_ref.at[page], vbuf.at[i], vsem.at[i]),
        )

    def start(i, carry):
        for copy in copies(i):
            copy.start()
        return carry

    lax.fori_loop(0, seqs * ups, start, 0)
    column = lax.broadcasted_iota(jnp.int32, (heads, width), 1)
    row = lax.broadcasted_iota(jnp.int32, (heads, width), 0)
    mine = (column // page_len) == (row // group)
    token = column % page_len
    ones = jnp.ones((width, head_dim), jnp.bfloat16)

    def block(b, carry):
        for j in range(unroll):
            for u in range(ups):
                for copy in copies((b * unroll + j) * ups + u):
                    copy.wait()
        for j in range(unroll):
            s = b * unroll + j
            q = q_ref[pl.ds(pl.multiple_of(s * heads, heads), heads), :]
            total = jnp.zeros((heads, 2 * head_dim), jnp.float32)
            for u in range(ups):
                k = kbuf[s * ups + u].reshape(width, head_dim)
                v = vbuf[s * ups + u].reshape(width, head_dim)
                allowed = mine & (token + u * page_len < lengths_ref[s])
                weight = jnp.where(allowed, weights_of(dot_t(q, k)), 0.0).astype(jnp.bfloat16)
                total = total + dot_n(weight, jnp.concatenate([v, ones], axis=1))
            num_ref[pl.ds(s, heads, stride=seqs), :] = total[:, :head_dim]
            tot_ref[pl.ds(s, heads, stride=seqs), :] = total[:, head_dim:]
        return carry

    lax.fori_loop(0, seqs // unroll, block, 0)


def own_terms(q, keys, values, user_pages, lengths):
    seqs, ups = user_pages.shape
    _, kv_heads, page_len, head_dim = keys.shape
    group = q.shape[1] // kv_heads
    heads = -(-q.shape[1] // 8) * 8
    q = jnp.pad(q, ((0, 0), (0, heads - q.shape[1]), (0, 0))).reshape(seqs * heads, head_dim)
    unroll = math.gcd(seqs, 16)
    any_space = pl.BlockSpec(memory_space=pltpu.HBM)
    whole = pl.BlockSpec(memory_space=pltpu.VMEM)
    out = jax.ShapeDtypeStruct((heads * seqs, head_dim), jnp.float32)
    count = seqs * ups
    buf = pltpu.VMEM((count, kv_heads, page_len, head_dim), jnp.bfloat16)
    return pl.pallas_call(
        functools.partial(own_kernel, seqs, ups, heads, group, kv_heads, unroll),
        out_shape=(out, out),
        in_specs=[pl.BlockSpec(memory_space=pltpu.SMEM)] * 2 + [whole, any_space, any_space],
        out_specs=(whole, whole),
        scratch_shapes=[buf, buf, pltpu.SemaphoreType.DMA((count,)), pltpu.SemaphoreType.DMA((count,))],
        compiler_params=pltpu.CompilerParams(vmem_limit_bytes=24 * MIB),
        name="own_pages",
    )(
        user_pages.reshape(count),
        lengths,
        q,
        pltpu.with_memory_space_constraint(keys, pltpu.HBM),
        pltpu.with_memory_space_constraint(values, pltpu.HBM),
    )


def hot_kernel(sources, seqs, heads, kv_heads, packed, pos_ref, *refs):
    used = refs[:sources]
    queries = refs[sources : 2 * sources]
    halves = (refs[2 * sources : 2 * sources + 2], refs[2 * sources + 2 : 2 * sources + 4])
    outs = refs[2 * sources + 4 : -2]
    staged, totals = refs[-2:]
    group = heads // kv_heads
    h = pl.program_id(0)
    cap, _, page_len, head_dim = halves[0][0].shape
    lane = lax.broadcasted_iota(jnp.int32, (seqs, head_dim), 1)

    @pl.when(h == 0)
    def _():
        for r in range(sources):
            staged[r] = queries[r][...].astype(jnp.float32)
        totals[...] = jnp.zeros_like(totals)

    rows = [
        staged[r, pl.ds(h * group + g, seqs, stride=heads), :].astype(jnp.bfloat16)
        for r in range(sources)
        for g in range(group)
    ]
    q = jnp.concatenate(rows, axis=0)
    used_rows = [u[...] for u in used]
    step = math.gcd(cap, 4)
    ones = jnp.ones((step * page_len, head_dim), jnp.bfloat16)
    acc = jnp.zeros((q.shape[0], 2 * head_dim), jnp.float32)
    for half, (k_ref, v_ref) in enumerate(halves):
        for c in range(0, cap, step):
            k = k_ref[c : c + step].reshape(step * page_len, head_dim)
            v = v_ref[c : c + step].reshape(step * page_len, head_dim)
            weight = weights_of(dot_t(q, k))
            parts = []
            for p in range(step):
                place = pos_ref[half * cap + c + p]
                masks = [u > place for u in used_rows for _ in range(group)]
                part = [
                    jnp.where(m, weight[i * seqs : (i + 1) * seqs, p * page_len : (p + 1) * page_len], 0.0)
                    for i, m in enumerate(masks)
                ]
                parts.append(jnp.concatenate(part, axis=0).astype(jnp.bfloat16))
            acc = acc + dot_n(jnp.concatenate(parts, axis=1), jnp.concatenate([v, ones], axis=1))
    for r in range(sources):
        for g in range(group):
            i = r * group + g
            head = h * group + g
            num = acc[i * seqs : (i + 1) * seqs, :head_dim]
            tot = acc[i * seqs : (i + 1) * seqs, head_dim:]
            if packed:
                rest = tot - tot.astype(jnp.bfloat16).astype(jnp.float32)
                outs[r][head] = num.astype(jnp.bfloat16)
                totals[r] = jnp.where(lane == head, tot, jnp.where(lane == heads + head, rest, totals[r]))
            else:
                outs[2 * r][pl.ds(pl.multiple_of(head * seqs, seqs), seqs), :] = num
                outs[2 * r + 1][pl.ds(pl.multiple_of(head * seqs, seqs), seqs), :] = tot
    if packed:

        @pl.when(h == kv_heads - 1)
        def _():
            for r in range(sources):
                outs[r][heads] = totals[r].astype(jnp.bfloat16)


def hot_terms(queries, used, position, own_kv, partner_kv, packed):
    sources = len(queries)
    seqs = used[0].shape[0]
    _, kv_heads, page_len, head_dim = own_kv[0].shape
    heads = queries[0].shape[0] // seqs
    kv_spec = pl.BlockSpec((HOT_CAP, 1, page_len, head_dim), lambda h, *_: (0, h, 0, 0))

    def fixed(shape):
        return pl.BlockSpec(shape, lambda h, *_: (0,) * len(shape))

    if packed:
        shapes = [((heads + 1, seqs, head_dim), jnp.bfloat16)] * sources
    else:
        shapes = [((heads * seqs, head_dim), jnp.float32)] * (2 * sources)
    return pl.pallas_call(
        functools.partial(hot_kernel, sources, seqs, heads, kv_heads, packed),
        out_shape=[jax.ShapeDtypeStruct(*s) for s in shapes],
        grid_spec=pltpu.PrefetchScalarGridSpec(
            num_scalar_prefetch=1,
            grid=(kv_heads,),
            in_specs=[fixed(u.shape) for u in used]
            + [fixed(q.shape) for q in queries]
            + [kv_spec] * 4,
            out_specs=[fixed(s[0]) for s in shapes],
            scratch_shapes=[
                pltpu.VMEM((sources, seqs * heads, head_dim), jnp.float32),
                pltpu.VMEM((sources, seqs, head_dim), jnp.float32),
            ],
        ),
        compiler_params=pltpu.CompilerParams(
            dimension_semantics=("arbitrary",), vmem_limit_bytes=20 * MIB
        ),
        name="hot_pages",
    )(position, *used, *queries, *own_kv, *partner_kv)


def project_kernel(received, seqs, heads, ways, z_ref, *refs):
    blocks = refs[:received]
    own_num, own_tot, hot_num, hot_tot, w_ref = refs[received : received + 5]
    outs = refs[received + 5 : received + 5 + ways]
    spread, att = refs[-2:]
    head_dim = own_num.shape[1]
    rows = seqs // ways

    @pl.when(pl.program_id(0) == 0)
    def _():
        far = jnp.zeros((seqs, head_dim), jnp.float32)
        for b in blocks:
            far = far + b[heads].astype(jnp.float32)
        for h in range(heads):
            part = pl.ds(h * seqs, seqs)
            num = own_num[part, :] + hot_num[part, :]
            tot = own_tot[part, :] + hot_tot[part, :]
            for b in blocks:
                num = num + b[h].astype(jnp.float32)
            if blocks:
                tot = tot + (far[:, h : h + 1] + far[:, heads + h : heads + h + 1])
            spread[:, h * head_dim : (h + 1) * head_dim] = num / tot
        for k in range(ways):
            target = lax.rem(z_ref[0] + k, ways)
            att[k * rows : (k + 1) * rows, :] = spread[
                pl.ds(pl.multiple_of(target * rows, rows), rows), :
            ].astype(jnp.bfloat16).astype(jnp.float32)

    res = dot_n(att[...].astype(jnp.bfloat16), w_ref[...])
    for k in range(ways):
        outs[k][...] = res[k * rows : (k + 1) * rows].astype(outs[k].dtype)


def project(blocks, own, hot, o_weight, z, ways):
    head_dim = own[0].shape[1]
    width, model = o_weight.shape
    heads = width // head_dim
    seqs = hot[0].shape[0] // heads
    rows = seqs // ways
    tile = math.gcd(model, 768)

    def fixed(x):
        return pl.BlockSpec(x.shape, lambda n, *_: (0,) * x.ndim)

    kinds = [jnp.float32] + [jnp.bfloat16] * (ways - 1)
    return pl.pallas_call(
        functools.partial(project_kernel, len(blocks), seqs, heads, ways),
        out_shape=[jax.ShapeDtypeStruct((rows, model), kind) for kind in kinds],
        grid_spec=pltpu.PrefetchScalarGridSpec(
            num_scalar_prefetch=1,
            grid=(model // tile,),
            in_specs=[fixed(b) for b in blocks]
            + [fixed(x) for x in (*own, *hot)]
            + [pl.BlockSpec((width, tile), lambda n, *_: (0, n))],
            out_specs=[pl.BlockSpec((rows, tile), lambda n, *_: (0, n))] * ways,
            scratch_shapes=[
                pltpu.VMEM((seqs, width), jnp.float32),
                pltpu.VMEM((seqs, width), jnp.float32),
            ],
        ),
        compiler_params=pltpu.CompilerParams(
            dimension_semantics=("arbitrary",), vmem_limit_bytes=20 * MIB
        ),
        name="project",
    )(z, *blocks, *own, *hot, o_weight)


def norm_kernel(*refs):
    parts, (residual, gain, out) = refs[:-3], refs[-3:]
    projected = parts[0][...]
    for p in parts[1:]:
        projected = projected + p[...].astype(jnp.float32)
    mean_sq = jnp.mean(projected * projected, axis=1, keepdims=True)
    normed = projected / jnp.sqrt(mean_sq + epsilon) * gain[...]
    out[...] = (residual[...].astype(jnp.float32) + normed).astype(jnp.bfloat16)


def finish(parts, residual, norm_gain):
    return pl.pallas_call(
        norm_kernel,
        out_shape=jax.ShapeDtypeStruct(residual.shape, residual.dtype),
        compiler_params=pltpu.CompilerParams(vmem_limit_bytes=8 * MIB),
        name="finish",
    )(*parts, residual, norm_gain.reshape(1, -1))


def per_device(
    chips, ways, queries, keys, values, hot_pages, hot_used, user_pages, lengths, o_weight, residual, norm_gain
):
    seqs, heads, head_dim = queries.shape
    page_count = keys.shape[0]
    me = lax.axis_index("pages")
    z = lax.axis_index("heads")
    devices = 2 * chips
    swap = [(i, i ^ 1) for i in range(devices)]
    power = chips & (chips - 1) == 0

    def there(i, k):
        return i ^ (2 * k) if power else (i + 2 * k) % devices

    q = queries.reshape(seqs * heads, head_dim)
    out_perm = [[(i, there(i, k)) for i in range(devices)] for k in range(chips)]
    back_perm = [[(j, i) for i, j in perm] for perm in out_perm]
    far_q = [lax.ppermute(q, "pages", out_perm[k]) for k in range(1, chips)]
    own_kv = (keys[:HOT_CAP], values[:HOT_CAP])
    partner_kv = tuple(lax.ppermute(x, "pages", swap) for x in own_kv)

    slot = jnp.arange(2 * HOT_CAP, dtype=jnp.int32)
    holder = jnp.where(slot < HOT_CAP, me, me ^ 1)
    page_ids = holder * page_count + slot % HOT_CAP
    matches = page_ids[:, None] == hot_pages[None, :]
    order = jnp.arange(hot_pages.shape[0], dtype=jnp.int32)
    absent = jnp.int32(jnp.iinfo(jnp.int32).max)
    position = jnp.min(jnp.where(matches, order[None, :], absent), axis=1)
    used_all = hot_used.reshape(devices, seqs)

    def used_of(k):
        origin = me ^ (2 * k) if power else lax.rem(me + devices - 2 * k, devices)
        row = lax.dynamic_index_in_dim(used_all, origin, 0, keepdims=False)
        return jnp.broadcast_to(row[:, None], (seqs, head_dim))

    own = own_terms(queries, keys, values, user_pages, lengths)
    blocks = []
    if chips > 1:
        own, far_q = lax.optimization_barrier((own, far_q))
        sent = hot_terms(
            far_q, [used_of(k) for k in range(1, chips)], position, own_kv, partner_kv, True
        )
        blocks = [lax.ppermute(sent[k - 1], "pages", back_perm[k]) for k in range(1, chips)]
        q, sent = lax.optimization_barrier((q, sent))
    hot = hot_terms([q], [used_of(0)], position, own_kv, partner_kv, False)
    parts = project(blocks, own, hot, o_weight, z.reshape(1), ways)
    arrived = [parts[0]] + [
        lax.ppermute(parts[k], "heads", [(i, (i + k) % ways) for i in range(ways)])
        for k in range(1, ways)
    ]
    return finish(arrived, residual, norm_gain)


def solution(mesh):
    in_specs = (
        P("pages", "heads", None),
        P("pages", "heads", None, None),
        P("pages", "heads", None, None),
        P(),
        P(),
        P("pages", None),
        P("pages"),
        P("heads", None),
        P(("pages", "heads"), None),
        P(),
    )
    out_specs = P(("pages", "heads"), None)
    body = functools.partial(per_device, mesh.shape["pages"] // 2, mesh.shape["heads"])
    return jax.shard_map(body, mesh=mesh, in_specs=in_specs, out_specs=out_specs, check_vma=False)
```

time: 160 us -> 63.4 us (0.40)
  waiting for transfers between devices: 79.3 us -> 9.14 us
  matrix products: 39.5 us -> 0 us
  Pallas kernels: 0 us -> 27.4 us
  starting transfers between devices: 0.31 us -> 14.2 us
  between operations: 13.2 us -> 0.13 us
  local copies, waits for them, and re-layouts: 21.9 us -> 11.2 us
  other arithmetic: 5 us -> 0.19 us
    reduce_scatter x2 -> x0, waiting for transfers between devices: 60.7 us -> none  [the longest x1 38.4 us: per_device(): lax.psum_scatter(numerator.astype(jnp.bfloat16), 'pages', scatter_dimensi...]
    dot_general x5 -> x0, matrix products: 39.5 us -> none  [the longest x1 10.1 us: shared_terms(): jnp.einsum('skgpt,pktd->skgd', weight.astype(jnp.bfloat16), page_values,...]
    pallas_call x0 -> x5, Pallas kernels: none -> 27.4 us  [the longest x2 12.6 us: hot_terms(): pl.pallas_call(functools.partial(hot_kernel, sources, seqs, heads, kv_hea...]
    gather x2 -> x0, local copies, waits for them, and re-layouts: 18.6 us -> none  [the longest x1 9.39 us: per_device(): owned_values = values[user_pages]]
    ppermute x0 -> x11, starting transfers between devices: none -> 14.2 us  [the longest x3 5.57 us: per_device(): lax.ppermute(parts[k], 'heads', [(i, (i + k) % ways) for i in range(ways)])]
    unnamed x5 -> x0, waiting for transfers between devices: 10.3 us -> none
    ppermute x0 -> x11, waiting for transfers between devices: none -> 9.14 us  [the longest x3 6.7 us: per_device(): lax.ppermute(parts[k], 'heads', [(i, (i + k) % ways) for i in range(ways)])]
    all_gather x1 -> x0, waiting for transfers between devices: 8.32 us -> none  [per_device(): everyone = lax.all_gather(queries, 'pages', axis=0, tiled=True)]
  transfers between devices with their start and end apart: 4 -> 11, of which waited for: 4 -> 3; matrix products, arithmetic and copies ran while one was open for 28% -> 4% of each run, Pallas kernels for 0% -> 23%
where the time goes in v1:
time: 63.4 us; the launch traced here: 62.2 us
  Pallas kernels  27.4 us (43%)
  starting transfers between devices  14.2 us (22%)
  local copies, waits for them, and re-layouts  11.2 us (18%)
  waiting for transfers between devices  9.14 us (14%)
    pallas_call x2, Pallas kernels, hot_terms(): pl.pallas_call(functools.partial(hot_kernel, sources, seqs, heads, kv_hea...  12.6 us
    pallas_call x1, Pallas kernels, own_terms(): pl.pallas_call(functools.partial(own_kernel, seqs, ups, heads, group, kv_...  9.44 us
    unnamed x20, local copies, waits for them, and re-layouts  7.54 us
    ppermute x3, waiting for transfers between devices, per_device(): lax.ppermute(parts[k], 'heads', [(i, (i + k) % ways) for i in range(ways)])  6.7 us
    ppermute x3, starting transfers between devices, per_device(): lax.ppermute(parts[k], 'heads', [(i, (i + k) % ways) for i in range(ways)])  5.57 us
    ppermute x3, starting transfers between devices, per_device(): far_q = [lax.ppermute(q, 'pages', out_perm[k]) for k in range(1, chips)]  4.49 us
    pallas_call x1, Pallas kernels, project(): pl.pallas_call(functools.partial(project_kernel, len(blocks), seqs, heads...  4.44 us
    ppermute x3, starting transfers between devices, per_device(): lax.ppermute(sent[k - 1], 'pages', back_perm[k])  3.49 us
  transfers between devices with their start and end apart: 11, of which 3 were waited for; matrix products, arithmetic and copies ran while one was open for 4% of the time, Pallas kernels for 23%

profile of v1, /device:TPU:0, one launch (start us, length us, event | category | flops | bytes accessed | tf_op | source)
XLA Modules:
  0.0 62.2 jit_solution(237901447089527850)
XLA Ops:
  0.0 1.3 %slice.6.refs_6_.refs_2_ = bf16[8,4,128,128]{3,2,1,0:T(8,128)(2,1)S(1)} slice(bf16[72,4,128,128]{3,2,1,0:T(8,128)(2,1)} %keys_ref.1), slice={[0:8], [0:4], [0:128], [0:128]} | slice | bytes 2097152 | tf_op jit(solution)/shard_map/slice | solution.py:312
  1.3 0.6 collective-permute-start.3
  1.9 1.3 %slice.7.refs_7_.refs_3_ = bf16[8,4,128,128]{3,2,1,0:T(8,128)(2,1)S(1)} slice(bf16[72,4,128,128]{3,2,1,0:T(8,128)(2,1)} %values_ref.1), slice={[0:8], [0:4], [0:128], [0:128]} | slice | bytes 2097152 | tf_op jit(solution)/shard_map/slice | solution.py:312
  3.2 0.1 collective-permute-start.4
  3.2 3.0 %collective-permute-start = (bf16[512,128]{1,0:T(8,128)(2,1)}, bf16[512,128]{1,0:T(8,128)(2,1)}, u32[]{:S(2)}, u32[]{:S(2)}) collective-permute-start(bf16[512,128]{1,0:T(8,128)(2,1)} %bitcast.11), channel_id=1, source_target_pairs={{0,8},{4,12},{8,0},{12,4},{16,24},{20,28},{24,16},{28,20},{1,9},{5... | collective-permute-start | bytes 393224 | tf_op jit(solution)/shard_map/ppermute | solution.py:311
  6.2 1.5 %collective-permute-start.1 = (bf16[512,128]{1,0:T(8,128)(2,1)}, bf16[512,128]{1,0:T(8,128)(2,1)}, u32[]{:S(2)}, u32[]{:S(2)}) collective-permute-start(bf16[512,128]{1,0:T(8,128)(2,1)} %bitcast.12), channel_id=1, source_target_pairs={{0,16},{4,20},{8,24},{12,28},{16,0},{20,4},{24,8},{28,12},{1,17},{... | collective-permute-start | bytes 393224 | tf_op jit(solution)/shard_map/ppermute | solution.py:311
  7.7 0.0 collective-permute-start.2
  7.7 0.8 %reshape.40 = s32[8,64]{1,0:T(8,128)S(1)} reshape(s32[512]{0:T(512)} %param.14) | data formatting | bytes 4096 | tf_op jit(solution)/shard_map/reshape | solution.py:322
  8.5 0.0 copy-start.1
  8.5 0.9 %copy-done.1 = bf16[64,8,128]{2,1,0:T(8,128)(2,1)S(1)} copy-done((bf16[64,8,128]{2,1,0:T(8,128)(2,1)S(1)}, bf16[64,8,128]{2,1,0:T(8,128)(2,1)}, u32[]{:S(2)}) %copy-start.1) | copy-done | bytes 131096
  9.4 0.0 copy-start.6
  9.4 0.7 %copy-done.6 = s32[64,1]{0,1:T(1,128)S(1)} copy-done((s32[64,1]{0,1:T(1,128)S(1)}, s32[64,1]{0,1:T(1,128)}, u32[]{:S(2)}) %copy-start.6) | copy-done | bytes 280
  10.1 0.7 %copy-done.7 = s32[64]{0:T(128)S(1)} copy-done((s32[64]{0:T(128)S(1)}, s32[64]{0:T(128)}, u32[]{:S(2)}) %copy-start.7) | copy-done | bytes 280
  10.7 9.4 %own_pages.1 = (f32[512,128]{1,0:T(8,128)S(1)}, f32[512,128]{1,0:T(8,128)S(1)}) custom-call(s32[64]{0:T(128)S(1)} %bitcast.16, s32[64]{0:T(128)S(1)} %copy-done.7, bf16[512,128]{1,0:T(8,128)(2,1)S(1)} %bitcast.14, bf16[72,4,128,128]{3,2,1,0:T(8,128)(2,1)} %keys_ref.1, bf16[72,4,128,128]{3,2,1,0:T(8,128)(2,1)} %values_ref.1), custom_call_target="tpu_custom_call" | custom-call | tf_op jit(solution)/shard_map/own_pages/pallas_call | solution.py:92
  20.2 0.0 copy-start.3
  20.2 0.7 %copy-done.3 = f32[512,128]{1,0:T(8,128)} copy-done((f32[512,128]{1,0:T(8,128)}, f32[512,128]{1,0:T(8,128)S(1)}, u32[]{:S(2)}) %copy-start.3) | copy-done | bytes 262168
  20.9 0.0 copy-done.9
  20.9 0.2 select_reduce_fusion.pos_ref
  21.1 0.0 collective-permute-done.refs_3_
  21.1 0.0 collective-permute-done.1.refs_4_
  21.1 0.0 collective-permute-done.2.refs_5_
  21.1 0.0 collective-permute-done.3.refs_8_.refs_4_
  21.1 0.0 collective-permute-done.4.refs_9_.refs_5_
  21.1 0.1 broadcast_in_dim.60.refs_0_
  21.2 0.1 broadcast_in_dim.62.refs_1_
  21.3 0.1 broadcast_in_dim.64.refs_2_
  21.3 8.1 %hot_pages.2 = (bf16[9,64,128]{2,1,0:T(8,128)(2,1)}, bf16[9,64,128]{2,1,0:T(8,128)(2,1)}, bf16[9,64,128]{2,1,0:T(8,128)(2,1)}) custom-call(s32[16]{0:T(128)S(1)} %select_reduce_fusion.pos_ref, s32[64,128]{1,0:T(8,128)S(1)} %broadcast_in_dim.60.refs_0_, s32[64,128]{1,0:T(8,128)S(1)} %broadcast_in_dim.62.refs_1_, s32[64,128]{1,0:T(8,128)S(1)} %broadcast_in_dim.64.refs_2_, ...), custom_call_target="tpu_custom_call" | custom-call | tf_op jit(solution)/shard_map/hot_pages/pallas_call | solution.py:186
  29.4 2.0 %collective-permute-start.5 = (bf16[9,64,128]{2,1,0:T(8,128)(2,1)}, bf16[9,64,128]{2,1,0:T(8,128)(2,1)}, u32[]{:S(2)}, u32[]{:S(2)}) collective-permute-start(bf16[9,64,128]{2,1,0:T(8,128)(2,1)} %get-tuple-element.27), channel_id=1, source_target_pairs={{8,0},{12,4},{0,8},{4,12},{24,16},{28,20},{16,24},{20,28},{9,1},{1... | collective-permute-start | bytes 442376 | tf_op jit(solution)/shard_map/ppermute | solution.py:336
  31.3 1.5 %collective-permute-start.6 = (bf16[9,64,128]{2,1,0:T(8,128)(2,1)}, bf16[9,64,128]{2,1,0:T(8,128)(2,1)}, u32[]{:S(2)}, u32[]{:S(2)}) collective-permute-start(bf16[9,64,128]{2,1,0:T(8,128)(2,1)} %get-tuple-element.28), channel_id=1, source_target_pairs={{16,0},{20,4},{24,8},{28,12},{0,16},{4,20},{8,24},{12,28},{17,1},{... | collective-permute-start | bytes 442376 | tf_op jit(solution)/shard_map/ppermute | solution.py:336
  32.9 0.0 collective-permute-start.7
  32.9 0.1 broadcast_in_dim.66.refs_0_
  32.9 0.0 copy-done.2
  32.9 4.6 %hot_pages.3 = (f32[512,128]{1,0:T(8,128)S(1)}, f32[512,128]{1,0:T(8,128)S(1)}) custom-call(s32[16]{0:T(128)S(1)} %select_reduce_fusion.pos_ref, s32[64,128]{1,0:T(8,128)S(1)} %broadcast_in_dim.66.refs_0_, bf16[512,128]{1,0:T(8,128)(2,1)S(1)} %bitcast.15, bf16[8,4,128,128]{3,2,1,0:T(8,128)(2,1)S(1)} %slice.6.refs_6_.refs_2_, ...), custom_call_target="tpu_custom_call" | custom-call | tf_op jit(solution)/shard_map/hot_pages/pallas_call | solution.py:186
  37.5 0.0 collective-permute-done.5.refs_0_
  37.5 2.4 %collective-permute-done.6.refs_1_ = bf16[9,64,128]{2,1,0:T(8,128)(2,1)} collective-permute-done((bf16[9,64,128]{2,1,0:T(8,128)(2,1)}, bf16[9,64,128]{2,1,0:T(8,128)(2,1)}, u32[]{:S(2)}, u32[]{:S(2)}) %collective-permute-start.6) | collective-permute-done | bytes 147488 | tf_op jit(solution)/shard_map/ppermute | solution.py:336
  40.0 0.0 collective-permute-done.7.refs_2_
  40.0 3.7 %copy-done = bf16[1024,4608]{1,0:T(8,128)(2,1)S(1)} copy-done((bf16[1024,4608]{1,0:T(8,128)(2,1)S(1)}, bf16[1024,4608]{1,0:T(8,128)(2,1)}, u32[]{:S(2)}) %copy-start) | copy-done | bytes 9437208
  43.7 0.9 %copy-done.4 = f32[512,128]{1,0:T(8,128)S(1)} copy-done((f32[512,128]{1,0:T(8,128)S(1)}, f32[512,128]{1,0:T(8,128)}, u32[]{:S(2)}) %copy-start.4) | copy-done | bytes 262168
  44.6 4.4 %project.1 = (f32[16,4608]{1,0:T(8,128)S(1)}, bf16[16,4608]{1,0:T(8,128)(2,1)S(1)}, bf16[16,4608]{1,0:T(8,128)(2,1)S(1)}, bf16[16,4608]{1,0:T(8,128)(2,1)S(1)}) custom-call(s32[1]{0:T(128)} %bitcast.z_ref, bf16[9,64,128]{2,1,0:T(8,128)(2,1)} %collective-permute-done.5.refs_0_, bf16[9,64,128]{2,1,0:T(8,128)(2,1)} %collective-permute-done.6.refs_1_, ...), custom_call_target="tpu_custom_call" | custom-call | tf_op jit(solution)/shard_map/project/pallas_call | solution.py:253
  49.1 1.6 %collective-permute-start.8 = (bf16[16,4608]{1,0:T(8,128)(2,1)S(1)}, bf16[16,4608]{1,0:T(8,128)(2,1)S(1)}, u32[]{:S(2)}, u32[]{:S(2)}) collective-permute-start(bf16[16,4608]{1,0:T(8,128)(2,1)S(1)} %get-tuple-element.36), channel_id=1, source_target_pairs={{0,1},{1,2},{2,3},{3,0},{4,5},{5,6},{6,7},{7,4},{8,9},{9,10},{10,1... | collective-permute-start | bytes 442376 | tf_op jit(solution)/shard_map/ppermute | solution.py:341
  50.7 2.6 %collective-permute-start.9 = (bf16[16,4608]{1,0:T(8,128)(2,1)S(1)}, bf16[16,4608]{1,0:T(8,128)(2,1)S(1)}, u32[]{:S(2)}, u32[]{:S(2)}) collective-permute-start(bf16[16,4608]{1,0:T(8,128)(2,1)S(1)} %get-tuple-element.37), channel_id=1, source_target_pairs={{0,2},{1,3},{2,0},{3,1},{4,6},{5,7},{6,4},{7,5},{8,10},{9,11},{10,... | collective-permute-start | bytes 442376 | tf_op jit(solution)/shard_map/ppermute | solution.py:341
  53.3 1.3 %collective-permute-start.10 = (bf16[16,4608]{1,0:T(8,128)(2,1)S(1)}, bf16[16,4608]{1,0:T(8,128)(2,1)S(1)}, u32[]{:S(2)}, u32[]{:S(2)}) collective-permute-start(bf16[16,4608]{1,0:T(8,128)(2,1)S(1)} %get-tuple-element.38), channel_id=1, source_target_pairs={{0,3},{1,0},{2,1},{3,2},{4,7},{5,4},{6,5},{7,6},{8,11},{9,8},{10,9... | collective-permute-start | bytes 442376 | tf_op jit(solution)/shard_map/ppermute | solution.py:341
  54.6 0.0 copy-done.8
  54.6 3.1 %collective-permute-done.8.refs_1_ = bf16[16,4608]{1,0:T(8,128)(2,1)S(1)} collective-permute-done((bf16[16,4608]{1,0:T(8,128)(2,1)S(1)}, bf16[16,4608]{1,0:T(8,128)(2,1)S(1)}, u32[]{:S(2)}, u32[]{:S(2)}) %collective-permute-start.8) | collective-permute-done | bytes 147488 | tf_op jit(solution)/shard_map/ppermute | solution.py:341
  57.7 3.6 %collective-permute-done.9.refs_2_ = bf16[16,4608]{1,0:T(8,128)(2,1)S(1)} collective-permute-done((bf16[16,4608]{1,0:T(8,128)(2,1)S(1)}, bf16[16,4608]{1,0:T(8,128)(2,1)S(1)}, u32[]{:S(2)}, u32[]{:S(2)}) %collective-permute-start.9) | collective-permute-done | bytes 147488 | tf_op jit(solution)/shard_map/ppermute | solution.py:341
  61.3 0.0 collective-permute-done.10.refs_3_
  61.3 0.0 copy-done.5
  61.3 0.9 %finish.1 = bf16[16,4608]{1,0:T(8,128)(2,1)} custom-call(f32[16,4608]{1,0:T(8,128)S(1)} %get-tuple-element.35.refs_0_, bf16[16,4608]{1,0:T(8,128)(2,1)S(1)} %collective-permute-done.8.refs_1_, bf16[16,4608]{1,0:T(8,128)(2,1)S(1)} %collective-permute-done.9.refs_2_, bf16[16,4608]{1,0:T(8,128)(2,1)S(1)} %collective-permute-done.10.refs_3_, ...), custom_call_target="tpu_custom_call" | custom-call | tf_op jit(solution)/shard_map/finish/pallas_call | solution.py:286
  (10 shorter events, 0.0 us)
Async XLA Ops:
  1.3 19.8 %collective-permute-start.3 = (bf16[8,4,128,128]{3,2,1,0:T(8,128)(2,1)S(1)}, bf16[8,4,128,128]{3,2,1,0:T(8,128)(2,1)S(1)}, u32[]{:S(2)}, u32[]{:S(2)}) collective-permute-start(bf16[8,4,128,128]{3,2,1,0:T(8,128)(2,1)S(1)} %slice.6.refs_6_.refs_2_), channel_id=1, source_target_pairs={{0,4},{4,0},{8,12},{12,8},{16,20},{20,16},{24,28},{28,24},{1,5},{5... | collective-permute-start | bytes 3145736 | tf_op jit(solution)/shard_map/ppermute | solution.py:313
  3.2 17.9 %collective-permute-start.4 = (bf16[8,4,128,128]{3,2,1,0:T(8,128)(2,1)S(1)}, bf16[8,4,128,128]{3,2,1,0:T(8,128)(2,1)}, u32[]{:S(2)}, u32[]{:S(2)}) collective-permute-start(bf16[8,4,128,128]{3,2,1,0:T(8,128)(2,1)S(1)} %slice.7.refs_7_.refs_3_), channel_id=1, source_target_pairs={{0,4},{4,0},{8,12},{12,8},{16,20},{20,16},{24,28},{28,24},{1,5},{5... | collective-permute-start | bytes 3145736 | tf_op jit(solution)/shard_map/ppermute | solution.py:313
  3.2 17.8 %collective-permute-start = (bf16[512,128]{1,0:T(8,128)(2,1)}, bf16[512,128]{1,0:T(8,128)(2,1)}, u32[]{:S(2)}, u32[]{:S(2)}) collective-permute-start(bf16[512,128]{1,0:T(8,128)(2,1)} %bitcast.11), channel_id=1, source_target_pairs={{0,8},{4,12},{8,0},{12,4},{16,24},{20,28},{24,16},{28,20},{1,9},{5... | collective-permute-start | bytes 393224 | tf_op jit(solution)/shard_map/ppermute | solution.py:311
  6.2 14.9 %collective-permute-start.1 = (bf16[512,128]{1,0:T(8,128)(2,1)}, bf16[512,128]{1,0:T(8,128)(2,1)}, u32[]{:S(2)}, u32[]{:S(2)}) collective-permute-start(bf16[512,128]{1,0:T(8,128)(2,1)} %bitcast.12), channel_id=1, source_target_pairs={{0,16},{4,20},{8,24},{12,28},{16,0},{20,4},{24,8},{28,12},{1,17},{... | collective-permute-start | bytes 393224 | tf_op jit(solution)/shard_map/ppermute | solution.py:311
  7.7 13.4 %collective-permute-start.2 = (bf16[512,128]{1,0:T(8,128)(2,1)}, bf16[512,128]{1,0:T(8,128)(2,1)}, u32[]{:S(2)}, u32[]{:S(2)}) collective-permute-start(bf16[512,128]{1,0:T(8,128)(2,1)} %bitcast.13), channel_id=1, source_target_pairs={{0,24},{4,28},{8,16},{12,20},{16,8},{20,12},{24,0},{28,4},{1,25},{... | collective-permute-start | bytes 393224 | tf_op jit(solution)/shard_map/ppermute | solution.py:311
  8.5 0.9 %copy-start.1 = (bf16[64,8,128]{2,1,0:T(8,128)(2,1)S(1)}, bf16[64,8,128]{2,1,0:T(8,128)(2,1)}, u32[]{:S(2)}) copy-start(bf16[64,8,128]{2,1,0:T(8,128)(2,1)} %param.10) | copy-start | bytes 393220
  9.4 0.7 %copy-start.6 = (s32[64,1]{0,1:T(1,128)S(1)}, s32[64,1]{0,1:T(1,128)}, u32[]{:S(2)}) copy-start(s32[64,1]{0,1:T(1,128)} %param.15) | copy-start | bytes 772
  10.1 0.7 %copy-start.7 = (s32[64]{0:T(128)S(1)}, s32[64]{0:T(128)}, u32[]{:S(2)}) copy-start(s32[64]{0:T(128)} %lengths_ref.1) | copy-start | bytes 772
  10.7 10.1 %copy-start.9 = (s32[64]{0:T(128)S(1)}, s32[64]{0:T(128)}, u32[]{:S(2)}) copy-start(s32[64]{0:T(128)} %param.13) | copy-start | bytes 772
  10.7 22.2 %copy-start.2 = (bf16[64,8,128]{2,1,0:T(8,128)(2,1)S(1)}, bf16[64,8,128]{2,1,0:T(8,128)(2,1)}, u32[]{:S(2)}) copy-start(bf16[64,8,128]{2,1,0:T(8,128)(2,1)} %param.10) | copy-start | bytes 393220
  20.2 0.7 %copy-start.3 = (f32[512,128]{1,0:T(8,128)}, f32[512,128]{1,0:T(8,128)S(1)}, u32[]{:S(2)}) copy-start(f32[512,128]{1,0:T(8,128)S(1)} %get-tuple-element.31.refs_4_) | copy-start | bytes 786436
  29.4 8.2 %collective-permute-start.5 = (bf16[9,64,128]{2,1,0:T(8,128)(2,1)}, bf16[9,64,128]{2,1,0:T(8,128)(2,1)}, u32[]{:S(2)}, u32[]{:S(2)}) collective-permute-start(bf16[9,64,128]{2,1,0:T(8,128)(2,1)} %get-tuple-element.27), channel_id=1, source_target_pairs={{8,0},{12,4},{0,8},{4,12},{24,16},{28,20},{16,24},{20,28},{9,1},{1... | collective-permute-start | bytes 442376 | tf_op jit(solution)/shard_map/ppermute | solution.py:336
  31.3 8.6 %collective-permute-start.6 = (bf16[9,64,128]{2,1,0:T(8,128)(2,1)}, bf16[9,64,128]{2,1,0:T(8,128)(2,1)}, u32[]{:S(2)}, u32[]{:S(2)}) collective-permute-start(bf16[9,64,128]{2,1,0:T(8,128)(2,1)} %get-tuple-element.28), channel_id=1, source_target_pairs={{16,0},{20,4},{24,8},{28,12},{0,16},{4,20},{8,24},{12,28},{17,1},{... | collective-permute-start | bytes 442376 | tf_op jit(solution)/shard_map/ppermute | solution.py:336
  32.9 7.1 %collective-permute-start.7 = (bf16[9,64,128]{2,1,0:T(8,128)(2,1)}, bf16[9,64,128]{2,1,0:T(8,128)(2,1)}, u32[]{:S(2)}, u32[]{:S(2)}) collective-permute-start(bf16[9,64,128]{2,1,0:T(8,128)(2,1)} %get-tuple-element.29), channel_id=1, source_target_pairs={{24,0},{28,4},{16,8},{20,12},{8,16},{12,20},{0,24},{4,28},{25,1},{... | collective-permute-start | bytes 442376 | tf_op jit(solution)/shard_map/ppermute | solution.py:336
  32.9 21.8 %copy-start.8 = (f32[4608]{0:T(1024)S(1)}, f32[4608]{0:T(1024)}, u32[]{:S(2)}) copy-start(f32[4608]{0:T(1024)} %param.19) | copy-start | bytes 55300
  32.9 28.5 %copy-start.5 = (bf16[16,4608]{1,0:T(8,128)(2,1)S(1)}, bf16[16,4608]{1,0:T(8,128)(2,1)}, u32[]{:S(2)}) copy-start(bf16[16,4608]{1,0:T(8,128)(2,1)} %refs_4_.1) | copy-start | bytes 442372
  40.0 3.7 %copy-start = (bf16[1024,4608]{1,0:T(8,128)(2,1)S(1)}, bf16[1024,4608]{1,0:T(8,128)(2,1)}, u32[]{:S(2)}) copy-start(bf16[1024,4608]{1,0:T(8,128)(2,1)} %refs_7_.1) | copy-start | bytes 28311556
  43.7 0.9 %copy-start.4 = (f32[512,128]{1,0:T(8,128)S(1)}, f32[512,128]{1,0:T(8,128)}, u32[]{:S(2)}) copy-start(f32[512,128]{1,0:T(8,128)} %copy-done.3) | copy-start | bytes 786436
  49.1 8.7 %collective-permute-start.8 = (bf16[16,4608]{1,0:T(8,128)(2,1)S(1)}, bf16[16,4608]{1,0:T(8,128)(2,1)S(1)}, u32[]{:S(2)}, u32[]{:S(2)}) collective-permute-start(bf16[16,4608]{1,0:T(8,128)(2,1)S(1)} %get-tuple-element.36), channel_id=1, source_target_pairs={{0,1},{1,2},{2,3},{3,0},{4,5},{5,6},{6,7},{7,4},{8,9},{9,10},{10,1... | collective-permute-start | bytes 442376 | tf_op jit(solution)/shard_map/ppermute | solution.py:341
  50.7 10.7 %collective-permute-start.9 = (bf16[16,4608]{1,0:T(8,128)(2,1)S(1)}, bf16[16,4608]{1,0:T(8,128)(2,1)S(1)}, u32[]{:S(2)}, u32[]{:S(2)}) collective-permute-start(bf16[16,4608]{1,0:T(8,128)(2,1)S(1)} %get-tuple-element.37), channel_id=1, source_target_pairs={{0,2},{1,3},{2,0},{3,1},{4,6},{5,7},{6,4},{7,5},{8,10},{9,11},{10,... | collective-permute-start | bytes 442376 | tf_op jit(solution)/shard_map/ppermute | solution.py:341
  53.3 8.1 %collective-permute-start.10 = (bf16[16,4608]{1,0:T(8,128)(2,1)S(1)}, bf16[16,4608]{1,0:T(8,128)(2,1)S(1)}, u32[]{:S(2)}, u32[]{:S(2)}) collective-permute-start(bf16[16,4608]{1,0:T(8,128)(2,1)S(1)} %get-tuple-element.38), channel_id=1, source_target_pairs={{0,3},{1,0},{2,1},{3,2},{4,7},{5,4},{6,5},{7,6},{8,11},{9,8},{10,9... | collective-permute-start | bytes 442376 | tf_op jit(solution)/shard_map/ppermute | solution.py:341

commit v2 on v1

v2 whole, which is shorter than its diff:
```python
import functools
import math

import jax
import jax.numpy as jnp
from jax import lax
from jax.experimental import pallas as pl
from jax.experimental.pallas import tpu as pltpu
from jax.sharding import PartitionSpec as P


HOT_CAP = 8
score_scale = 1.0 / 12.0
soft_cap = 50.0
epsilon = 1e-06
inner = score_scale / soft_cap
outer = soft_cap * math.log2(math.e)
MIB = 1 << 20


def weights_of(logits):
    return jnp.exp2(outer * jnp.tanh(logits * inner))


def dot_t(a, b):
    return lax.dot_general(a, b, (((1,), (1,)), ((), ())), preferred_element_type=jnp.float32)


def dot_n(a, b):
    return lax.dot_general(a, b, (((1,), (0,)), ((), ())), preferred_element_type=jnp.float32)


def lead_kernel(keys_ref, values_ref, k_out, v_out, sems):
    copies = [
        pltpu.make_async_copy(src.at[pl.ds(0, dst.shape[0])], dst, sems.at[i])
        for i, (src, dst) in enumerate(((keys_ref, k_out), (values_ref, v_out)))
    ]
    for copy in copies:
        copy.start()
    for copy in copies:
        copy.wait()


def in_hbm(x):
    return pltpu.with_memory_space_constraint(x, pltpu.HBM)


HBM = pl.BlockSpec(memory_space=pltpu.HBM)
VMEM = pl.BlockSpec(memory_space=pltpu.VMEM)
SMEM = pl.BlockSpec(memory_space=pltpu.SMEM)


def lead_pages(keys, values):
    out = jax.ShapeDtypeStruct((HOT_CAP, *keys.shape[1:]), keys.dtype)
    return pl.pallas_call(
        lead_kernel,
        out_shape=(out, out),
        in_specs=[HBM, HBM],
        out_specs=(VMEM, VMEM),
        scratch_shapes=[pltpu.SemaphoreType.DMA((2,))],
        compiler_params=pltpu.CompilerParams(vmem_limit_bytes=4 * MIB),
        name="lead_pages",
    )(in_hbm(keys), in_hbm(values))


def own_kernel(
    seqs, ups, heads, group, kv_heads, unroll,
    lengths_ref, q_ref, kbuf, vbuf, w_hbm, num_ref, tot_ref, w_ref, sem,
):
    page_len, head_dim = kbuf.shape[2], kbuf.shape[3]
    width = kv_heads * page_len
    prefetch = pltpu.make_async_copy(w_hbm, w_ref, sem)
    prefetch.start()
    column = lax.broadcasted_iota(jnp.int32, (heads, width), 1)
    row = lax.broadcasted_iota(jnp.int32, (heads, width), 0)
    mine = (column // page_len) == (row // group)
    token = jnp.where(mine, column % page_len, ups * page_len)
    ones = jnp.ones((width, head_dim), jnp.bfloat16)

    def block(b, carry):
        for j in range(unroll):
            s = b * unroll + j
            q = q_ref[pl.ds(pl.multiple_of(s * heads, heads), heads), :]
            total = jnp.zeros((heads, 2 * head_dim), jnp.float32)
            for u in range(ups):
                k = kbuf[s * ups + u].reshape(width, head_dim)
                v = vbuf[s * ups + u].reshape(width, head_dim)
                allowed = token < lengths_ref[s] - u * page_len
                weight = jnp.where(allowed, weights_of(dot_t(q, k)), 0.0).astype(jnp.bfloat16)
                total = total + dot_n(weight, jnp.concatenate([v, ones], axis=1))
            num_ref[pl.ds(s, heads, stride=seqs), :] = total[:, :head_dim]
            tot_ref[pl.ds(s, heads, stride=seqs), :] = total[:, head_dim:]
        return carry

    lax.fori_loop(0, seqs // unroll, block, 0)
    prefetch.wait()


def own_terms(q, own_k, own_v, lengths, o_weight):
    seqs, _, head_dim = q.shape
    count, kv_heads, _, _ = own_k.shape
    group = q.shape[1] // kv_heads
    heads = -(-q.shape[1] // 8) * 8
    q = jnp.pad(q, ((0, 0), (0, heads - q.shape[1]), (0, 0))).reshape(seqs * heads, head_dim)
    unroll = math.gcd(seqs, 32)
    out = jax.ShapeDtypeStruct((heads * seqs, head_dim), jnp.float32)
    num, tot, w = pl.pallas_call(
        functools.partial(own_kernel, seqs, count // seqs, heads, group, kv_heads, unroll),
        out_shape=(out, out, jax.ShapeDtypeStruct(o_weight.shape, o_weight.dtype)),
        in_specs=[SMEM, VMEM, VMEM, VMEM, HBM],
        out_specs=(VMEM, VMEM, VMEM),
        scratch_shapes=[pltpu.SemaphoreType.DMA],
        compiler_params=pltpu.CompilerParams(vmem_limit_bytes=8 * MIB),
        name="own_pages",
    )(lengths, q, own_k, own_v, in_hbm(o_weight))
    return (num, tot), w


def hot_kernel(sources, seqs, heads, kv_heads, packed, fetch, pos_ref, *refs):
    if fetch:
        pages_ref, cache_ref, *refs = refs
        *refs, pages_out, staged, sems = refs

        def copy(i):
            return pltpu.make_async_copy(cache_ref.at[pages_ref[i]], pages_out.at[i], sems.at[i])

        def start(i, carry):
            copy(i).start()
            return carry

        def wait(i, carry):
            copy(i).wait()
            return carry

        lax.fori_loop(0, fetch, start, 0)
    else:
        *refs, staged = refs
    used = refs[:sources]
    queries = refs[sources : 2 * sources]
    halves = (refs[2 * sources : 2 * sources + 2], refs[2 * sources + 2 : 2 * sources + 4])
    outs = refs[2 * sources + 4 :]
    group = heads // kv_heads
    cap, _, page_len, head_dim = halves[0][0].shape
    lane = lax.broadcasted_iota(jnp.int32, (seqs, head_dim), 1)
    for r in range(sources):
        staged[r] = queries[r][...].astype(jnp.float32)
    used_rows = [u[...] for u in used]
    step = 2
    ones = jnp.ones((step * page_len, head_dim), jnp.bfloat16)
    totals = [jnp.zeros((seqs, head_dim), jnp.float32) for _ in range(sources)]
    for h in range(kv_heads):
        rows = [
            staged[r, pl.ds(h * group + g, seqs, stride=heads), :].astype(jnp.bfloat16)
            for r in range(sources)
            for g in range(group)
        ]
        q = jnp.concatenate(rows, axis=0)
        acc = jnp.zeros((q.shape[0], 2 * head_dim), jnp.float32)
        for half, (k_ref, v_ref) in enumerate(halves):
            for c in range(0, cap, step):
                k = k_ref[c : c + step, h].reshape(step * page_len, head_dim)
                v = v_ref[c : c + step, h].reshape(step * page_len, head_dim)
                weight = weights_of(dot_t(q, k))
                parts = []
                for p in range(step):
                    place = pos_ref[half * cap + c + p]
                    columns = slice(p * page_len, (p + 1) * page_len)
                    part = []
                    for r in range(sources):
                        mask = used_rows[r] > place
                        for i in range(r * group, (r + 1) * group):
                            part.append(jnp.where(mask, weight[i * seqs : (i + 1) * seqs, columns], 0.0))
                    parts.append(jnp.concatenate(part, axis=0).astype(jnp.bfloat16))
                acc = acc + dot_n(jnp.concatenate(parts, axis=1), jnp.concatenate([v, ones], axis=1))
        for r in range(sources):
            for g in range(group):
                i = r * group + g
                head = h * group + g
                num = acc[i * seqs : (i + 1) * seqs, :head_dim]
                tot = acc[i * seqs : (i + 1) * seqs, head_dim:]
                if packed:
                    rest = tot - tot.astype(jnp.bfloat16).astype(jnp.float32)
                    outs[r][head] = num.astype(jnp.bfloat16)
                    low = jnp.where(lane == heads + head, rest, totals[r])
                    totals[r] = jnp.where(lane == head, tot, low)
                else:
                    outs[2 * r][head * seqs : (head + 1) * seqs, :] = num
                    outs[2 * r + 1][head * seqs : (head + 1) * seqs, :] = tot
    if packed:
        for r in range(sources):
            outs[r][heads] = totals[r].astype(jnp.bfloat16)
    if fetch:
        lax.fori_loop(0, fetch, wait, 0)


def hot_terms(queries, used, position, own_kv, partner_kv, packed, pages=None, cache=None):
    sources = len(queries)
    seqs = used[0].shape[0]
    _, kv_heads, page_len, head_dim = own_kv[0].shape
    heads = queries[0].shape[0] // seqs
    if packed:
        shapes = [((heads + 1, seqs, head_dim), jnp.bfloat16)] * sources
    else:
        shapes = [((heads * seqs, head_dim), jnp.float32)] * (2 * sources)
    scratch = [pltpu.VMEM((sources, seqs * heads, head_dim), jnp.float32)]
    operands = [position, *used, *queries, *own_kv, *partner_kv]
    specs = [SMEM] + [VMEM] * (2 * sources + 4)
    count = 0
    if pages is not None:
        count = pages.shape[0]
        operands[1:1] = [pages, in_hbm(cache)]
        specs[1:1] = [SMEM, HBM]
        shapes.append(((count, kv_heads, page_len, head_dim), cache.dtype))
        scratch.append(pltpu.SemaphoreType.DMA((count,)))
    return pl.pallas_call(
        functools.partial(hot_kernel, sources, seqs, heads, kv_heads, packed, count),
        out_shape=[jax.ShapeDtypeStruct(*s) for s in shapes],
        in_specs=specs,
        out_specs=[VMEM] * len(shapes),
        scratch_shapes=scratch,
        compiler_params=pltpu.CompilerParams(vmem_limit_bytes=12 * MIB),
        name="hot_pages",
    )(*operands)


def project_kernel(received, seqs, heads, ways, z_ref, *refs):
    blocks = refs[:received]
    own_num, own_tot, hot_num, hot_tot, w_ref = refs[received : received + 5]
    outs = refs[received + 5 : received + 5 + ways]
    spread = refs[-1]
    head_dim = own_num.shape[1]
    rows = seqs // ways
    far = jnp.zeros((seqs, head_dim), jnp.float32)
    for b in blocks:
        far = far + b[heads].astype(jnp.float32)
    for h in range(heads):
        part = pl.ds(h * seqs, seqs)
        num = own_num[part, :] + hot_num[part, :]
        tot = own_tot[part, :] + hot_tot[part, :]
        for b in blocks:
            num = num + b[h].astype(jnp.float32)
        if blocks:
            tot = tot + (far[:, h : h + 1] + far[:, heads + h : heads + h + 1])
        spread[:, h * head_dim : (h + 1) * head_dim] = num / tot
    turned = []
    for k in range(ways):
        target = lax.rem(z_ref[0] + k, ways)
        turned.append(spread[pl.ds(pl.multiple_of(target * rows, rows), rows), :])
    att = jnp.concatenate(turned, axis=0).astype(jnp.bfloat16)
    model = w_ref.shape[1]
    tile = math.gcd(model, 768)
    for n in range(0, model, tile):
        res = dot_n(att, w_ref[:, n : n + tile])
        for k in range(ways):
            outs[k][:, n : n + tile] = res[k * rows : (k + 1) * rows].astype(outs[k].dtype)


def project(blocks, own, hot, o_weight, z, ways):
    head_dim = own[0].shape[1]
    width, model = o_weight.shape
    heads = width // head_dim
    seqs = hot[0].shape[0] // heads
    rows = seqs // ways
    kinds = [jnp.float32] + [jnp.bfloat16] * (ways - 1)
    return pl.pallas_call(
        functools.partial(project_kernel, len(blocks), seqs, heads, ways),
        out_shape=[jax.ShapeDtypeStruct((rows, model), kind) for kind in kinds],
        in_specs=[SMEM] + [VMEM] * (len(blocks) + 5),
        out_specs=[VMEM] * ways,
        scratch_shapes=[pltpu.VMEM((seqs, width), jnp.float32)],
        compiler_params=pltpu.CompilerParams(vmem_limit_bytes=8 * MIB),
        name="project",
    )(z, *blocks, *own, *hot, o_weight)


def norm_kernel(*refs):
    parts, (residual, gain, out) = refs[:-3], refs[-3:]
    projected = parts[0][...]
    for p in parts[1:]:
        projected = projected + p[...].astype(jnp.float32)
    mean_sq = jnp.mean(projected * projected, axis=1, keepdims=True)
    normed = projected / jnp.sqrt(mean_sq + epsilon) * gain[...]
    out[...] = (residual[...].astype(jnp.float32) + normed).astype(jnp.bfloat16)


def finish(parts, residual, norm_gain):
    return pl.pallas_call(
        norm_kernel,
        out_shape=jax.ShapeDtypeStruct(residual.shape, residual.dtype),
        compiler_params=pltpu.CompilerParams(vmem_limit_bytes=8 * MIB),
        name="finish",
    )(*parts, residual, norm_gain.reshape(1, -1))


def layer(
    chips, ways, queries, keys, values, hot_pages, hot_used, user_pages, lengths, o_weight, residual, norm_gain
):
    seqs, heads, head_dim = queries.shape
    page_count = keys.shape[0]
    me = lax.axis_index("pages")
    z = lax.axis_index("heads")
    devices = 2 * chips
    swap = [(i, i ^ 1) for i in range(devices)]
    power = chips & (chips - 1) == 0

    def there(i, k):
        return i ^ (2 * k) if power else (i + 2 * k) % devices

    q = queries.reshape(seqs * heads, head_dim)
    pages = user_pages.reshape(-1)
    out_perm = [[(i, there(i, k)) for i in range(devices)] for k in range(chips)]
    back_perm = [[(j, i) for i, j in perm] for perm in out_perm]
    own_kv = lead_pages(keys, values)
    partner_kv = tuple(lax.ppermute(x, "pages", swap) for x in own_kv)
    q, own_kv = lax.optimization_barrier((q, own_kv))
    late = [2] if chips > 2 else []
    soon = [k for k in reversed(range(1, chips)) if k not in late]
    far_q = {k: lax.ppermute(q, "pages", out_perm[k]) for k in soon + late}

    slot = jnp.arange(2 * HOT_CAP, dtype=jnp.int32)
    holder = jnp.where(slot < HOT_CAP, me, me ^ 1)
    page_ids = holder * page_count + slot % HOT_CAP
    matches = page_ids[:, None] == hot_pages[None, :]
    order = jnp.arange(hot_pages.shape[0], dtype=jnp.int32)
    absent = jnp.int32(jnp.iinfo(jnp.int32).max)
    position = jnp.min(jnp.where(matches, order[None, :], absent), axis=1)

    def used_of(k):
        origin = me ^ (2 * k) if power else lax.rem(me + devices - 2 * k, devices)
        row = lax.dynamic_slice_in_dim(hot_used, origin * seqs, seqs)
        return jnp.broadcast_to(row[:, None], (seqs, head_dim))

    used = [used_of(k) for k in range(chips)]
    turn, position, used = lax.optimization_barrier((z.reshape(1), position, used))
    *hot, own_k = hot_terms([q], [used[0]], position, own_kv, partner_kv, False, pages, keys)
    blocks = []
    own_v = None
    before = hot
    for ks in (soon, late):
        if not ks:
            continue
        before, arrived = lax.optimization_barrier((before, [far_q[k] for k in ks]))
        rest = (pages, values) if own_v is None else ()
        sent = hot_terms(arrived, [used[k] for k in ks], position, own_kv, partner_kv, True, *rest)
        if rest:
            *sent, own_v = sent
        for k, b in zip(ks, sent):
            blocks.append(lax.ppermute(b, "pages", back_perm[k]))
        before = sent
    if own_v is None:
        own_v = jnp.take(values, pages, axis=0)
    queries, before = lax.optimization_barrier((queries, before))
    own, weight = own_terms(queries, own_k, own_v, lengths, o_weight)
    parts = project(blocks, own, hot, weight, turn, ways)
    arrived = [parts[0]] + [
        lax.ppermute(parts[k], "heads", [(i, (i + k) % ways) for i in range(ways)])
        for k in range(1, ways)
    ]
    return finish(arrived, residual, norm_gain)


def solution(mesh):
    in_specs = (
        P("pages", "heads", None),
        P("pages", "heads", None, None),
        P("pages", "heads", None, None),
        P(),
        P(),
        P("pages", None),
        P("pages"),
        P("heads", None),
        P(("pages", "heads"), None),
        P(),
    )
    out_specs = P(("pages", "heads"), None)
    chips = mesh.shape["pages"] // 2
    body = functools.partial(layer, chips, mesh.shape["heads"])
    return jax.shard_map(body, mesh=mesh, in_specs=in_specs, out_specs=out_specs, check_vma=False)
```

time: 63.4 us -> 49.9 us (0.79)
  the two profiles are of different devices: /device:TPU:0 before, /device:TPU:9 now
where the time goes in v2:
time: 49.9 us; the launch traced here: 49.7 us
  Pallas kernels  23.3 us (47%)
  waiting for transfers between devices  12.3 us (25%)
  starting transfers between devices  10.1 us (20%)
  local copies, waits for them, and re-layouts  2.46 us (5%)
  other arithmetic  1.38 us (3%)
    pallas_call x3, Pallas kernels, hot_terms(): pl.pallas_call(functools.partial(hot_kernel, sources, seqs, heads, kv_hea...  13.4 us
    ppermute x3, waiting for transfers between devices, layer(): lax.ppermute(parts[k], 'heads', [(i, (i + k) % ways) for i in range(ways)])  12.3 us
    pallas_call x1, Pallas kernels, own_terms(): pl.pallas_call(functools.partial(own_kernel, seqs, count // seqs, heads,...  5.46 us
    ppermute x3, starting transfers between devices, layer(): lax.ppermute(parts[k], 'heads', [(i, (i + k) % ways) for i in range(ways)])  3.83 us
    ppermute x3, starting transfers between devices, layer(): blocks.append(lax.ppermute(b, 'pages', back_perm[k]))  2.78 us
    ppermute x3, starting transfers between devices, layer(): far_q = {k: lax.ppermute(q, 'pages', out_perm[k]) for k in soon + late}  2.65 us
    pallas_call x1, Pallas kernels, project(): pl.pallas_call(functools.partial(project_kernel, len(blocks), seqs, heads...  1.93 us
    pallas_call x1, Pallas kernels, lead_pages(): pl.pallas_call(lead_kernel, out_shape=(out, out), in_specs=[HBM, HBM], ou...  1.59 us
  transfers between devices with their start and end apart: 11, of which 3 were waited for; matrix products, arithmetic and copies ran while one was open for 8% of the time, Pallas kernels for 38%

profile of v2, /device:TPU:9, one launch (start us, length us, event | category | flops | bytes accessed | tf_op | source)
XLA Modules:
  0.0 49.7 jit_solution(7156637401918994739)
XLA Ops:
  0.0 0.0 copy-start
  0.0 0.0 copy-start.2
  0.0 1.6 %lead_pages.1 = (bf16[8,4,128,128]{3,2,1,0:T(8,128)(2,1)S(1)}, bf16[8,4,128,128]{3,2,1,0:T(8,128)(2,1)S(1)}) custom-call(bf16[72,4,128,128]{3,2,1,0:T(8,128)(2,1)} %refs_1_.2, bf16[72,4,128,128]{3,2,1,0:T(8,128)(2,1)} %refs_1_.3), custom_call_target="tpu_custom_call" | custom-call | tf_op jit(solution)/shard_map/lead_pages/pallas_call | solution.py:55
  1.6 0.7 %collective-permute-start = (bf16[8,4,128,128]{3,2,1,0:T(8,128)(2,1)S(1)}, bf16[8,4,128,128]{3,2,1,0:T(8,128)(2,1)S(1)}, u32[]{:S(2)}, u32[]{:S(2)}) collective-permute-start(bf16[8,4,128,128]{3,2,1,0:T(8,128)(2,1)S(1)} %get-tuple-element.41.refs_4_.refs_6_.refs_2_), channel_id=1, source_target_pairs={{0,4},{4,0},{8,12},{12,8},{16,20},{20,16},{24,28},{28,24},{1,5},{5... | collective-permute-start | bytes 3145736 | tf_op jit(solution)/shard_map/ppermute | solution.py:314
  2.3 0.1 collective-permute-start.1
  2.4 0.0 copy-done
  2.4 2.2 %collective-permute-start.2 = (bf16[512,128]{1,0:T(8,128)(2,1)S(1)}, bf16[512,128]{1,0:T(8,128)(2,1)S(1)}, u32[]{:S(2)}, u32[]{:S(2)}) collective-permute-start(bf16[512,128]{1,0:T(8,128)(2,1)S(1)} %bitcast.4), channel_id=1, source_target_pairs={{0,24},{4,28},{8,16},{12,20},{16,8},{20,12},{24,0},{28,4},{1,25},{... | collective-permute-start | bytes 393224 | tf_op jit(solution)/shard_map/ppermute | solution.py:318
  4.6 0.3 collective-permute-start.3
  4.9 0.2 collective-permute-start.6
  5.1 1.5 %fusion.2 = (s32[64]{0:T(128)S(1)}, s32[64]{0:T(128)S(1)}, s32[64]{0:T(128)}, s32[64]{0:T(128)S(1)}) fusion(s32[512]{0:T(512)} %param.14, s32[]{:T(128)S(6)} %select_n.41, s32[]{:T(128)S(6)} %select_n.39, s32[]{:T(128)S(6)} %select_n.38, s32[]{:T(128)S(6)} %select_n.40), kind=kLoop, calls=%fused_computation.5 | loop fusion | bytes 2064 | tf_op jit(solution)/shard_map/dynamic_slice | solution.py:330
  6.6 0.5 %fusion = s32[16]{0:T(128)} fusion(s32[]{:T(128)S(6)} %xor.12, s32[]{:T(128)S(6)} %axis_index.25), kind=kLoop, calls=%fused_computation.3 | loop fusion | flops 160 | bytes 72 | tf_op jit(solution)/shard_map/add | solution.py:322
  7.1 0.8 %select_reduce_fusion.pos_ref = s32[16]{0:T(128)S(1)} fusion(s32[64]{0:T(128)} %param.13, s32[16]{0:T(128)} %fusion), kind=kLoop, calls=%fused_computation | loop fusion | flops 3056 | bytes 384 | tf_op jit(solution)/shard_map/reduce_min | solution.py:326
  7.9 0.7 %broadcast_in_dim.51.refs_2_ = s32[64,128]{1,0:T(8,128)S(1)} broadcast(s32[64]{0:T(128)} %get-tuple-element.63), dimensions={0} | broadcast | bytes 33024 | tf_op jit(solution)/shard_map/broadcast_in_dim | solution.py:331
  8.7 0.1 broadcast_in_dim.52.refs_3_
  8.7 0.1 broadcast_in_dim.53.refs_0_
  8.8 0.1 broadcast_in_dim.54.refs_2_
  8.9 0.0 collective-permute-done.refs_6_.refs_8_.refs_4_
  8.9 0.0 collective-permute-done.1.refs_7_.refs_9_.refs_5_
  8.9 0.0 copy-done.2
  8.9 5.3 %hot_pages.3 = (f32[512,128]{1,0:T(8,128)S(1)}, f32[512,128]{1,0:T(8,128)S(1)}, bf16[64,4,128,128]{3,2,1,0:T(8,128)(2,1)S(1)}) custom-call(s32[16]{0:T(128)S(1)} %select_reduce_fusion.pos_ref, s32[64]{0:T(128)S(1)} %bitcast.9, bf16[72,4,128,128]{3,2,1,0:T(8,128)(2,1)} %refs_1_.2, s32[64,128]{1,0:T(8,128)S(1)} %broadcast_in_dim.51.refs_2_, ...), custom_call_target="tpu_custom_call" | custom-call | tf_op jit(solution)/shard_map/hot_pages/pallas_call | solution.py:215
  14.3 0.0 copy-start.3
  14.3 0.0 collective-permute-done.2.refs_4_
  14.3 0.0 collective-permute-done.3.refs_5_
  14.3 5.3 %hot_pages.4 = (bf16[9,64,128]{2,1,0:T(8,128)(2,1)S(1)}, bf16[9,64,128]{2,1,0:T(8,128)(2,1)S(1)}, bf16[64,4,128,128]{3,2,1,0:T(8,128)(2,1)S(1)}) custom-call(s32[16]{0:T(128)S(1)} %select_reduce_fusion.pos_ref, s32[64]{0:T(128)S(1)} %bitcast.10, bf16[72,4,128,128]{3,2,1,0:T(8,128)(2,1)} %refs_1_.3, s32[64,128]{1,0:T(8,128)S(1)} %broadcast_in_dim.54.refs_2_, ...), custom_call_target="tpu_custom_call" | custom-call | tf_op jit(solution)/shard_map/hot_pages/pallas_call | solution.py:215
  19.6 2.2 %collective-permute-start.4 = (bf16[9,64,128]{2,1,0:T(8,128)(2,1)S(1)}, bf16[9,64,128]{2,1,0:T(8,128)(2,1)S(1)}, u32[]{:S(2)}, u32[]{:S(2)}) collective-permute-start(bf16[9,64,128]{2,1,0:T(8,128)(2,1)S(1)} %get-tuple-element.47), channel_id=1, source_target_pairs={{24,0},{28,4},{16,8},{20,12},{8,16},{12,20},{0,24},{4,28},{25,1},{... | collective-permute-start | bytes 442376 | tf_op jit(solution)/shard_map/ppermute | solution.py:348
  21.9 0.3 collective-permute-start.5
  22.1 0.0 collective-permute-done.6.refs_1_
  22.1 2.7 %hot_pages.5 = bf16[9,64,128]{2,1,0:T(8,128)(2,1)S(1)} custom-call(s32[16]{0:T(128)S(1)} %select_reduce_fusion.pos_ref, s32[64,128]{1,0:T(8,128)S(1)} %broadcast_in_dim.53.refs_0_, bf16[512,128]{1,0:T(8,128)(2,1)} %collective-permute-done.6.refs_1_, bf16[8,4,128,128]{3,2,1,0:T(8,128)(2,1)S(1)} %get-tuple-element.41.refs_4_.refs_6_.refs_2_, ...), custom_call_target="tpu_custom_call" | custom-call | tf_op jit(solution)/shard_map/hot_pages/pallas_call | solution.py:215
  24.9 0.3 collective-permute-start.7
  25.2 0.0 copy-done.3
  25.2 5.5 %own_pages.1 = (f32[512,128]{1,0:T(8,128)S(1)}, f32[512,128]{1,0:T(8,128)S(1)}, bf16[1024,4608]{1,0:T(8,128)(2,1)S(1)}) custom-call(s32[64]{0:T(128)S(1)} %copy-done.3, bf16[512,128]{1,0:T(8,128)(2,1)S(1)} %bitcast.8, bf16[64,4,128,128]{3,2,1,0:T(8,128)(2,1)S(1)} %get-tuple-element.52.kbuf, bf16[64,4,128,128]{3,2,1,0:T(8,128)(2,1)S(1)} %get-tuple-element.53.vbuf, ...), custom_call_target="tpu_custom_call" | custom-call | tf_op jit(solution)/shard_map/own_pages/pallas_call | solution.py:107
  30.6 0.0 copy-start.4
  30.7 0.0 copy-start.1
  30.7 0.0 collective-permute-done.4.refs_0_
  30.7 0.0 collective-permute-done.5.refs_1_
  30.7 0.0 collective-permute-done.7.refs_2_
  30.7 1.9 %project.1 = (f32[16,4608]{1,0:T(8,128)S(1)}, bf16[16,4608]{1,0:T(8,128)(2,1)S(1)}, bf16[16,4608]{1,0:T(8,128)(2,1)S(1)}, bf16[16,4608]{1,0:T(8,128)(2,1)S(1)}) custom-call(s32[1]{0:T(128)} %bitcast.z_ref, bf16[9,64,128]{2,1,0:T(8,128)(2,1)S(1)} %collective-permute-done.4.refs_0_, bf16[9,64,128]{2,1,0:T(8,128)(2,1)S(1)} %collective-permute-done.5.refs_1_, ...), custom_call_target="tpu_custom_call" | custom-call | tf_op jit(solution)/shard_map/project/pallas_call | solution.py:265
  32.6 1.3 %collective-permute-start.8 = (bf16[16,4608]{1,0:T(8,128)(2,1)S(1)}, bf16[16,4608]{1,0:T(8,128)(2,1)S(1)}, u32[]{:S(2)}, u32[]{:S(2)}) collective-permute-start(bf16[16,4608]{1,0:T(8,128)(2,1)S(1)} %get-tuple-element.58), channel_id=1, source_target_pairs={{0,1},{1,2},{2,3},{3,0},{4,5},{5,6},{6,7},{7,4},{8,9},{9,10},{10,1... | collective-permute-start | bytes 442376 | tf_op jit(solution)/shard_map/ppermute | solution.py:356
  34.0 1.1 %collective-permute-start.9 = (bf16[16,4608]{1,0:T(8,128)(2,1)S(1)}, bf16[16,4608]{1,0:T(8,128)(2,1)S(1)}, u32[]{:S(2)}, u32[]{:S(2)}) collective-permute-start(bf16[16,4608]{1,0:T(8,128)(2,1)S(1)} %get-tuple-element.59), channel_id=1, source_target_pairs={{0,2},{1,3},{2,0},{3,1},{4,6},{5,7},{6,4},{7,5},{8,10},{9,11},{10,... | collective-permute-start | bytes 442376 | tf_op jit(solution)/shard_map/ppermute | solution.py:356
  35.1 1.4 %collective-permute-start.10 = (bf16[16,4608]{1,0:T(8,128)(2,1)S(1)}, bf16[16,4608]{1,0:T(8,128)(2,1)S(1)}, u32[]{:S(2)}, u32[]{:S(2)}) collective-permute-start(bf16[16,4608]{1,0:T(8,128)(2,1)S(1)} %get-tuple-element.60), channel_id=1, source_target_pairs={{0,3},{1,0},{2,1},{3,2},{4,7},{5,4},{6,5},{7,6},{8,11},{9,8},{10,9... | collective-permute-start | bytes 442376 | tf_op jit(solution)/shard_map/ppermute | solution.py:356
  36.5 0.0 copy-done.4
  36.5 0.2 collective-permute-done.8.refs_1_
  36.7 3.4 %collective-permute-done.9.refs_2_ = bf16[16,4608]{1,0:T(8,128)(2,1)S(1)} collective-permute-done((bf16[16,4608]{1,0:T(8,128)(2,1)S(1)}, bf16[16,4608]{1,0:T(8,128)(2,1)S(1)}, u32[]{:S(2)}, u32[]{:S(2)}) %collective-permute-start.9) | collective-permute-done | bytes 147488 | tf_op jit(solution)/shard_map/ppermute | solution.py:356
  40.1 8.7 %collective-permute-done.10.refs_3_ = bf16[16,4608]{1,0:T(8,128)(2,1)S(1)} collective-permute-done((bf16[16,4608]{1,0:T(8,128)(2,1)S(1)}, bf16[16,4608]{1,0:T(8,128)(2,1)S(1)}, u32[]{:S(2)}, u32[]{:S(2)}) %collective-permute-start.10) | collective-permute-done | bytes 147488 | tf_op jit(solution)/shard_map/ppermute | solution.py:356
  48.8 0.0 copy-done.1
  48.8 0.9 %finish.1 = bf16[16,4608]{1,0:T(8,128)(2,1)} custom-call(f32[16,4608]{1,0:T(8,128)S(1)} %get-tuple-element.57.refs_0_, bf16[16,4608]{1,0:T(8,128)(2,1)S(1)} %collective-permute-done.8.refs_1_, bf16[16,4608]{1,0:T(8,128)(2,1)S(1)} %collective-permute-done.9.refs_2_, bf16[16,4608]{1,0:T(8,128)(2,1)S(1)} %collective-permute-done.10.refs_3_, ...), custom_call_target="tpu_custom_call" | custom-call | tf_op jit(solution)/shard_map/finish/pallas_call | solution.py:287
  (1 shorter events, 0.0 us)
Async XLA Ops:
  0.0 2.4 %copy-start = (bf16[64,8,128]{2,1,0:T(8,128)(2,1)S(1)}, bf16[64,8,128]{2,1,0:T(8,128)(2,1)}, u32[]{:S(2)}) copy-start(bf16[64,8,128]{2,1,0:T(8,128)(2,1)} %param.10) | copy-start | bytes 393220
  0.0 8.9 %copy-start.2 = (s32[64,1]{0,1:T(1,128)S(1)}, s32[64,1]{0,1:T(1,128)}, u32[]{:S(2)}) copy-start(s32[64,1]{0,1:T(1,128)} %param.15) | copy-start | bytes 772
  1.6 7.3 %collective-permute-start = (bf16[8,4,128,128]{3,2,1,0:T(8,128)(2,1)S(1)}, bf16[8,4,128,128]{3,2,1,0:T(8,128)(2,1)S(1)}, u32[]{:S(2)}, u32[]{:S(2)}) collective-permute-start(bf16[8,4,128,128]{3,2,1,0:T(8,128)(2,1)S(1)} %get-tuple-element.41.refs_4_.refs_6_.refs_2_), channel_id=1, source_target_pairs={{0,4},{4,0},{8,12},{12,8},{16,20},{20,16},{24,28},{28,24},{1,5},{5... | collective-permute-start | bytes 3145736 | tf_op jit(solution)/shard_map/ppermute | solution.py:314
  2.3 6.6 %collective-permute-start.1 = (bf16[8,4,128,128]{3,2,1,0:T(8,128)(2,1)S(1)}, bf16[8,4,128,128]{3,2,1,0:T(8,128)(2,1)}, u32[]{:S(2)}, u32[]{:S(2)}) collective-permute-start(bf16[8,4,128,128]{3,2,1,0:T(8,128)(2,1)S(1)} %get-tuple-element.42.refs_5_.refs_7_.refs_3_), channel_id=1, source_target_pairs={{0,4},{4,0},{8,12},{12,8},{16,20},{20,16},{24,28},{28,24},{1,5},{5... | collective-permute-start | bytes 3145736 | tf_op jit(solution)/shard_map/ppermute | solution.py:314
  2.4 11.8 %collective-permute-start.2 = (bf16[512,128]{1,0:T(8,128)(2,1)S(1)}, bf16[512,128]{1,0:T(8,128)(2,1)S(1)}, u32[]{:S(2)}, u32[]{:S(2)}) collective-permute-start(bf16[512,128]{1,0:T(8,128)(2,1)S(1)} %bitcast.4), channel_id=1, source_target_pairs={{0,24},{4,28},{8,16},{12,20},{16,8},{20,12},{24,0},{28,4},{1,25},{... | collective-permute-start | bytes 393224 | tf_op jit(solution)/shard_map/ppermute | solution.py:318
  4.6 9.7 %collective-permute-start.3 = (bf16[512,128]{1,0:T(8,128)(2,1)S(1)}, bf16[512,128]{1,0:T(8,128)(2,1)S(1)}, u32[]{:S(2)}, u32[]{:S(2)}) collective-permute-start(bf16[512,128]{1,0:T(8,128)(2,1)S(1)} %bitcast.5), channel_id=1, source_target_pairs={{0,8},{4,12},{8,0},{12,4},{16,24},{20,28},{24,16},{28,20},{1,9},{5... | collective-permute-start | bytes 393224 | tf_op jit(solution)/shard_map/ppermute | solution.py:318
  4.9 17.3 %collective-permute-start.6 = (bf16[512,128]{1,0:T(8,128)(2,1)S(1)}, bf16[512,128]{1,0:T(8,128)(2,1)}, u32[]{:S(2)}, u32[]{:S(2)}) collective-permute-start(bf16[512,128]{1,0:T(8,128)(2,1)S(1)} %bitcast.6), channel_id=1, source_target_pairs={{0,16},{4,20},{8,24},{12,28},{16,0},{20,4},{24,8},{28,12},{1,17},{... | collective-permute-start | bytes 393224 | tf_op jit(solution)/shard_map/ppermute | solution.py:318
  14.3 10.9 %copy-start.3 = (s32[64]{0:T(128)S(1)}, s32[64]{0:T(128)}, u32[]{:S(2)}) copy-start(s32[64]{0:T(128)} %lengths_ref.1) | copy-start | bytes 772
  19.6 11.0 %collective-permute-start.4 = (bf16[9,64,128]{2,1,0:T(8,128)(2,1)S(1)}, bf16[9,64,128]{2,1,0:T(8,128)(2,1)S(1)}, u32[]{:S(2)}, u32[]{:S(2)}) collective-permute-start(bf16[9,64,128]{2,1,0:T(8,128)(2,1)S(1)} %get-tuple-element.47), channel_id=1, source_target_pairs={{24,0},{28,4},{16,8},{20,12},{8,16},{12,20},{0,24},{4,28},{25,1},{... | collective-permute-start | bytes 442376 | tf_op jit(solution)/shard_map/ppermute | solution.py:348
  21.9 8.8 %collective-permute-start.5 = (bf16[9,64,128]{2,1,0:T(8,128)(2,1)S(1)}, bf16[9,64,128]{2,1,0:T(8,128)(2,1)S(1)}, u32[]{:S(2)}, u32[]{:S(2)}) collective-permute-start(bf16[9,64,128]{2,1,0:T(8,128)(2,1)S(1)} %get-tuple-element.48), channel_id=1, source_target_pairs={{8,0},{12,4},{0,8},{4,12},{24,16},{28,20},{16,24},{20,28},{9,1},{1... | collective-permute-start | bytes 442376 | tf_op jit(solution)/shard_map/ppermute | solution.py:348
  24.9 5.8 %collective-permute-start.7 = (bf16[9,64,128]{2,1,0:T(8,128)(2,1)S(1)}, bf16[9,64,128]{2,1,0:T(8,128)(2,1)S(1)}, u32[]{:S(2)}, u32[]{:S(2)}) collective-permute-start(bf16[9,64,128]{2,1,0:T(8,128)(2,1)S(1)} %hot_pages.5), channel_id=1, source_target_pairs={{16,0},{20,4},{24,8},{28,12},{0,16},{4,20},{8,24},{12,28},{17,1},{... | collective-permute-start | bytes 442376 | tf_op jit(solution)/shard_map/ppermute | solution.py:348
  30.6 5.8 %copy-start.4 = (f32[4608]{0:T(1024)S(1)}, f32[4608]{0:T(1024)}, u32[]{:S(2)}) copy-start(f32[4608]{0:T(1024)} %param.19) | copy-start | bytes 55300
  30.7 18.1 %copy-start.1 = (bf16[16,4608]{1,0:T(8,128)(2,1)S(1)}, bf16[16,4608]{1,0:T(8,128)(2,1)}, u32[]{:S(2)}) copy-start(bf16[16,4608]{1,0:T(8,128)(2,1)} %refs_4_.1) | copy-start | bytes 442372
  32.6 4.0 %collective-permute-start.8 = (bf16[16,4608]{1,0:T(8,128)(2,1)S(1)}, bf16[16,4608]{1,0:T(8,128)(2,1)S(1)}, u32[]{:S(2)}, u32[]{:S(2)}) collective-permute-start(bf16[16,4608]{1,0:T(8,128)(2,1)S(1)} %get-tuple-element.58), channel_id=1, source_target_pairs={{0,1},{1,2},{2,3},{3,0},{4,5},{5,6},{6,7},{7,4},{8,9},{9,10},{10,1... | collective-permute-start | bytes 442376 | tf_op jit(solution)/shard_map/ppermute | solution.py:356
  34.0 6.1 %collective-permute-start.9 = (bf16[16,4608]{1,0:T(8,128)(2,1)S(1)}, bf16[16,4608]{1,0:T(8,128)(2,1)S(1)}, u32[]{:S(2)}, u32[]{:S(2)}) collective-permute-start(bf16[16,4608]{1,0:T(8,128)(2,1)S(1)} %get-tuple-element.59), channel_id=1, source_target_pairs={{0,2},{1,3},{2,0},{3,1},{4,6},{5,7},{6,4},{7,5},{8,10},{9,11},{10,... | collective-permute-start | bytes 442376 | tf_op jit(solution)/shard_map/ppermute | solution.py:356
  35.1 13.7 %collective-permute-start.10 = (bf16[16,4608]{1,0:T(8,128)(2,1)S(1)}, bf16[16,4608]{1,0:T(8,128)(2,1)S(1)}, u32[]{:S(2)}, u32[]{:S(2)}) collective-permute-start(bf16[16,4608]{1,0:T(8,128)(2,1)S(1)} %get-tuple-element.60), channel_id=1, source_target_pairs={{0,3},{1,0},{2,1},{3,2},{4,7},{5,4},{6,5},{7,6},{8,11},{9,8},{10,9... | collective-permute-start | bytes 442376 | tf_op jit(solution)/shard_map/ppermute | solution.py:356

commit v3 on v2

--- a/solution.py
+++ b/solution.py
@@ -64,9 +64,10 @@
 
 
 def own_kernel(
-    seqs, ups, heads, group, kv_heads, unroll,
-    lengths_ref, q_ref, kbuf, vbuf, w_hbm, num_ref, tot_ref, w_ref, sem,
+    seqs, ups, heads, group, kv_heads,
+    lengths_ref, q_ref, kbuf, *refs,
 ):
+    *vbufs, w_hbm, num_ref, tot_ref, w_ref, sem = refs
     page_len, head_dim = kbuf.shape[2], kbuf.shape[3]
     width = kv_heads * page_len
     prefetch = pltpu.make_async_copy(w_hbm, w_ref, sem)
@@ -77,22 +78,29 @@
     token = jnp.where(mine, column % page_len, ups * page_len)
     ones = jnp.ones((width, head_dim), jnp.bfloat16)
 
-    def block(b, carry):
-        for j in range(unroll):
-            s = b * unroll + j
-            q = q_ref[pl.ds(pl.multiple_of(s * heads, heads), heads), :]
-            total = jnp.zeros((heads, 2 * head_dim), jnp.float32)
-            for u in range(ups):
-                k = kbuf[s * ups + u].reshape(width, head_dim)
-                v = vbuf[s * ups + u].reshape(width, head_dim)
-                allowed = token < lengths_ref[s] - u * page_len
-                weight = jnp.where(allowed, weights_of(dot_t(q, k)), 0.0).astype(jnp.bfloat16)
-                total = total + dot_n(weight, jnp.concatenate([v, ones], axis=1))
-            num_ref[pl.ds(s, heads, stride=seqs), :] = total[:, :head_dim]
-            tot_ref[pl.ds(s, heads, stride=seqs), :] = total[:, head_dim:]
-        return carry
-
-    lax.fori_loop(0, seqs // unroll, block, 0)
+    done = 0
+    for vbuf in vbufs:
+        part = vbuf.shape[0] // ups
+        unroll = math.gcd(part, 16)
+
+        def block(b, carry, first=done, unroll=unroll, vbuf=vbuf):
+            for j in range(unroll):
+                at = b * unroll + j
+                s = first + at
+                q = q_ref[pl.ds(pl.multiple_of(s * heads, heads), heads), :]
+                total = jnp.zeros((heads, 2 * head_dim), jnp.float32)
+                for u in range(ups):
+                    k = kbuf[s * ups + u].reshape(width, head_dim)
+                    v = vbuf[at * ups + u].reshape(width, head_dim)
+                    allowed = token < lengths_ref[s] - u * page_len
+                    weight = jnp.where(allowed, weights_of(dot_t(q, k)), 0.0).astype(jnp.bfloat16)
+                    total = total + dot_n(weight, jnp.concatenate([v, ones], axis=1))
+                num_ref[pl.ds(s, heads, stride=seqs), :] = total[:, :head_dim]
+                tot_ref[pl.ds(s, heads, stride=seqs), :] = total[:, head_dim:]
+            return carry
+
+        lax.fori_loop(0, part // unroll, block, 0)
+        done += part
     prefetch.wait()
 
 
@@ -102,24 +110,45 @@
     group = q.shape[1] // kv_heads
     heads = -(-q.shape[1] // 8) * 8
     q = jnp.pad(q, ((0, 0), (0, heads - q.shape[1]), (0, 0))).reshape(seqs * heads, head_dim)
-    unroll = math.gcd(seqs, 32)
     out = jax.ShapeDtypeStruct((heads * seqs, head_dim), jnp.float32)
     num, tot, w = pl.pallas_call(
-        functools.partial(own_kernel, seqs, count // seqs, heads, group, kv_heads, unroll),
+        functools.partial(own_kernel, seqs, count // seqs, heads, group, kv_heads),
         out_shape=(out, out, jax.ShapeDtypeStruct(o_weight.shape, o_weight.dtype)),
-        in_specs=[SMEM, VMEM, VMEM, VMEM, HBM],
+        in_specs=[SMEM, VMEM, VMEM] + [VMEM] * len(own_v) + [HBM],
         out_specs=(VMEM, VMEM, VMEM),
         scratch_shapes=[pltpu.SemaphoreType.DMA],
         compiler_params=pltpu.CompilerParams(vmem_limit_bytes=8 * MIB),
         name="own_pages",
-    )(lengths, q, own_k, own_v, in_hbm(o_weight))
+    )(lengths, q, own_k, *own_v, in_hbm(o_weight))
     return (num, tot), w
 
 
-def hot_kernel(sources, seqs, heads, kv_heads, packed, fetch, pos_ref, *refs):
+def shared_places(me, cap, page_count, hot_ref, lanes):
+    shape = (2 * cap, hot_ref.shape[1])
+    slot = lax.broadcasted_iota(jnp.int32, shape, 0)
+    lane = lax.broadcasted_iota(jnp.int32, shape, 1).astype(jnp.float32)
+    first = jnp.where(slot < cap, me * page_count, (me ^ 1) * page_count - cap)
+    matches = jnp.broadcast_to(hot_ref[...], shape) == first + slot
+    place = jnp.min(jnp.where(matches, lane, 1e9), axis=1, keepdims=True)
+    return jnp.broadcast_to(place, (2 * cap, lanes))
+
+
+def used_column(origin, seqs, used_ref, lanes):
+    span = used_ref.shape[1]
+    row = used_ref[pl.ds(origin * seqs // span, 1), :].astype(jnp.float32)
+    shape = (seqs, span)
+    lane = lax.broadcasted_iota(jnp.int32, shape, 1)
+    sequence = lax.broadcasted_iota(jnp.int32, shape, 0) + origin * seqs % span
+    picked = jnp.where(lane == sequence, jnp.broadcast_to(row, shape), 0.0)
+    return jnp.broadcast_to(jnp.sum(picked, axis=1, keepdims=True), (seqs, lanes))
+
+
+def hot_kernel(
+    sources, seqs, heads, kv_heads, packed, fetch, shifts, page_count, hot_ref, used_ref, *refs
+):
     if fetch:
         pages_ref, cache_ref, *refs = refs
-        *refs, pages_out, staged, sems = refs
+        *refs, pages_out, staged, places, sems = refs
 
         def copy(i):
             return pltpu.make_async_copy(cache_ref.at[pages_ref[i]], pages_out.at[i], sems.at[i])
@@ -134,17 +163,18 @@
 
         lax.fori_loop(0, fetch, start, 0)
     else:
-        *refs, staged = refs
-    used = refs[:sources]
-    queries = refs[sources : 2 * sources]
-    halves = (refs[2 * sources : 2 * sources + 2], refs[2 * sources + 2 : 2 * sources + 4])
-    outs = refs[2 * sources + 4 :]
+        *refs, staged, places = refs
+    queries = refs[:sources]
+    halves = (refs[sources : sources + 2], refs[sources + 2 : sources + 4])
+    outs = refs[sources + 4 :]
     group = heads // kv_heads
     cap, _, page_len, head_dim = halves[0][0].shape
     lane = lax.broadcasted_iota(jnp.int32, (seqs, head_dim), 1)
     for r in range(sources):
         staged[r] = queries[r][...].astype(jnp.float32)
-    used_rows = [u[...] for u in used]
+    me = lax.axis_index("pages")
+    places[...] = shared_places(me, cap, page_count, hot_ref, head_dim)
+    used_rows = [used_column(shift(me), seqs, used_ref, head_dim) for shift in shifts]
     step = 2
     ones = jnp.ones((step * page_len, head_dim), jnp.bfloat16)
     totals = [jnp.zeros((seqs, head_dim), jnp.float32) for _ in range(sources)]
@@ -163,7 +193,8 @@
                 weight = weights_of(dot_t(q, k))
                 parts = []
                 for p in range(step):
-                    place = pos_ref[half * cap + c + p]
+                    slot = half * cap + c + p
+                    place = jnp.broadcast_to(places[slot : slot + 1, :], (seqs, page_len))
                     columns = slice(p * page_len, (p + 1) * page_len)
                     part = []
                     for r in range(sources):
@@ -193,27 +224,33 @@
         lax.fori_loop(0, fetch, wait, 0)
 
 
-def hot_terms(queries, used, position, own_kv, partner_kv, packed, pages=None, cache=None):
+def hot_terms(queries, shifts, page_count, tables, own_kv, partner_kv, packed, fetch=()):
     sources = len(queries)
-    seqs = used[0].shape[0]
     _, kv_heads, page_len, head_dim = own_kv[0].shape
-    heads = queries[0].shape[0] // seqs
+    seqs, heads = queries[0].shape[:2]
     if packed:
         shapes = [((heads + 1, seqs, head_dim), jnp.bfloat16)] * sources
     else:
         shapes = [((heads * seqs, head_dim), jnp.float32)] * (2 * sources)
-    scratch = [pltpu.VMEM((sources, seqs * heads, head_dim), jnp.float32)]
-    operands = [position, *used, *queries, *own_kv, *partner_kv]
-    specs = [SMEM] + [VMEM] * (2 * sources + 4)
+    scratch = [
+        pltpu.VMEM((sources, seqs * heads, head_dim), jnp.float32),
+        pltpu.VMEM((2 * HOT_CAP, head_dim), jnp.float32),
+    ]
+    flat = [q.reshape(seqs * heads, head_dim) for q in queries]
+    operands = [*tables, *flat, *own_kv, *partner_kv]
+    specs = [VMEM] * len(operands)
     count = 0
-    if pages is not None:
+    if fetch:
+        pages, cache = fetch
         count = pages.shape[0]
-        operands[1:1] = [pages, in_hbm(cache)]
-        specs[1:1] = [SMEM, HBM]
+        operands[2:2] = [pages, in_hbm(cache)]
+        specs[2:2] = [SMEM, HBM]
         shapes.append(((count, kv_heads, page_len, head_dim), cache.dtype))
         scratch.append(pltpu.SemaphoreType.DMA((count,)))
     return pl.pallas_call(
-        functools.partial(hot_kernel, sources, seqs, heads, kv_heads, packed, count),
+        functools.partial(
+            hot_kernel, sources, seqs, heads, kv_heads, packed, count, shifts, page_count
+        ),
         out_shape=[jax.ShapeDtypeStruct(*s) for s in shapes],
         in_specs=specs,
         out_specs=[VMEM] * len(shapes),
@@ -223,7 +260,15 @@
     )(*operands)
 
 
-def project_kernel(received, seqs, heads, ways, z_ref, *refs):
+def row_owner(i, k, ways):
+    return i ^ k if ways & (ways - 1) == 0 else lax.rem(i + k, ways)
+
+
+def row_order(ways):
+    return [2, 3, 1] if ways == 4 else list(range(ways - 1, 0, -1))
+
+
+def project_kernel(received, seqs, heads, ways, *refs):
     blocks = refs[:received]
     own_num, own_tot, hot_num, hot_tot, w_ref = refs[received : received + 5]
     outs = refs[received + 5 : received + 5 + ways]
@@ -244,7 +289,7 @@
         spread[:, h * head_dim : (h + 1) * head_dim] = num / tot
     turned = []
     for k in range(ways):
-        target = lax.rem(z_ref[0] + k, ways)
+        target = row_owner(lax.axis_index("heads"), k, ways)
         turned.append(spread[pl.ds(pl.multiple_of(target * rows, rows), rows), :])
     att = jnp.concatenate(turned, axis=0).astype(jnp.bfloat16)
     model = w_ref.shape[1]
@@ -255,7 +300,7 @@
             outs[k][:, n : n + tile] = res[k * rows : (k + 1) * rows].astype(outs[k].dtype)
 
 
-def project(blocks, own, hot, o_weight, z, ways):
+def project(blocks, own, hot, o_weight, ways):
     head_dim = own[0].shape[1]
     width, model = o_weight.shape
     heads = width // head_dim
@@ -265,12 +310,12 @@
     return pl.pallas_call(
         functools.partial(project_kernel, len(blocks), seqs, heads, ways),
         out_shape=[jax.ShapeDtypeStruct((rows, model), kind) for kind in kinds],
-        in_specs=[SMEM] + [VMEM] * (len(blocks) + 5),
+        in_specs=[VMEM] * (len(blocks) + 5),
         out_specs=[VMEM] * ways,
         scratch_shapes=[pltpu.VMEM((seqs, width), jnp.float32)],
         compiler_params=pltpu.CompilerParams(vmem_limit_bytes=8 * MIB),
         name="project",
-    )(z, *blocks, *own, *hot, o_weight)
+    )(*blocks, *own, *hot, o_weight)
 
 
 def norm_kernel(*refs):
@@ -295,10 +340,7 @@
 def layer(
     chips, ways, queries, keys, values, hot_pages, hot_used, user_pages, lengths, o_weight, residual, norm_gain
 ):
-    seqs, heads, head_dim = queries.shape
     page_count = keys.shape[0]
-    me = lax.axis_index("pages")
-    z = lax.axis_index("heads")
     devices = 2 * chips
     swap = [(i, i ^ 1) for i in range(devices)]
     power = chips & (chips - 1) == 0
@@ -306,56 +348,50 @@
     def there(i, k):
         return i ^ (2 * k) if power else (i + 2 * k) % devices
 
-    q = queries.reshape(seqs * heads, head_dim)
     pages = user_pages.reshape(-1)
     out_perm = [[(i, there(i, k)) for i in range(devices)] for k in range(chips)]
     back_perm = [[(j, i) for i, j in perm] for perm in out_perm]
     own_kv = lead_pages(keys, values)
     partner_kv = tuple(lax.ppermute(x, "pages", swap) for x in own_kv)
-    q, own_kv = lax.optimization_barrier((q, own_kv))
-    late = [2] if chips > 2 else []
-    soon = [k for k in reversed(range(1, chips)) if k not in late]
-    far_q = {k: lax.ppermute(q, "pages", out_perm[k]) for k in soon + late}
-
-    slot = jnp.arange(2 * HOT_CAP, dtype=jnp.int32)
-    holder = jnp.where(slot < HOT_CAP, me, me ^ 1)
-    page_ids = holder * page_count + slot % HOT_CAP
-    matches = page_ids[:, None] == hot_pages[None, :]
-    order = jnp.arange(hot_pages.shape[0], dtype=jnp.int32)
-    absent = jnp.int32(jnp.iinfo(jnp.int32).max)
-    position = jnp.min(jnp.where(matches, order[None, :], absent), axis=1)
-
-    def used_of(k):
-        origin = me ^ (2 * k) if power else lax.rem(me + devices - 2 * k, devices)
-        row = lax.dynamic_slice_in_dim(hot_used, origin * seqs, seqs)
-        return jnp.broadcast_to(row[:, None], (seqs, head_dim))
-
-    used = [used_of(k) for k in range(chips)]
-    turn, position, used = lax.optimization_barrier((z.reshape(1), position, used))
-    *hot, own_k = hot_terms([q], [used[0]], position, own_kv, partner_kv, False, pages, keys)
-    blocks = []
-    own_v = None
+    q, own_kv = lax.optimization_barrier((queries, own_kv))
+    late = [chips - 1] if chips > 2 else []
+    soon = [k for k in range(1, chips) if k not in late]
+    far_q = {}
+    for k in soon + late:
+        far_q[k] = lax.ppermute(q, "pages", out_perm[k])
+
+    def shift(k):
+        if power:
+            return lambda i: i ^ (2 * k)
+        return lambda i: lax.rem(i + devices - 2 * k, devices)
+
+    tables = (hot_pages.reshape(1, -1), hot_used.reshape(-1, 128))
+    *hot, own_k = hot_terms(
+        [queries], [shift(0)], page_count, tables, own_kv, partner_kv, False, (pages, keys)
+    )
+    groups = [ks for ks in (soon, late) if ks]
+    blocks, own_v = [], []
     before = hot
-    for ks in (soon, late):
-        if not ks:
-            continue
+    half = pages.shape[0] // 2 if len(groups) == 2 else pages.shape[0]
+    for n, ks in enumerate(groups):
         before, arrived = lax.optimization_barrier((before, [far_q[k] for k in ks]))
-        rest = (pages, values) if own_v is None else ()
-        sent = hot_terms(arrived, [used[k] for k in ks], position, own_kv, partner_kv, True, *rest)
-        if rest:
-            *sent, own_v = sent
+        fetch = (pages[n * half : (n + 1) * half], values)
+        *sent, part = hot_terms(
+            arrived, [shift(k) for k in ks], page_count, tables, own_kv, partner_kv, True, fetch
+        )
+        own_v.append(part)
         for k, b in zip(ks, sent):
             blocks.append(lax.ppermute(b, "pages", back_perm[k]))
         before = sent
-    if own_v is None:
-        own_v = jnp.take(values, pages, axis=0)
+    if not groups:
+        own_v = [jnp.take(values, pages, axis=0)]
     queries, before = lax.optimization_barrier((queries, before))
     own, weight = own_terms(queries, own_k, own_v, lengths, o_weight)
-    parts = project(blocks, own, hot, weight, turn, ways)
-    arrived = [parts[0]] + [
-        lax.ppermute(parts[k], "heads", [(i, (i + k) % ways) for i in range(ways)])
-        for k in range(1, ways)
-    ]
+    parts = project(blocks, own, hot, weight, ways)
+    arrived = [parts[0]]
+    for k in row_order(ways):
+        pairs = [(i, i ^ k if ways & (ways - 1) == 0 else (i + k) % ways) for i in range(ways)]
+        arrived.append(lax.ppermute(parts[k], "heads", pairs))
     return finish(arrived, residual, norm_gain)
 
 

time: 49.9 us -> 47 us (0.942)
  the two profiles are of different devices: /device:TPU:9 before, /device:TPU:0 now
where the time goes in v3:
time: 47 us; the launch traced here: 46.6 us
  Pallas kernels  22 us (47%)
  starting transfers between devices  13.1 us (28%)
  waiting for transfers between devices  11.3 us (24%)
    pallas_call x3, Pallas kernels, hot_terms(): pl.pallas_call(functools.partial(hot_kernel, sources, seqs, heads, kv_hea...  11.5 us
    ppermute x3, waiting for transfers between devices, layer(): arrived.append(lax.ppermute(parts[k], 'heads', pairs))  9.55 us
    pallas_call x1, Pallas kernels, own_terms(): pl.pallas_call(functools.partial(own_kernel, seqs, count // seqs, heads,...  6 us
    ppermute x3, starting transfers between devices, layer(): arrived.append(lax.ppermute(parts[k], 'heads', pairs))  4.45 us
    ppermute x3, starting transfers between devices, layer(): far_q[k] = lax.ppermute(q, 'pages', out_perm[k])  4.43 us
    ppermute x3, starting transfers between devices, layer(): blocks.append(lax.ppermute(b, 'pages', back_perm[k]))  3.55 us
    pallas_call x1, Pallas kernels, project(): pl.pallas_call(functools.partial(project_kernel, len(blocks), seqs, heads...  1.98 us
    ppermute x3, waiting for transfers between devices, layer(): far_q[k] = lax.ppermute(q, 'pages', out_perm[k])  1.74 us
  transfers between devices with their start and end apart: 11, of which 3 were waited for; matrix products, arithmetic and copies ran while one was open for 0% of the time, Pallas kernels for 31%

profile of v3, /device:TPU:0, one launch (start us, length us, event | category | flops | bytes accessed | tf_op | source)
XLA Modules:
  0.0 46.6 jit_solution(2284177314936723248)
XLA Ops:
  0.0 0.0 copy-start
  0.0 0.0 copy-start.4
  0.0 0.0 copy-start.3
  0.0 0.0 copy-start.2
  0.0 1.6 %lead_pages.1 = (bf16[8,4,128,128]{3,2,1,0:T(8,128)(2,1)S(1)}, bf16[8,4,128,128]{3,2,1,0:T(8,128)(2,1)S(1)}) custom-call(bf16[72,4,128,128]{3,2,1,0:T(8,128)(2,1)} %refs_1_.3, bf16[72,4,128,128]{3,2,1,0:T(8,128)(2,1)} %refs_1_.5), custom_call_target="tpu_custom_call" | custom-call | tf_op jit(solution)/shard_map/lead_pages/pallas_call | solution.py:55
  1.6 0.6 %collective-permute-start = (bf16[8,4,128,128]{3,2,1,0:T(8,128)(2,1)S(1)}, bf16[8,4,128,128]{3,2,1,0:T(8,128)(2,1)S(1)}, u32[]{:S(2)}, u32[]{:S(2)}) collective-permute-start(bf16[8,4,128,128]{3,2,1,0:T(8,128)(2,1)S(1)} %get-tuple-element.31.refs_3_.refs_4_), channel_id=1, source_target_pairs={{0,4},{4,0},{8,12},{12,8},{16,20},{20,16},{24,28},{28,24},{1,5},{5... | collective-permute-start | bytes 3145736 | tf_op jit(solution)/shard_map/ppermute | solution.py:355
  2.2 0.1 collective-permute-start.1
  2.3 0.0 copy-done
  2.3 2.9 %collective-permute-start.2 = (bf16[64,8,128]{2,1,0:T(8,128)(2,1)S(1)}, bf16[64,8,128]{2,1,0:T(8,128)(2,1)S(1)}, u32[]{:S(2)}, u32[]{:S(2)}) collective-permute-start(bf16[64,8,128]{2,1,0:T(8,128)(2,1)S(1)} %copy-done), channel_id=1, source_target_pairs={{0,8},{4,12},{8,0},{12,4},{16,24},{20,28},{24,16},{28,20},{1,9},{5... | collective-permute-start | bytes 393224 | tf_op jit(solution)/shard_map/ppermute | solution.py:361
  5.2 1.5 %collective-permute-start.3 = (bf16[64,8,128]{2,1,0:T(8,128)(2,1)S(1)}, bf16[64,8,128]{2,1,0:T(8,128)(2,1)S(1)}, u32[]{:S(2)}, u32[]{:S(2)}) collective-permute-start(bf16[64,8,128]{2,1,0:T(8,128)(2,1)S(1)} %copy-done), channel_id=1, source_target_pairs={{0,16},{4,20},{8,24},{12,28},{16,0},{20,4},{24,8},{28,12},{1,17},{... | collective-permute-start | bytes 393224 | tf_op jit(solution)/shard_map/ppermute | solution.py:361
  6.7 0.0 collective-permute-start.6
  6.7 0.0 copy-done.4
  6.7 0.1 slice_bitcast_fusion
  6.8 0.0 collective-permute-done.refs_5_.refs_6_
  6.8 0.0 collective-permute-done.1.refs_6_.refs_7_
  6.8 0.0 copy-done.3
  6.8 0.0 copy-done.2
  6.8 4.6 %hot_pages.3 = (f32[512,128]{1,0:T(8,128)S(1)}, f32[512,128]{1,0:T(8,128)S(1)}, bf16[64,4,128,128]{3,2,1,0:T(8,128)(2,1)S(1)}) custom-call(s32[1,64]{1,0:T(1,128)S(1)} %bitcast.20, s32[4,128]{1,0:T(4,128)S(1)} %bitcast.17, s32[64]{0:T(128)S(1)} %bitcast.23, bf16[72,4,128,128]{3,2,1,0:T(8,128)(2,1)} %refs_1_.3, bf16[512,128]{1,0:T(8,128)(2,1)S(1)} %bitcast.12, ...), custom_call_target="tpu_custom_call" | custom-call | tf_op jit(solution)/shard_map/hot_pages/pallas_call | solution.py:250
  11.4 0.0 collective-permute-done.2
  11.4 1.7 %collective-permute-done.3 = bf16[64,8,128]{2,1,0:T(8,128)(2,1)S(1)} collective-permute-done((bf16[64,8,128]{2,1,0:T(8,128)(2,1)S(1)}, bf16[64,8,128]{2,1,0:T(8,128)(2,1)S(1)}, u32[]{:S(2)}, u32[]{:S(2)}) %collective-permute-start.3) | collective-permute-done | bytes 131104 | tf_op jit(solution)/shard_map/ppermute | solution.py:361
  13.2 3.8 %hot_pages.4 = (bf16[9,64,128]{2,1,0:T(8,128)(2,1)S(1)}, bf16[9,64,128]{2,1,0:T(8,128)(2,1)S(1)}, bf16[32,4,128,128]{3,2,1,0:T(8,128)(2,1)S(1)}) custom-call(s32[1,64]{1,0:T(1,128)S(1)} %bitcast.21, s32[4,128]{1,0:T(4,128)S(1)} %bitcast.18, s32[32]{0:T(128)S(1)} %get-tuple-element.54.refs_0_, bf16[72,4,128,128]{3,2,1,0:T(8,128)(2,1)} %refs_1_.5, ...), custom_call_target="tpu_custom_call" | custom-call | tf_op jit(solution)/shard_map/hot_pages/pallas_call | solution.py:250
  17.0 0.0 copy-start.5
  17.0 0.0 collective-permute-done.6
  17.0 3.1 %hot_pages.5 = (bf16[9,64,128]{2,1,0:T(8,128)(2,1)S(1)}, bf16[32,4,128,128]{3,2,1,0:T(8,128)(2,1)S(1)}) custom-call(s32[1,64]{1,0:T(1,128)S(1)} %bitcast.22, s32[4,128]{1,0:T(4,128)S(1)} %bitcast.19, s32[32]{0:T(128)S(1)} %get-tuple-element.53.refs_0_, bf16[72,4,128,128]{3,2,1,0:T(8,128)(2,1)} %refs_1_.5, bf16[512,128]{1,0:T(8,128)(2,1)S(1)} %bitcast.14, ...), custom_call_target="tpu_custom_call" | custom-call | tf_op jit(solution)/shard_map/hot_pages/pallas_call | solution.py:250
  20.1 1.6 %collective-permute-start.7 = (bf16[9,64,128]{2,1,0:T(8,128)(2,1)S(1)}, bf16[9,64,128]{2,1,0:T(8,128)(2,1)S(1)}, u32[]{:S(2)}, u32[]{:S(2)}) collective-permute-start(bf16[9,64,128]{2,1,0:T(8,128)(2,1)S(1)} %get-tuple-element.41), channel_id=1, source_target_pairs={{24,0},{28,4},{16,8},{20,12},{8,16},{12,20},{0,24},{4,28},{25,1},{... | collective-permute-start | bytes 442376 | tf_op jit(solution)/shard_map/ppermute | solution.py:384
  21.7 1.5 %collective-permute-start.4 = (bf16[9,64,128]{2,1,0:T(8,128)(2,1)S(1)}, bf16[9,64,128]{2,1,0:T(8,128)(2,1)S(1)}, u32[]{:S(2)}, u32[]{:S(2)}) collective-permute-start(bf16[9,64,128]{2,1,0:T(8,128)(2,1)S(1)} %get-tuple-element.38), channel_id=1, source_target_pairs={{8,0},{12,4},{0,8},{4,12},{24,16},{28,20},{16,24},{20,28},{9,1},{1... | collective-permute-start | bytes 442376 | tf_op jit(solution)/shard_map/ppermute | solution.py:384
  23.2 0.5 %collective-permute-start.5 = (bf16[9,64,128]{2,1,0:T(8,128)(2,1)S(1)}, bf16[9,64,128]{2,1,0:T(8,128)(2,1)S(1)}, u32[]{:S(2)}, u32[]{:S(2)}) collective-permute-start(bf16[9,64,128]{2,1,0:T(8,128)(2,1)S(1)} %get-tuple-element.39), channel_id=1, source_target_pairs={{16,0},{20,4},{24,8},{28,12},{0,16},{4,20},{8,24},{12,28},{17,1},{... | collective-permute-start | bytes 442376 | tf_op jit(solution)/shard_map/ppermute | solution.py:384
  23.7 0.0 copy-done.5
  23.7 6.0 %own_pages.1 = (f32[512,128]{1,0:T(8,128)S(1)}, f32[512,128]{1,0:T(8,128)S(1)}, bf16[1024,4608]{1,0:T(8,128)(2,1)S(1)}) custom-call(s32[64]{0:T(128)S(1)} %copy-done.5, bf16[512,128]{1,0:T(8,128)(2,1)S(1)} %bitcast.13, bf16[64,4,128,128]{3,2,1,0:T(8,128)(2,1)S(1)} %get-tuple-element.43.kbuf, bf16[32,4,128,128]{3,2,1,0:T(8,128)(2,1)S(1)} %get-tuple-element.44.refs_0_, ...), custom_call_target="tpu_custom_call" | custom-call | tf_op jit(solution)/shard_map/own_pages/pallas_call | solution.py:114
  29.7 0.0 copy-start.6
  29.7 0.0 copy-start.1
  29.7 0.0 collective-permute-done.7.refs_2_
  29.7 0.0 collective-permute-done.4.refs_0_
  29.7 0.0 collective-permute-done.5.refs_1_
  29.7 2.0 %project.1 = (f32[16,4608]{1,0:T(8,128)S(1)}, bf16[16,4608]{1,0:T(8,128)(2,1)S(1)}, bf16[16,4608]{1,0:T(8,128)(2,1)S(1)}, bf16[16,4608]{1,0:T(8,128)(2,1)S(1)}) custom-call(bf16[9,64,128]{2,1,0:T(8,128)(2,1)S(1)} %collective-permute-done.4.refs_0_, bf16[9,64,128]{2,1,0:T(8,128)(2,1)S(1)} %collective-permute-done.5.refs_1_, ...), custom_call_target="tpu_custom_call" | custom-call | tf_op jit(solution)/shard_map/project/pallas_call | solution.py:310
  31.7 1.6 %collective-permute-start.10 = (bf16[16,4608]{1,0:T(8,128)(2,1)S(1)}, bf16[16,4608]{1,0:T(8,128)(2,1)S(1)}, u32[]{:S(2)}, u32[]{:S(2)}) collective-permute-start(bf16[16,4608]{1,0:T(8,128)(2,1)S(1)} %get-tuple-element.52), channel_id=1, source_target_pairs={{0,1},{1,0},{2,3},{3,2},{4,5},{5,4},{6,7},{7,6},{8,9},{9,8},{10,11... | collective-permute-start | bytes 442376 | tf_op jit(solution)/shard_map/ppermute | solution.py:394
  33.4 2.6 %collective-permute-start.8 = (bf16[16,4608]{1,0:T(8,128)(2,1)S(1)}, bf16[16,4608]{1,0:T(8,128)(2,1)S(1)}, u32[]{:S(2)}, u32[]{:S(2)}) collective-permute-start(bf16[16,4608]{1,0:T(8,128)(2,1)S(1)} %get-tuple-element.50), channel_id=1, source_target_pairs={{0,2},{1,3},{2,0},{3,1},{4,6},{5,7},{6,4},{7,5},{8,10},{9,11},{10,... | collective-permute-start | bytes 442376 | tf_op jit(solution)/shard_map/ppermute | solution.py:394
  36.0 0.2 collective-permute-start.9
  36.2 0.0 copy-done.6
  36.2 1.7 %collective-permute-done.10.refs_3_ = bf16[16,4608]{1,0:T(8,128)(2,1)S(1)} collective-permute-done((bf16[16,4608]{1,0:T(8,128)(2,1)S(1)}, bf16[16,4608]{1,0:T(8,128)(2,1)S(1)}, u32[]{:S(2)}, u32[]{:S(2)}) %collective-permute-start.10) | collective-permute-done | bytes 147488 | tf_op jit(solution)/shard_map/ppermute | solution.py:394
  37.9 7.9 %collective-permute-done.8.refs_1_ = bf16[16,4608]{1,0:T(8,128)(2,1)S(1)} collective-permute-done((bf16[16,4608]{1,0:T(8,128)(2,1)S(1)}, bf16[16,4608]{1,0:T(8,128)(2,1)S(1)}, u32[]{:S(2)}, u32[]{:S(2)}) %collective-permute-start.8) | collective-permute-done | bytes 147488 | tf_op jit(solution)/shard_map/ppermute | solution.py:394
  45.7 0.0 collective-permute-done.9.refs_2_
  45.7 0.0 copy-done.1
  45.8 0.9 %finish.1 = bf16[16,4608]{1,0:T(8,128)(2,1)} custom-call(f32[16,4608]{1,0:T(8,128)S(1)} %get-tuple-element.49.refs_0_, bf16[16,4608]{1,0:T(8,128)(2,1)S(1)} %collective-permute-done.8.refs_1_, bf16[16,4608]{1,0:T(8,128)(2,1)S(1)} %collective-permute-done.9.refs_2_, bf16[16,4608]{1,0:T(8,128)(2,1)S(1)} %collective-permute-done.10.refs_3_, ...), custom_call_target="tpu_custom_call" | custom-call | tf_op jit(solution)/shard_map/finish/pallas_call | solution.py:332
  (1 shorter events, 0.0 us)
Async XLA Ops:
  0.0 2.3 %copy-start = (bf16[64,8,128]{2,1,0:T(8,128)(2,1)S(1)}, bf16[64,8,128]{2,1,0:T(8,128)(2,1)}, u32[]{:S(2)}) copy-start(bf16[64,8,128]{2,1,0:T(8,128)(2,1)} %param.10) | copy-start | bytes 393220
  0.0 6.7 %copy-start.4 = (s32[64,1]{0,1:T(1,128)S(1)}, s32[64,1]{0,1:T(1,128)}, u32[]{:S(2)}) copy-start(s32[64,1]{0,1:T(1,128)} %param.15) | copy-start | bytes 772
  0.0 6.8 %copy-start.3 = (s32[64]{0:T(128)S(1)}, s32[64]{0:T(128)}, u32[]{:S(2)}) copy-start(s32[64]{0:T(128)} %param.13) | copy-start | bytes 772
  0.0 6.8 %copy-start.2 = (s32[512]{0:T(512)S(1)}, s32[512]{0:T(512)}, u32[]{:S(2)}) copy-start(s32[512]{0:T(512)} %param.14) | copy-start | bytes 6148
  1.6 5.2 %collective-permute-start = (bf16[8,4,128,128]{3,2,1,0:T(8,128)(2,1)S(1)}, bf16[8,4,128,128]{3,2,1,0:T(8,128)(2,1)S(1)}, u32[]{:S(2)}, u32[]{:S(2)}) collective-permute-start(bf16[8,4,128,128]{3,2,1,0:T(8,128)(2,1)S(1)} %get-tuple-element.31.refs_3_.refs_4_), channel_id=1, source_target_pairs={{0,4},{4,0},{8,12},{12,8},{16,20},{20,16},{24,28},{28,24},{1,5},{5... | collective-permute-start | bytes 3145736 | tf_op jit(solution)/shard_map/ppermute | solution.py:355
  2.2 4.6 %collective-permute-start.1 = (bf16[8,4,128,128]{3,2,1,0:T(8,128)(2,1)S(1)}, bf16[8,4,128,128]{3,2,1,0:T(8,128)(2,1)S(1)}, u32[]{:S(2)}, u32[]{:S(2)}) collective-permute-start(bf16[8,4,128,128]{3,2,1,0:T(8,128)(2,1)S(1)} %get-tuple-element.32.refs_4_.refs_5_), channel_id=1, source_target_pairs={{0,4},{4,0},{8,12},{12,8},{16,20},{20,16},{24,28},{28,24},{1,5},{5... | collective-permute-start | bytes 3145736 | tf_op jit(solution)/shard_map/ppermute | solution.py:355
  2.3 9.2 %collective-permute-start.2 = (bf16[64,8,128]{2,1,0:T(8,128)(2,1)S(1)}, bf16[64,8,128]{2,1,0:T(8,128)(2,1)S(1)}, u32[]{:S(2)}, u32[]{:S(2)}) collective-permute-start(bf16[64,8,128]{2,1,0:T(8,128)(2,1)S(1)} %copy-done), channel_id=1, source_target_pairs={{0,8},{4,12},{8,0},{12,4},{16,24},{20,28},{24,16},{28,20},{1,9},{5... | collective-permute-start | bytes 393224 | tf_op jit(solution)/shard_map/ppermute | solution.py:361
  5.2 8.0 %collective-permute-start.3 = (bf16[64,8,128]{2,1,0:T(8,128)(2,1)S(1)}, bf16[64,8,128]{2,1,0:T(8,128)(2,1)S(1)}, u32[]{:S(2)}, u32[]{:S(2)}) collective-permute-start(bf16[64,8,128]{2,1,0:T(8,128)(2,1)S(1)} %copy-done), channel_id=1, source_target_pairs={{0,16},{4,20},{8,24},{12,28},{16,0},{20,4},{24,8},{28,12},{1,17},{... | collective-permute-start | bytes 393224 | tf_op jit(solution)/shard_map/ppermute | solution.py:361
  6.7 10.3 %collective-permute-start.6 = (bf16[64,8,128]{2,1,0:T(8,128)(2,1)S(1)}, bf16[64,8,128]{2,1,0:T(8,128)(2,1)S(1)}, u32[]{:S(2)}, u32[]{:S(2)}) collective-permute-start(bf16[64,8,128]{2,1,0:T(8,128)(2,1)S(1)} %copy-done), channel_id=1, source_target_pairs={{0,24},{4,28},{8,16},{12,20},{16,8},{20,12},{24,0},{28,4},{1,25},{... | collective-permute-start | bytes 393224 | tf_op jit(solution)/shard_map/ppermute | solution.py:361
  17.0 6.7 %copy-start.5 = (s32[64]{0:T(128)S(1)}, s32[64]{0:T(128)}, u32[]{:S(2)}) copy-start(s32[64]{0:T(128)} %lengths_ref.1) | copy-start | bytes 772
  20.1 9.6 %collective-permute-start.7 = (bf16[9,64,128]{2,1,0:T(8,128)(2,1)S(1)}, bf16[9,64,128]{2,1,0:T(8,128)(2,1)S(1)}, u32[]{:S(2)}, u32[]{:S(2)}) collective-permute-start(bf16[9,64,128]{2,1,0:T(8,128)(2,1)S(1)} %get-tuple-element.41), channel_id=1, source_target_pairs={{24,0},{28,4},{16,8},{20,12},{8,16},{12,20},{0,24},{4,28},{25,1},{... | collective-permute-start | bytes 442376 | tf_op jit(solution)/shard_map/ppermute | solution.py:384
  21.7 8.0 %collective-permute-start.4 = (bf16[9,64,128]{2,1,0:T(8,128)(2,1)S(1)}, bf16[9,64,128]{2,1,0:T(8,128)(2,1)S(1)}, u32[]{:S(2)}, u32[]{:S(2)}) collective-permute-start(bf16[9,64,128]{2,1,0:T(8,128)(2,1)S(1)} %get-tuple-element.38), channel_id=1, source_target_pairs={{8,0},{12,4},{0,8},{4,12},{24,16},{28,20},{16,24},{20,28},{9,1},{1... | collective-permute-start | bytes 442376 | tf_op jit(solution)/shard_map/ppermute | solution.py:384
  23.2 6.6 %collective-permute-start.5 = (bf16[9,64,128]{2,1,0:T(8,128)(2,1)S(1)}, bf16[9,64,128]{2,1,0:T(8,128)(2,1)S(1)}, u32[]{:S(2)}, u32[]{:S(2)}) collective-permute-start(bf16[9,64,128]{2,1,0:T(8,128)(2,1)S(1)} %get-tuple-element.39), channel_id=1, source_target_pairs={{16,0},{20,4},{24,8},{28,12},{0,16},{4,20},{8,24},{12,28},{17,1},{... | collective-permute-start | bytes 442376 | tf_op jit(solution)/shard_map/ppermute | solution.py:384
  29.7 6.5 %copy-start.6 = (f32[4608]{0:T(1024)S(1)}, f32[4608]{0:T(1024)}, u32[]{:S(2)}) copy-start(f32[4608]{0:T(1024)} %param.19) | copy-start | bytes 55300
  29.7 16.1 %copy-start.1 = (bf16[16,4608]{1,0:T(8,128)(2,1)S(1)}, bf16[16,4608]{1,0:T(8,128)(2,1)}, u32[]{:S(2)}) copy-start(bf16[16,4608]{1,0:T(8,128)(2,1)} %refs_4_.1) | copy-start | bytes 442372
  31.7 6.1 %collective-permute-start.10 = (bf16[16,4608]{1,0:T(8,128)(2,1)S(1)}, bf16[16,4608]{1,0:T(8,128)(2,1)S(1)}, u32[]{:S(2)}, u32[]{:S(2)}) collective-permute-start(bf16[16,4608]{1,0:T(8,128)(2,1)S(1)} %get-tuple-element.52), channel_id=1, source_target_pairs={{0,1},{1,0},{2,3},{3,2},{4,5},{5,4},{6,7},{7,6},{8,9},{9,8},{10,11... | collective-permute-start | bytes 442376 | tf_op jit(solution)/shard_map/ppermute | solution.py:394
  33.4 12.4 %collective-permute-start.8 = (bf16[16,4608]{1,0:T(8,128)(2,1)S(1)}, bf16[16,4608]{1,0:T(8,128)(2,1)S(1)}, u32[]{:S(2)}, u32[]{:S(2)}) collective-permute-start(bf16[16,4608]{1,0:T(8,128)(2,1)S(1)} %get-tuple-element.50), channel_id=1, source_target_pairs={{0,2},{1,3},{2,0},{3,1},{4,6},{5,7},{6,4},{7,5},{8,10},{9,11},{10,... | collective-permute-start | bytes 442376 | tf_op jit(solution)/shard_map/ppermute | solution.py:394
  36.0 9.8 %collective-permute-start.9 = (bf16[16,4608]{1,0:T(8,128)(2,1)S(1)}, bf16[16,4608]{1,0:T(8,128)(2,1)S(1)}, u32[]{:S(2)}, u32[]{:S(2)}) collective-permute-start(bf16[16,4608]{1,0:T(8,128)(2,1)S(1)} %get-tuple-element.51), channel_id=1, source_target_pairs={{0,3},{1,2},{2,1},{3,0},{4,7},{5,6},{6,5},{7,4},{8,11},{9,10},{10,... | collective-permute-start | bytes 442376 | tf_op jit(solution)/shard_map/ppermute | solution.py:394

commit v4 on v3

v4 whole, which is shorter than its diff:
```python
import functools
import math

import jax
import jax.numpy as jnp
from jax import lax
from jax.experimental import pallas as pl
from jax.experimental.pallas import tpu as pltpu
from jax.sharding import PartitionSpec as P


HOT_CAP = 8
score_scale = 1.0 / 12.0
soft_cap = 50.0
epsilon = 1e-06
inner = score_scale / soft_cap
outer = soft_cap * math.log2(math.e)
MIB = 1 << 20


def weights_of(logits):
    return jnp.exp2(outer * jnp.tanh(logits * inner))


def dot_t(a, b):
    return lax.dot_general(a, b, (((1,), (1,)), ((), ())), preferred_element_type=jnp.float32)


def dot_n(a, b):
    return lax.dot_general(a, b, (((1,), (0,)), ((), ())), preferred_element_type=jnp.float32)


def lead_kernel(keys_ref, values_ref, k_out, v_out, sems):
    copies = [
        pltpu.make_async_copy(src.at[pl.ds(0, dst.shape[0])], dst, sems.at[i])
        for i, (src, dst) in enumerate(((keys_ref, k_out), (values_ref, v_out)))
    ]
    for copy in copies:
        copy.start()
    for copy in copies:
        copy.wait()


def in_hbm(x):
    return pltpu.with_memory_space_constraint(x, pltpu.HBM)


HBM = pl.BlockSpec(memory_space=pltpu.HBM)
VMEM = pl.BlockSpec(memory_space=pltpu.VMEM)
SMEM = pl.BlockSpec(memory_space=pltpu.SMEM)


def lead_pages(keys, values):
    out = jax.ShapeDtypeStruct((HOT_CAP, *keys.shape[1:]), keys.dtype)
    return pl.pallas_call(
        lead_kernel,
        out_shape=(out, out),
        in_specs=[HBM, HBM],
        out_specs=(VMEM, VMEM),
        scratch_shapes=[pltpu.SemaphoreType.DMA((2,))],
        compiler_params=pltpu.CompilerParams(vmem_limit_bytes=4 * MIB),
        name="lead_pages",
    )(in_hbm(keys), in_hbm(values))


def own_kernel(
    seqs, ups, heads, group, kv_heads,
    pages_ref, lengths_ref, q_ref, first_k, last_k, first_v, v_hbm, w_hbm,
    num_ref, tot_ref, w_ref, last_v, sem, tail_sem,
):
    page_len, head_dim = first_v.shape[2:]
    early, late = first_k.shape[0], last_k.shape[0]

    def tail(act):
        def one(i, carry):
            act(pltpu.make_async_copy(v_hbm.at[pages_ref[early + i]], last_v.at[i], tail_sem.at[i]))
            return carry

        lax.fori_loop(0, late, one, 0)

    tail(lambda copy: copy.start())
    width = kv_heads * page_len
    prefetch = pltpu.make_async_copy(w_hbm, w_ref, sem)
    prefetch.start()
    column = lax.broadcasted_iota(jnp.int32, (heads, width), 1)
    row = lax.broadcasted_iota(jnp.int32, (heads, width), 0)
    mine = (column // page_len) == (row // group)
    token = jnp.where(mine, column % page_len, ups * page_len)
    ones = jnp.ones((width, head_dim), jnp.bfloat16)
    done = 0
    for kbuf, vbuf in ((first_k, first_v), (last_k, last_v)):
        if kbuf is last_k:
            tail(lambda copy: copy.wait())
        part = kbuf.shape[0] // ups
        unroll = math.gcd(part, 16)

        def block(b, carry, first=done, unroll=unroll, kbuf=kbuf, vbuf=vbuf):
            for j in range(unroll):
                at = b * unroll + j
                s = first + at
                q = q_ref[pl.ds(pl.multiple_of(s * heads, heads), heads), :]
                total = jnp.zeros((heads, 2 * head_dim), jnp.float32)
                for u in range(ups):
                    k = kbuf[at * ups + u].reshape(width, head_dim)
                    v = vbuf[at * ups + u].reshape(width, head_dim)
                    allowed = token < lengths_ref[s] - u * page_len
                    weight = jnp.where(allowed, weights_of(dot_t(q, k)), 0.0).astype(jnp.bfloat16)
                    total = total + dot_n(weight, jnp.concatenate([v, ones], axis=1))
                num_ref[pl.ds(s, heads, stride=seqs), :] = total[:, :head_dim]
                tot_ref[pl.ds(s, heads, stride=seqs), :] = total[:, head_dim:]
            return carry

        lax.fori_loop(0, part // unroll, block, 0)
        done += part
    prefetch.wait()


def own_terms(q, pages, own_k, first_v, values, lengths, o_weight):
    seqs, _, head_dim = q.shape
    _, kv_heads, page_len, _ = first_v.shape
    count, late = pages.shape[0], own_k[1].shape[0]
    group = q.shape[1] // kv_heads
    heads = -(-q.shape[1] // 8) * 8
    q = jnp.pad(q, ((0, 0), (0, heads - q.shape[1]), (0, 0))).reshape(seqs * heads, head_dim)
    out = jax.ShapeDtypeStruct((heads * seqs, head_dim), jnp.float32)
    num, tot, w = pl.pallas_call(
        functools.partial(own_kernel, seqs, count // seqs, heads, group, kv_heads),
        out_shape=(out, out, jax.ShapeDtypeStruct(o_weight.shape, o_weight.dtype)),
        in_specs=[SMEM, SMEM] + [VMEM] * 4 + [HBM, HBM],
        out_specs=(VMEM, VMEM, VMEM),
        scratch_shapes=[
            pltpu.VMEM((late, kv_heads, page_len, head_dim), values.dtype),
            pltpu.SemaphoreType.DMA,
            pltpu.SemaphoreType.DMA((late,)),
        ],
        compiler_params=pltpu.CompilerParams(vmem_limit_bytes=8 * MIB),
        name="own_pages",
    )(pages, lengths, q, *own_k, first_v, in_hbm(values), in_hbm(o_weight))
    return (num, tot), w


def shared_places(me, cap, page_count, hot_ref, lanes):
    shape = (2 * cap, hot_ref.shape[1])
    slot = lax.broadcasted_iota(jnp.int32, shape, 0)
    lane = lax.broadcasted_iota(jnp.int32, shape, 1).astype(jnp.float32)
    first = jnp.where(slot < cap, me * page_count, (me ^ 1) * page_count - cap)
    matches = jnp.broadcast_to(hot_ref[...], shape) == first + slot
    place = jnp.min(jnp.where(matches, lane, 1e9), axis=1, keepdims=True)
    return jnp.broadcast_to(place, (2 * cap, lanes))


def used_column(origin, seqs, used_ref, lanes):
    span = used_ref.shape[1]
    row = used_ref[pl.ds(origin * seqs // span, 1), :].astype(jnp.float32)
    shape = (seqs, span)
    lane = lax.broadcasted_iota(jnp.int32, shape, 1)
    sequence = lax.broadcasted_iota(jnp.int32, shape, 0) + origin * seqs % span
    picked = jnp.where(lane == sequence, jnp.broadcast_to(row, shape), 0.0)
    return jnp.broadcast_to(jnp.sum(picked, axis=1, keepdims=True), (seqs, lanes))


def hot_kernel(sources, halves, seqs, heads, kv_heads, fetches, page_count, hot_ref, used_ref, *refs):
    pages_ref, *refs = refs
    jobs = len(fetches)
    caches, refs = refs[:jobs], refs[jobs:]
    refs, fetched, (staged, places), sems = (
        refs[: -2 * jobs - 2], refs[-2 * jobs - 2 : -jobs - 2], refs[-jobs - 2 : -jobs], refs[-jobs:]
    )

    def each(act):
        for n, (first, last) in enumerate(fetches):

            def one(i, carry, n=n, first=first):
                src = caches[n].at[pages_ref[first + i]]
                act(pltpu.make_async_copy(src, fetched[n].at[i], sems[n].at[i]))
                return carry

            lax.fori_loop(0, last - first, one, 0)

    each(lambda copy: copy.start())
    count = len(sources)
    queries, refs = refs[:count], refs[count:]
    kv = [(refs[2 * i], refs[2 * i + 1]) for i in range(len(halves))]
    outs = list(refs[2 * len(halves) :])
    group = heads // kv_heads
    cap, _, page_len, head_dim = kv[0][0].shape
    lane = lax.broadcasted_iota(jnp.int32, (8, head_dim), 1)
    for r in range(count):
        staged[r] = queries[r][...].astype(jnp.float32)
    me = lax.axis_index("pages")
    places[...] = shared_places(me, cap, page_count, hot_ref, head_dim)
    used_rows = [used_column(shift(me), seqs, used_ref, head_dim) for shift, _, _ in sources]
    step = 2
    ones = jnp.ones((step * page_len, head_dim), jnp.bfloat16)
    dests = []
    for _, _, packed in sources:
        dests.append(outs.pop(0) if packed else (outs.pop(0), outs.pop(0)))
    totals = [jnp.zeros((8, head_dim), jnp.float32) for _ in range(count)]
    for h in range(kv_heads):
        rows = [
            [
                staged[r, pl.ds(h * group + g, seqs, stride=heads), :].astype(jnp.bfloat16)
                for g in range(group)
            ]
            for r in range(count)
        ]
        acc = [jnp.zeros((group * seqs, 2 * head_dim), jnp.float32) for _ in range(count)]
        for half, (k_ref, v_ref) in zip(halves, kv):
            active = [r for r in range(count) if half in sources[r][1]]
            q = jnp.concatenate([row for r in active for row in rows[r]], axis=0)
            for c in range(0, cap, step):
                k = k_ref[c : c + step, h].reshape(step * page_len, head_dim)
                v = v_ref[c : c + step, h].reshape(step * page_len, head_dim)
                weight = weights_of(dot_t(q, k))
                parts = []
                for p in range(step):
                    slot = half * cap + c + p
                    place = jnp.broadcast_to(places[slot : slot + 1, :], (seqs, page_len))
                    columns = slice(p * page_len, (p + 1) * page_len)
                    part = []
                    for n, r in enumerate(active):
                        mask = used_rows[r] > place
                        for i in range(n * group, (n + 1) * group):
                            part.append(jnp.where(mask, weight[i * seqs : (i + 1) * seqs, columns], 0.0))
                    parts.append(jnp.concatenate(part, axis=0).astype(jnp.bfloat16))
                res = dot_n(jnp.concatenate(parts, axis=1), jnp.concatenate([v, ones], axis=1))
                for n, r in enumerate(active):
                    acc[r] = acc[r] + res[n * group * seqs : (n + 1) * group * seqs]
        for r, (_, _, packed) in enumerate(sources):
            for g in range(group):
                head = h * group + g
                num = acc[r][g * seqs : (g + 1) * seqs, :head_dim]
                tot = acc[r][g * seqs : (g + 1) * seqs, head_dim:]
                if packed:
                    rest = tot - tot.astype(jnp.bfloat16).astype(jnp.float32)
                    dests[r][head * seqs : (head + 1) * seqs, :] = num.astype(jnp.bfloat16)
                    for j in range(seqs // 8):
                        at, fold = 2 * heads * j + head, slice(8 * j, 8 * j + 8)
                        low = jnp.where(lane == at + heads, rest[fold], totals[r])
                        totals[r] = jnp.where(lane == at, tot[fold], low)
                else:
                    dests[r][0][head * seqs : (head + 1) * seqs, :] = num
                    dests[r][1][head * seqs : (head + 1) * seqs, :] = tot
    for r, (_, _, packed) in enumerate(sources):
        if packed:
            padded = jnp.concatenate([totals[r], jnp.zeros_like(totals[r])], axis=0)
            dests[r][heads * seqs :, :] = padded.astype(jnp.bfloat16)
    each(lambda copy: copy.wait())


def hot_terms(queries, sources, halves, kv, page_count, tables, pages, fetch):
    _, kv_heads, page_len, head_dim = kv[0].shape
    seqs, heads = queries[0].shape[:2]
    shapes = []
    for _, _, packed in sources:
        if packed:
            shapes.append(((heads * seqs + 16, head_dim), jnp.bfloat16))
        else:
            shapes += [((heads * seqs, head_dim), jnp.float32)] * 2
    counts = [last - first for _, first, last in fetch]
    shapes += [((n, kv_heads, page_len, head_dim), kv[0].dtype) for n in counts]
    fetches = tuple((first, last) for _, first, last in fetch)
    flat = [q.reshape(seqs * heads, head_dim) for q in queries]
    operands = [*tables, pages, *(in_hbm(f[0]) for f in fetch), *flat, *kv]
    return pl.pallas_call(
        functools.partial(
            hot_kernel, sources, halves, seqs, heads, kv_heads, fetches, page_count
        ),
        out_shape=[jax.ShapeDtypeStruct(*s) for s in shapes],
        in_specs=[VMEM, VMEM, SMEM] + [HBM] * len(fetch) + [VMEM] * (len(flat) + len(kv)),
        out_specs=[VMEM] * len(shapes),
        scratch_shapes=[
            pltpu.VMEM((len(sources), seqs * heads, head_dim), jnp.float32),
            pltpu.VMEM((2 * HOT_CAP, head_dim), jnp.float32),
            *(pltpu.SemaphoreType.DMA((n,)) for n in counts),
        ],
        compiler_params=pltpu.CompilerParams(vmem_limit_bytes=12 * MIB),
        name="hot_pages",
    )(*operands)


def row_owner(i, k, ways):
    return i ^ k if ways & (ways - 1) == 0 else lax.rem(i + k, ways)


def row_order(ways):
    return [2, 1, 3] if ways == 4 else list(range(ways - 1, 0, -1))


def project_kernel(received, seqs, heads, ways, *refs):
    blocks = refs[:received]
    nums, tots = refs[received : received + 3], refs[received + 3 : received + 6]
    w_ref, outs, spread = refs[received + 6], refs[received + 7 : received + 7 + ways], refs[-1]
    head_dim = nums[0].shape[1]
    rows = seqs // ways
    far = jnp.zeros((16, head_dim), jnp.float32)
    for b in blocks:
        far = far + b[heads * seqs :, :].astype(jnp.float32)
    for h in range(heads):
        part = pl.ds(h * seqs, seqs)
        num = nums[0][part, :] + nums[1][part, :] + nums[2][part, :]
        tot = tots[0][part, :] + tots[1][part, :] + tots[2][part, :]
        for b in blocks:
            num = num + b[part, :].astype(jnp.float32)
        if blocks:
            folds = []
            for at in range(h, 2 * heads * (seqs // 8), 2 * heads):
                fold = far[:8, at : at + 1] + far[:8, at + heads : at + heads + 1]
                folds.append(jnp.broadcast_to(fold, (8, head_dim)))
            tot = tot + jnp.concatenate(folds, axis=0)
        spread[:, h * head_dim : (h + 1) * head_dim] = num / tot
    turned = []
    for k in range(ways):
        target = row_owner(lax.axis_index("heads"), k, ways)
        turned.append(spread[pl.ds(pl.multiple_of(target * rows, rows), rows), :])
    att = jnp.concatenate(turned, axis=0).astype(jnp.bfloat16)
    model = w_ref.shape[1]
    tile = math.gcd(model, 768)
    for n in range(0, model, tile):
        res = dot_n(att, w_ref[:, n : n + tile])
        for k in range(ways):
            outs[k][:, n : n + tile] = res[k * rows : (k + 1) * rows].astype(outs[k].dtype)


def project(blocks, near, rest, own, o_weight, ways):
    head_dim = own[0].shape[1]
    width, model = o_weight.shape
    heads = width // head_dim
    seqs = near[0].shape[0] // heads
    rows = seqs // ways
    kinds = [jnp.float32] + [jnp.bfloat16] * (ways - 1)
    return pl.pallas_call(
        functools.partial(project_kernel, len(blocks), seqs, heads, ways),
        out_shape=[jax.ShapeDtypeStruct((rows, model), kind) for kind in kinds],
        in_specs=[VMEM] * (len(blocks) + 7),
        out_specs=[VMEM] * ways,
        scratch_shapes=[pltpu.VMEM((seqs, width), jnp.float32)],
        compiler_params=pltpu.CompilerParams(vmem_limit_bytes=8 * MIB),
        name="project",
    )(*blocks, near[0], rest[0], own[0], near[1], rest[1], own[1], o_weight)


def norm_kernel(*refs):
    parts, (residual, gain, out) = refs[:-3], refs[-3:]
    projected = parts[0][...]
    for p in parts[1:]:
        projected = projected + p[...].astype(jnp.float32)
    mean_sq = jnp.mean(projected * projected, axis=1, keepdims=True)
    normed = projected / jnp.sqrt(mean_sq + epsilon) * gain[...]
    out[...] = (residual[...].astype(jnp.float32) + normed).astype(jnp.bfloat16)


def finish(parts, residual, norm_gain):
    return pl.pallas_call(
        norm_kernel,
        out_shape=jax.ShapeDtypeStruct(residual.shape, residual.dtype),
        compiler_params=pltpu.CompilerParams(vmem_limit_bytes=8 * MIB),
        name="finish",
    )(*parts, residual, norm_gain.reshape(1, -1))


def layer(
    chips, ways, queries, keys, values, hot_pages, hot_used, user_pages, lengths, o_weight, residual, norm_gain
):
    page_count = keys.shape[0]
    devices = 2 * chips
    swap = [(i, i ^ 1) for i in range(devices)]
    power = chips & (chips - 1) == 0

    def there(i, k):
        return i ^ (2 * k) if power else (i + 2 * k) % devices

    pages = user_pages.reshape(-1)
    out_perm = [[(i, there(i, k)) for i in range(devices)] for k in range(chips)]
    back_perm = [[(j, i) for i, j in perm] for perm in out_perm]
    far_q = []
    for k in range(1, chips):
        far_q.append(lax.ppermute(queries, "pages", out_perm[k]))
    own_kv = lead_pages(keys, values)
    partner_kv = tuple(lax.ppermute(x, "pages", swap) for x in own_kv)

    def shift(k):
        if power:
            return lambda i: i ^ (2 * k)
        return lambda i: lax.rem(i + devices - 2 * k, devices)

    tables = (hot_pages.reshape(1, -1), hot_used.reshape(-1, 128))
    count = pages.shape[0]
    early = count // 4 * 3 // user_pages.shape[1] * user_pages.shape[1]
    *near, first_k = hot_terms(
        [queries], [(shift(0), (0,), False)], (0,), own_kv, page_count, tables, pages,
        [(keys, 0, early)],
    )
    near, far_q, partner_kv = lax.optimization_barrier((near, far_q, partner_kv))
    sources = [(shift(k), (0, 1), True) for k in range(1, chips)] + [(shift(0), (1,), False)]
    *sent, rest_num, rest_tot, last_k, first_v = hot_terms(
        [*far_q, queries], sources, (0, 1), (*own_kv, *partner_kv), page_count, tables, pages,
        [(keys, early, count), (values, 0, early)],
    )
    blocks = []
    for k, b in zip(range(1, chips), sent):
        blocks.append(lax.ppermute(b, "pages", back_perm[k]))
    queries, rest_num = lax.optimization_barrier((queries, rest_num))
    own, weight = own_terms(queries, pages, (first_k, last_k), first_v, values, lengths, o_weight)
    parts = project(blocks, near, (rest_num, rest_tot), own, weight, ways)
    arrived = [parts[0]]
    for k in row_order(ways):
        pairs = [(i, i ^ k if ways & (ways - 1) == 0 else (i + k) % ways) for i in range(ways)]
        arrived.append(lax.ppermute(parts[k], "heads", pairs))
    return finish(arrived, residual, norm_gain)


def solution(mesh):
    in_specs = (
        P("pages", "heads", None),
        P("pages", "heads", None, None),
        P("pages", "heads", None, None),
        P(),
        P(),
        P("pages", None),
        P("pages"),
        P("heads", None),
        P(("pages", "heads"), None),
        P(),
    )
    out_specs = P(("pages", "heads"), None)
    chips = mesh.shape["pages"] // 2
    body = functools.partial(layer, chips, mesh.shape["heads"])
    return jax.shard_map(body, mesh=mesh, in_specs=in_specs, out_specs=out_specs, check_vma=False)
```

time: 47 us -> 45.1 us (0.960)
  Pallas kernels: 22 us -> 20.8 us
  waiting for transfers between devices: 11.3 us -> 10.5 us
    ppermute x3, waiting for transfers between devices: 9.55 us -> 7.96 us  [layer(): arrived.append(lax.ppermute(parts[k], 'heads', pairs))]
    pallas_call x3 -> x2, Pallas kernels: 11.5 us -> 9.97 us  [hot_terms(): pl.pallas_call(functools.partial(hot_kernel, sources, halves, seqs, heads...]
    ppermute x3, waiting for transfers between devices: 1.74 us -> 2.58 us  [layer(): far_q.append(lax.ppermute(queries, 'pages', out_perm[k]))]
  transfers between devices with their start and end apart: 11 -> 11, of which waited for: 3 -> 2; matrix products, arithmetic and copies ran while one was open for 0% -> 0% of each run, Pallas kernels for 31% -> 23%
where the time goes in v4:
time: 45.1 us; the launch traced here: 44.6 us
  Pallas kernels  20.8 us (46%)
  starting transfers between devices  13.1 us (29%)
  waiting for transfers between devices  10.5 us (23%)
    pallas_call x2, Pallas kernels, hot_terms(): pl.pallas_call(functools.partial(hot_kernel, sources, halves, seqs, heads...  9.97 us
    ppermute x3, waiting for transfers between devices, layer(): arrived.append(lax.ppermute(parts[k], 'heads', pairs))  7.96 us
    pallas_call x1, Pallas kernels, own_terms(): pl.pallas_call(functools.partial(own_kernel, seqs, count // seqs, heads,...  6.32 us
    ppermute x3, starting transfers between devices, layer(): arrived.append(lax.ppermute(parts[k], 'heads', pairs))  4.45 us
    ppermute x3, starting transfers between devices, layer(): far_q.append(lax.ppermute(queries, 'pages', out_perm[k]))  4.43 us
    ppermute x3, starting transfers between devices, layer(): blocks.append(lax.ppermute(b, 'pages', back_perm[k]))  3.55 us
    ppermute x3, waiting for transfers between devices, layer(): far_q.append(lax.ppermute(queries, 'pages', out_perm[k]))  2.58 us
    pallas_call x1, Pallas kernels, project(): pl.pallas_call(functools.partial(project_kernel, len(blocks), seqs, heads...  2.02 us
  transfers between devices with their start and end apart: 11, of which 2 were waited for; matrix products, arithmetic and copies ran while one was open for 0% of the time, Pallas kernels for 23%

profile of v4, /device:TPU:0, one launch (start us, length us, event | category | flops | bytes accessed | tf_op | source)
XLA Modules:
  0.0 44.6 jit_solution(142511215514420231)
XLA Ops:
  0.0 0.0 copy-start
  0.0 0.0 copy-start.4
  0.0 0.0 copy-start.2
  0.0 0.0 copy-start.3
  0.0 1.6 %lead_pages.1 = (bf16[8,4,128,128]{3,2,1,0:T(8,128)(2,1)S(1)}, bf16[8,4,128,128]{3,2,1,0:T(8,128)(2,1)S(1)}) custom-call(bf16[72,4,128,128]{3,2,1,0:T(8,128)(2,1)} %refs_1_.3, bf16[72,4,128,128]{3,2,1,0:T(8,128)(2,1)} %v_hbm.1), custom_call_target="tpu_custom_call" | custom-call | tf_op jit(solution)/shard_map/lead_pages/pallas_call | solution.py:55
  1.6 0.6 %collective-permute-start.3 = (bf16[8,4,128,128]{3,2,1,0:T(8,128)(2,1)S(1)}, bf16[8,4,128,128]{3,2,1,0:T(8,128)(2,1)S(1)}, u32[]{:S(2)}, u32[]{:S(2)}) collective-permute-start(bf16[8,4,128,128]{3,2,1,0:T(8,128)(2,1)S(1)} %get-tuple-element.33.refs_3_.refs_7_), channel_id=1, source_target_pairs={{0,4},{4,0},{8,12},{12,8},{16,20},{20,16},{24,28},{28,24},{1,5},{5... | collective-permute-start | bytes 3145736 | tf_op jit(solution)/shard_map/ppermute | solution.py:380
  2.2 0.1 collective-permute-start.4
  2.3 0.0 copy-done
  2.3 2.9 %collective-permute-start = (bf16[64,8,128]{2,1,0:T(8,128)(2,1)S(1)}, bf16[64,8,128]{2,1,0:T(8,128)(2,1)S(1)}, u32[]{:S(2)}, u32[]{:S(2)}) collective-permute-start(bf16[64,8,128]{2,1,0:T(8,128)(2,1)S(1)} %copy-done), channel_id=1, source_target_pairs={{0,8},{4,12},{8,0},{12,4},{16,24},{20,28},{24,16},{28,20},{1,9},{5... | collective-permute-start | bytes 393224 | tf_op jit(solution)/shard_map/ppermute | solution.py:378
  5.2 1.5 %collective-permute-start.1 = (bf16[64,8,128]{2,1,0:T(8,128)(2,1)S(1)}, bf16[64,8,128]{2,1,0:T(8,128)(2,1)S(1)}, u32[]{:S(2)}, u32[]{:S(2)}) collective-permute-start(bf16[64,8,128]{2,1,0:T(8,128)(2,1)S(1)} %copy-done), channel_id=1, source_target_pairs={{0,16},{4,20},{8,24},{12,28},{16,0},{20,4},{24,8},{28,12},{1,17},{... | collective-permute-start | bytes 393224 | tf_op jit(solution)/shard_map/ppermute | solution.py:378
  6.7 0.0 collective-permute-start.2
  6.7 0.0 copy-done.4
  6.7 0.0 copy-done.2
  6.7 0.0 copy-done.3
  6.7 3.9 %hot_pages.2 = (f32[512,128]{1,0:T(8,128)S(1)}, f32[512,128]{1,0:T(8,128)S(1)}, bf16[48,4,128,128]{3,2,1,0:T(8,128)(2,1)S(1)}) custom-call(s32[1,64]{1,0:T(1,128)S(1)} %bitcast.19, s32[4,128]{1,0:T(4,128)S(1)} %bitcast.14, s32[64]{0:T(128)S(1)} %bitcast.16, bf16[72,4,128,128]{3,2,1,0:T(8,128)(2,1)} %refs_1_.3, bf16[512,128]{1,0:T(8,128)(2,1)S(1)} %bitcast.8, ...), custom_call_target="tpu_custom_call" | custom-call | tf_op jit(solution)/shard_map/hot_pages/pallas_call | solution.py:265
  10.6 0.0 collective-permute-done
  10.6 2.6 %collective-permute-done.1 = bf16[64,8,128]{2,1,0:T(8,128)(2,1)S(1)} collective-permute-done((bf16[64,8,128]{2,1,0:T(8,128)(2,1)S(1)}, bf16[64,8,128]{2,1,0:T(8,128)(2,1)S(1)}, u32[]{:S(2)}, u32[]{:S(2)}) %collective-permute-start.1) | collective-permute-done | bytes 131104 | tf_op jit(solution)/shard_map/ppermute | solution.py:378
  13.2 0.0 collective-permute-done.2
  13.2 0.0 collective-permute-done.3.refs_9_
  13.2 0.0 collective-permute-done.4.refs_10_
  13.2 0.0 copy-start.5
  13.2 6.1 %hot_pages.3 = (bf16[528,128]{1,0:T(8,128)(2,1)S(1)}, bf16[528,128]{1,0:T(8,128)(2,1)S(1)}, bf16[528,128]{1,0:T(8,128)(2,1)S(1)}, f32[512,128]{1,0:T(8,128)S(1)}...) custom-call(s32[1,64]{1,0:T(1,128)S(1)} %bitcast.20, ...), custom_call_target="tpu_custom_call" | custom-call | tf_op jit(solution)/shard_map/hot_pages/pallas_call | solution.py:265
  19.3 1.3 %collective-permute-start.5 = (bf16[528,128]{1,0:T(8,128)(2,1)S(1)}, bf16[528,128]{1,0:T(8,128)(2,1)S(1)}, u32[]{:S(2)}, u32[]{:S(2)}) collective-permute-start(bf16[528,128]{1,0:T(8,128)(2,1)S(1)} %get-tuple-element.42), channel_id=1, source_target_pairs={{8,0},{12,4},{0,8},{4,12},{24,16},{28,20},{16,24},{20,28},{9,1},{1... | collective-permute-start | bytes 405512 | tf_op jit(solution)/shard_map/ppermute | solution.py:402
  20.6 0.8 %collective-permute-start.6 = (bf16[528,128]{1,0:T(8,128)(2,1)S(1)}, bf16[528,128]{1,0:T(8,128)(2,1)S(1)}, u32[]{:S(2)}, u32[]{:S(2)}) collective-permute-start(bf16[528,128]{1,0:T(8,128)(2,1)S(1)} %get-tuple-element.43), channel_id=1, source_target_pairs={{16,0},{20,4},{24,8},{28,12},{0,16},{4,20},{8,24},{12,28},{17,1},{... | collective-permute-start | bytes 405512 | tf_op jit(solution)/shard_map/ppermute | solution.py:402
  21.4 1.4 %collective-permute-start.7 = (bf16[528,128]{1,0:T(8,128)(2,1)S(1)}, bf16[528,128]{1,0:T(8,128)(2,1)S(1)}, u32[]{:S(2)}, u32[]{:S(2)}) collective-permute-start(bf16[528,128]{1,0:T(8,128)(2,1)S(1)} %get-tuple-element.44), channel_id=1, source_target_pairs={{24,0},{28,4},{16,8},{20,12},{8,16},{12,20},{0,24},{4,28},{25,1},{... | collective-permute-start | bytes 405512 | tf_op jit(solution)/shard_map/ppermute | solution.py:402
  22.9 0.0 copy-done.5
  22.9 6.3 %own_pages.1 = (f32[512,128]{1,0:T(8,128)S(1)}, f32[512,128]{1,0:T(8,128)S(1)}, bf16[1024,4608]{1,0:T(8,128)(2,1)S(1)}) custom-call(s32[64]{0:T(128)S(1)} %bitcast.18, s32[64]{0:T(128)S(1)} %copy-done.5, bf16[512,128]{1,0:T(8,128)(2,1)S(1)} %bitcast.10, bf16[48,4,128,128]{3,2,1,0:T(8,128)(2,1)S(1)} %get-tuple-element.49.first_k, ...), custom_call_target="tpu_custom_call" | custom-call | tf_op jit(solution)/shard_map/own_pages/pallas_call | solution.py:126
  29.2 0.0 copy-start.6
  29.2 0.0 copy-start.1
  29.2 0.0 collective-permute-done.5.refs_0_
  29.2 0.0 collective-permute-done.6.refs_1_
  29.2 0.0 collective-permute-done.7.refs_2_
  29.2 2.0 %project.1 = (f32[16,4608]{1,0:T(8,128)S(1)}, bf16[16,4608]{1,0:T(8,128)(2,1)S(1)}, bf16[16,4608]{1,0:T(8,128)(2,1)S(1)}, bf16[16,4608]{1,0:T(8,128)(2,1)S(1)}) custom-call(bf16[528,128]{1,0:T(8,128)(2,1)S(1)} %collective-permute-done.5.refs_0_, bf16[528,128]{1,0:T(8,128)(2,1)S(1)} %collective-permute-done.6.refs_1_, ...), custom_call_target="tpu_custom_call" | custom-call | tf_op jit(solution)/shard_map/project/pallas_call | solution.py:332
  31.3 2.7 %collective-permute-start.8 = (bf16[16,4608]{1,0:T(8,128)(2,1)S(1)}, bf16[16,4608]{1,0:T(8,128)(2,1)S(1)}, u32[]{:S(2)}, u32[]{:S(2)}) collective-permute-start(bf16[16,4608]{1,0:T(8,128)(2,1)S(1)} %get-tuple-element.58), channel_id=1, source_target_pairs={{0,2},{1,3},{2,0},{3,1},{4,6},{5,7},{6,4},{7,5},{8,10},{9,11},{10,... | collective-permute-start | bytes 442376 | tf_op jit(solution)/shard_map/ppermute | solution.py:409
  33.9 1.6 %collective-permute-start.9 = (bf16[16,4608]{1,0:T(8,128)(2,1)S(1)}, bf16[16,4608]{1,0:T(8,128)(2,1)S(1)}, u32[]{:S(2)}, u32[]{:S(2)}) collective-permute-start(bf16[16,4608]{1,0:T(8,128)(2,1)S(1)} %get-tuple-element.59), channel_id=1, source_target_pairs={{0,1},{1,0},{2,3},{3,2},{4,5},{5,4},{6,7},{7,6},{8,9},{9,8},{10,11... | collective-permute-start | bytes 442376 | tf_op jit(solution)/shard_map/ppermute | solution.py:409
  35.5 0.2 collective-permute-start.10
  35.7 0.0 copy-done.6
  35.7 8.0 %collective-permute-done.8.refs_1_ = bf16[16,4608]{1,0:T(8,128)(2,1)S(1)} collective-permute-done((bf16[16,4608]{1,0:T(8,128)(2,1)S(1)}, bf16[16,4608]{1,0:T(8,128)(2,1)S(1)}, u32[]{:S(2)}, u32[]{:S(2)}) %collective-permute-start.8) | collective-permute-done | bytes 147488 | tf_op jit(solution)/shard_map/ppermute | solution.py:409
  43.7 0.0 collective-permute-done.9.refs_2_
  43.7 0.0 collective-permute-done.10.refs_3_
  43.7 0.0 copy-done.1
  43.7 0.9 %finish.1 = bf16[16,4608]{1,0:T(8,128)(2,1)} custom-call(f32[16,4608]{1,0:T(8,128)S(1)} %get-tuple-element.57.refs_0_, bf16[16,4608]{1,0:T(8,128)(2,1)S(1)} %collective-permute-done.8.refs_1_, bf16[16,4608]{1,0:T(8,128)(2,1)S(1)} %collective-permute-done.9.refs_2_, bf16[16,4608]{1,0:T(8,128)(2,1)S(1)} %collective-permute-done.10.refs_3_, ...), custom_call_target="tpu_custom_call" | custom-call | tf_op jit(solution)/shard_map/finish/pallas_call | solution.py:354
  (1 shorter events, 0.0 us)
Async XLA Ops:
  0.0 2.3 %copy-start = (bf16[64,8,128]{2,1,0:T(8,128)(2,1)S(1)}, bf16[64,8,128]{2,1,0:T(8,128)(2,1)}, u32[]{:S(2)}) copy-start(bf16[64,8,128]{2,1,0:T(8,128)(2,1)} %param.10) | copy-start | bytes 393220
  0.0 6.7 %copy-start.4 = (s32[64]{0:T(128)S(1)}, s32[64]{0:T(128)}, u32[]{:S(2)}) copy-start(s32[64]{0:T(128)} %param.13) | copy-start | bytes 772
  0.0 6.7 %copy-start.2 = (s32[512]{0:T(512)S(1)}, s32[512]{0:T(512)}, u32[]{:S(2)}) copy-start(s32[512]{0:T(512)} %param.14) | copy-start | bytes 6148
  0.0 6.7 %copy-start.3 = (s32[64,1]{0,1:T(1,128)S(1)}, s32[64,1]{0,1:T(1,128)}, u32[]{:S(2)}) copy-start(s32[64,1]{0,1:T(1,128)} %param.15) | copy-start | bytes 772
  1.6 11.6 %collective-permute-start.3 = (bf16[8,4,128,128]{3,2,1,0:T(8,128)(2,1)S(1)}, bf16[8,4,128,128]{3,2,1,0:T(8,128)(2,1)S(1)}, u32[]{:S(2)}, u32[]{:S(2)}) collective-permute-start(bf16[8,4,128,128]{3,2,1,0:T(8,128)(2,1)S(1)} %get-tuple-element.33.refs_3_.refs_7_), channel_id=1, source_target_pairs={{0,4},{4,0},{8,12},{12,8},{16,20},{20,16},{24,28},{28,24},{1,5},{5... | collective-permute-start | bytes 3145736 | tf_op jit(solution)/shard_map/ppermute | solution.py:380
  2.2 11.0 %collective-permute-start.4 = (bf16[8,4,128,128]{3,2,1,0:T(8,128)(2,1)S(1)}, bf16[8,4,128,128]{3,2,1,0:T(8,128)(2,1)S(1)}, u32[]{:S(2)}, u32[]{:S(2)}) collective-permute-start(bf16[8,4,128,128]{3,2,1,0:T(8,128)(2,1)S(1)} %get-tuple-element.34.refs_4_.refs_8_), channel_id=1, source_target_pairs={{0,4},{4,0},{8,12},{12,8},{16,20},{20,16},{24,28},{28,24},{1,5},{5... | collective-permute-start | bytes 3145736 | tf_op jit(solution)/shard_map/ppermute | solution.py:380
  2.3 8.3 %collective-permute-start = (bf16[64,8,128]{2,1,0:T(8,128)(2,1)S(1)}, bf16[64,8,128]{2,1,0:T(8,128)(2,1)S(1)}, u32[]{:S(2)}, u32[]{:S(2)}) collective-permute-start(bf16[64,8,128]{2,1,0:T(8,128)(2,1)S(1)} %copy-done), channel_id=1, source_target_pairs={{0,8},{4,12},{8,0},{12,4},{16,24},{20,28},{24,16},{28,20},{1,9},{5... | collective-permute-start | bytes 393224 | tf_op jit(solution)/shard_map/ppermute | solution.py:378
  5.2 8.0 %collective-permute-start.1 = (bf16[64,8,128]{2,1,0:T(8,128)(2,1)S(1)}, bf16[64,8,128]{2,1,0:T(8,128)(2,1)S(1)}, u32[]{:S(2)}, u32[]{:S(2)}) collective-permute-start(bf16[64,8,128]{2,1,0:T(8,128)(2,1)S(1)} %copy-done), channel_id=1, source_target_pairs={{0,16},{4,20},{8,24},{12,28},{16,0},{20,4},{24,8},{28,12},{1,17},{... | collective-permute-start | bytes 393224 | tf_op jit(solution)/shard_map/ppermute | solution.py:378
  6.7 6.5 %collective-permute-start.2 = (bf16[64,8,128]{2,1,0:T(8,128)(2,1)S(1)}, bf16[64,8,128]{2,1,0:T(8,128)(2,1)S(1)}, u32[]{:S(2)}, u32[]{:S(2)}) collective-permute-start(bf16[64,8,128]{2,1,0:T(8,128)(2,1)S(1)} %copy-done), channel_id=1, source_target_pairs={{0,24},{4,28},{8,16},{12,20},{16,8},{20,12},{24,0},{28,4},{1,25},{... | collective-permute-start | bytes 393224 | tf_op jit(solution)/shard_map/ppermute | solution.py:378
  13.2 9.7 %copy-start.5 = (s32[64]{0:T(128)S(1)}, s32[64]{0:T(128)}, u32[]{:S(2)}) copy-start(s32[64]{0:T(128)} %lengths_ref.1) | copy-start | bytes 772
  19.3 9.9 %collective-permute-start.5 = (bf16[528,128]{1,0:T(8,128)(2,1)S(1)}, bf16[528,128]{1,0:T(8,128)(2,1)S(1)}, u32[]{:S(2)}, u32[]{:S(2)}) collective-permute-start(bf16[528,128]{1,0:T(8,128)(2,1)S(1)} %get-tuple-element.42), channel_id=1, source_target_pairs={{8,0},{12,4},{0,8},{4,12},{24,16},{28,20},{16,24},{20,28},{9,1},{1... | collective-permute-start | bytes 405512 | tf_op jit(solution)/shard_map/ppermute | solution.py:402
  20.6 8.6 %collective-permute-start.6 = (bf16[528,128]{1,0:T(8,128)(2,1)S(1)}, bf16[528,128]{1,0:T(8,128)(2,1)S(1)}, u32[]{:S(2)}, u32[]{:S(2)}) collective-permute-start(bf16[528,128]{1,0:T(8,128)(2,1)S(1)} %get-tuple-element.43), channel_id=1, source_target_pairs={{16,0},{20,4},{24,8},{28,12},{0,16},{4,20},{8,24},{12,28},{17,1},{... | collective-permute-start | bytes 405512 | tf_op jit(solution)/shard_map/ppermute | solution.py:402
  21.4 7.8 %collective-permute-start.7 = (bf16[528,128]{1,0:T(8,128)(2,1)S(1)}, bf16[528,128]{1,0:T(8,128)(2,1)S(1)}, u32[]{:S(2)}, u32[]{:S(2)}) collective-permute-start(bf16[528,128]{1,0:T(8,128)(2,1)S(1)} %get-tuple-element.44), channel_id=1, source_target_pairs={{24,0},{28,4},{16,8},{20,12},{8,16},{12,20},{0,24},{4,28},{25,1},{... | collective-permute-start | bytes 405512 | tf_op jit(solution)/shard_map/ppermute | solution.py:402
  29.2 6.5 %copy-start.6 = (f32[4608]{0:T(1024)S(1)}, f32[4608]{0:T(1024)}, u32[]{:S(2)}) copy-start(f32[4608]{0:T(1024)} %param.19) | copy-start | bytes 55300
  29.2 14.5 %copy-start.1 = (bf16[16,4608]{1,0:T(8,128)(2,1)S(1)}, bf16[16,4608]{1,0:T(8,128)(2,1)}, u32[]{:S(2)}) copy-start(bf16[16,4608]{1,0:T(8,128)(2,1)} %refs_4_.1) | copy-start | bytes 442372
  31.3 12.4 %collective-permute-start.8 = (bf16[16,4608]{1,0:T(8,128)(2,1)S(1)}, bf16[16,4608]{1,0:T(8,128)(2,1)S(1)}, u32[]{:S(2)}, u32[]{:S(2)}) collective-permute-start(bf16[16,4608]{1,0:T(8,128)(2,1)S(1)} %get-tuple-element.58), channel_id=1, source_target_pairs={{0,2},{1,3},{2,0},{3,1},{4,6},{5,7},{6,4},{7,5},{8,10},{9,11},{10,... | collective-permute-start | bytes 442376 | tf_op jit(solution)/shard_map/ppermute | solution.py:409
  33.9 9.8 %collective-permute-start.9 = (bf16[16,4608]{1,0:T(8,128)(2,1)S(1)}, bf16[16,4608]{1,0:T(8,128)(2,1)S(1)}, u32[]{:S(2)}, u32[]{:S(2)}) collective-permute-start(bf16[16,4608]{1,0:T(8,128)(2,1)S(1)} %get-tuple-element.59), channel_id=1, source_target_pairs={{0,1},{1,0},{2,3},{3,2},{4,5},{5,4},{6,7},{7,6},{8,9},{9,8},{10,11... | collective-permute-start | bytes 442376 | tf_op jit(solution)/shard_map/ppermute | solution.py:409
  35.5 8.2 %collective-permute-start.10 = (bf16[16,4608]{1,0:T(8,128)(2,1)S(1)}, bf16[16,4608]{1,0:T(8,128)(2,1)S(1)}, u32[]{:S(2)}, u32[]{:S(2)}) collective-permute-start(bf16[16,4608]{1,0:T(8,128)(2,1)S(1)} %get-tuple-element.60), channel_id=1, source_target_pairs={{0,3},{1,2},{2,1},{3,0},{4,7},{5,6},{6,5},{7,4},{8,11},{9,10},{10,... | collective-permute-start | bytes 442376 | tf_op jit(solution)/shard_map/ppermute | solution.py:409

commit v5 on v4

--- a/solution.py
+++ b/solution.py
@@ -65,8 +65,8 @@
 
 def own_kernel(
     seqs, ups, heads, group, kv_heads,
-    pages_ref, lengths_ref, q_ref, first_k, last_k, first_v, v_hbm, w_hbm,
-    num_ref, tot_ref, w_ref, last_v, sem, tail_sem,
+    pages_ref, lengths_ref, q_ref, first_k, last_k, first_v, v_hbm,
+    num_ref, tot_ref, last_v, tail_sem,
 ):
     page_len, head_dim = first_v.shape[2:]
     early, late = first_k.shape[0], last_k.shape[0]
@@ -80,8 +80,6 @@
 
     tail(lambda copy: copy.start())
     width = kv_heads * page_len
-    prefetch = pltpu.make_async_copy(w_hbm, w_ref, sem)
-    prefetch.start()
     column = lax.broadcasted_iota(jnp.int32, (heads, width), 1)
     row = lax.broadcasted_iota(jnp.int32, (heads, width), 0)
     mine = (column // page_len) == (row // group)
@@ -112,10 +110,9 @@
 
         lax.fori_loop(0, part // unroll, block, 0)
         done += part
-    prefetch.wait()
-
-
-def own_terms(q, pages, own_k, first_v, values, lengths, o_weight):
+
+
+def own_terms(q, pages, own_k, first_v, values, lengths):
     seqs, _, head_dim = q.shape
     _, kv_heads, page_len, _ = first_v.shape
     count, late = pages.shape[0], own_k[1].shape[0]
@@ -123,20 +120,18 @@
     heads = -(-q.shape[1] // 8) * 8
     q = jnp.pad(q, ((0, 0), (0, heads - q.shape[1]), (0, 0))).reshape(seqs * heads, head_dim)
     out = jax.ShapeDtypeStruct((heads * seqs, head_dim), jnp.float32)
-    num, tot, w = pl.pallas_call(
+    return pl.pallas_call(
         functools.partial(own_kernel, seqs, count // seqs, heads, group, kv_heads),
-        out_shape=(out, out, jax.ShapeDtypeStruct(o_weight.shape, o_weight.dtype)),
-        in_specs=[SMEM, SMEM] + [VMEM] * 4 + [HBM, HBM],
-        out_specs=(VMEM, VMEM, VMEM),
+        out_shape=(out, out),
+        in_specs=[SMEM, SMEM] + [VMEM] * 4 + [HBM],
+        out_specs=(VMEM, VMEM),
         scratch_shapes=[
             pltpu.VMEM((late, kv_heads, page_len, head_dim), values.dtype),
-            pltpu.SemaphoreType.DMA,
             pltpu.SemaphoreType.DMA((late,)),
         ],
         compiler_params=pltpu.CompilerParams(vmem_limit_bytes=8 * MIB),
         name="own_pages",
-    )(pages, lengths, q, *own_k, first_v, in_hbm(values), in_hbm(o_weight))
-    return (num, tot), w
+    )(pages, lengths, q, *own_k, first_v, in_hbm(values))
 
 
 def shared_places(me, cap, page_count, hot_ref, lanes):
@@ -401,8 +396,10 @@
     for k, b in zip(range(1, chips), sent):
         blocks.append(lax.ppermute(b, "pages", back_perm[k]))
     queries, rest_num = lax.optimization_barrier((queries, rest_num))
-    own, weight = own_terms(queries, pages, (first_k, last_k), first_v, values, lengths, o_weight)
-    parts = project(blocks, near, (rest_num, rest_tot), own, weight, ways)
+    own = own_terms(
+        queries, pages, (first_k, last_k), first_v, values, lengths
+    )
+    parts = project(blocks, near, (rest_num, rest_tot), own, o_weight, ways)
     arrived = [parts[0]]
     for k in row_order(ways):
         pairs = [(i, i ^ k if ways & (ways - 1) == 0 else (i + k) % ways) for i in range(ways)]

time: 45.1 us -> 46.7 us (1.035)
  waiting for transfers between devices: 10.5 us -> 12.4 us
    ppermute x3, waiting for transfers between devices: 7.96 us -> 9.85 us  [layer(): arrived.append(lax.ppermute(parts[k], 'heads', pairs))]
  transfers between devices with their start and end apart: 11 -> 11, of which waited for: 2 -> 3; matrix products, arithmetic and copies ran while one was open for 0% -> 0% of each run, Pallas kernels for 23% -> 22%
where the time goes in v5:
time: 46.7 us; the launch traced here: 46.5 us
  Pallas kernels  20.8 us (45%)
  starting transfers between devices  13.1 us (28%)
  waiting for transfers between devices  12.4 us (27%)
    pallas_call x2, Pallas kernels, hot_terms(): pl.pallas_call(functools.partial(hot_kernel, sources, halves, seqs, heads...  9.97 us
    ppermute x3, waiting for transfers between devices, layer(): arrived.append(lax.ppermute(parts[k], 'heads', pairs))  9.85 us
    pallas_call x1, Pallas kernels, own_terms(): pl.pallas_call(functools.partial(own_kernel, seqs, count // seqs, heads,...  6.31 us
    ppermute x3, starting transfers between devices, layer(): arrived.append(lax.ppermute(parts[k], 'heads', pairs))  4.45 us
    ppermute x3, starting transfers between devices, layer(): far_q.append(lax.ppermute(queries, 'pages', out_perm[k]))  4.43 us
    ppermute x3, starting transfers between devices, layer(): blocks.append(lax.ppermute(b, 'pages', back_perm[k]))  3.55 us
    ppermute x3, waiting for transfers between devices, layer(): far_q.append(lax.ppermute(queries, 'pages', out_perm[k]))  2.58 us
    pallas_call x1, Pallas kernels, project(): pl.pallas_call(functools.partial(project_kernel, len(blocks), seqs, heads...  2.03 us
  transfers between devices with their start and end apart: 11, of which 3 were waited for; matrix products, arithmetic and copies ran while one was open for 0% of the time, Pallas kernels for 22%

profile of v5, /device:TPU:0, one launch (start us, length us, event | category | flops | bytes accessed | tf_op | source)
XLA Modules:
  0.0 46.5 jit_solution(5883683260945834894)
XLA Ops:
  0.0 0.0 copy-start
  0.0 0.0 copy-start.3
  0.0 0.0 copy-start.4
  0.0 0.0 copy-start.2
  0.0 1.6 %lead_pages.1 = (bf16[8,4,128,128]{3,2,1,0:T(8,128)(2,1)S(1)}, bf16[8,4,128,128]{3,2,1,0:T(8,128)(2,1)S(1)}) custom-call(bf16[72,4,128,128]{3,2,1,0:T(8,128)(2,1)} %refs_1_.3, bf16[72,4,128,128]{3,2,1,0:T(8,128)(2,1)} %v_hbm.1), custom_call_target="tpu_custom_call" | custom-call | tf_op jit(solution)/shard_map/lead_pages/pallas_call | solution.py:55
  1.6 0.6 %collective-permute-start.3 = (bf16[8,4,128,128]{3,2,1,0:T(8,128)(2,1)S(1)}, bf16[8,4,128,128]{3,2,1,0:T(8,128)(2,1)S(1)}, u32[]{:S(2)}, u32[]{:S(2)}) collective-permute-start(bf16[8,4,128,128]{3,2,1,0:T(8,128)(2,1)S(1)} %get-tuple-element.32.refs_3_.refs_7_), channel_id=1, source_target_pairs={{0,4},{4,0},{8,12},{12,8},{16,20},{20,16},{24,28},{28,24},{1,5},{5... | collective-permute-start | bytes 3145736 | tf_op jit(solution)/shard_map/ppermute | solution.py:375
  2.2 0.1 collective-permute-start.4
  2.3 0.0 copy-done
  2.3 2.9 %collective-permute-start = (bf16[64,8,128]{2,1,0:T(8,128)(2,1)S(1)}, bf16[64,8,128]{2,1,0:T(8,128)(2,1)S(1)}, u32[]{:S(2)}, u32[]{:S(2)}) collective-permute-start(bf16[64,8,128]{2,1,0:T(8,128)(2,1)S(1)} %copy-done), channel_id=1, source_target_pairs={{0,8},{4,12},{8,0},{12,4},{16,24},{20,28},{24,16},{28,20},{1,9},{5... | collective-permute-start | bytes 393224 | tf_op jit(solution)/shard_map/ppermute | solution.py:373
  5.2 1.5 %collective-permute-start.1 = (bf16[64,8,128]{2,1,0:T(8,128)(2,1)S(1)}, bf16[64,8,128]{2,1,0:T(8,128)(2,1)S(1)}, u32[]{:S(2)}, u32[]{:S(2)}) collective-permute-start(bf16[64,8,128]{2,1,0:T(8,128)(2,1)S(1)} %copy-done), channel_id=1, source_target_pairs={{0,16},{4,20},{8,24},{12,28},{16,0},{20,4},{24,8},{28,12},{1,17},{... | collective-permute-start | bytes 393224 | tf_op jit(solution)/shard_map/ppermute | solution.py:373
  6.7 0.0 collective-permute-start.2
  6.7 0.0 copy-done.3
  6.7 0.0 copy-done.4
  6.7 0.0 copy-done.2
  6.7 3.9 %hot_pages.2 = (f32[512,128]{1,0:T(8,128)S(1)}, f32[512,128]{1,0:T(8,128)S(1)}, bf16[48,4,128,128]{3,2,1,0:T(8,128)(2,1)S(1)}) custom-call(s32[1,64]{1,0:T(1,128)S(1)} %bitcast.21, s32[4,128]{1,0:T(4,128)S(1)} %bitcast.16, s32[64]{0:T(128)S(1)} %bitcast.18, bf16[72,4,128,128]{3,2,1,0:T(8,128)(2,1)} %refs_1_.3, bf16[512,128]{1,0:T(8,128)(2,1)S(1)} %bitcast.10, ...), custom_call_target="tpu_custom_call" | custom-call | tf_op jit(solution)/shard_map/hot_pages/pallas_call | solution.py:260
  10.6 0.0 collective-permute-done
  10.6 2.6 %collective-permute-done.1 = bf16[64,8,128]{2,1,0:T(8,128)(2,1)S(1)} collective-permute-done((bf16[64,8,128]{2,1,0:T(8,128)(2,1)S(1)}, bf16[64,8,128]{2,1,0:T(8,128)(2,1)S(1)}, u32[]{:S(2)}, u32[]{:S(2)}) %collective-permute-start.1) | collective-permute-done | bytes 131104 | tf_op jit(solution)/shard_map/ppermute | solution.py:373
  13.2 0.0 collective-permute-done.2
  13.2 0.0 collective-permute-done.3.refs_9_
  13.2 0.0 collective-permute-done.4.refs_10_
  13.2 0.0 copy-start.5
  13.2 0.0 slice-start
  13.2 0.0 slice-start.1
  13.2 6.1 %hot_pages.3 = (bf16[528,128]{1,0:T(8,128)(2,1)S(1)}, bf16[528,128]{1,0:T(8,128)(2,1)S(1)}, bf16[528,128]{1,0:T(8,128)(2,1)S(1)}, f32[512,128]{1,0:T(8,128)S(1)}...) custom-call(s32[1,64]{1,0:T(1,128)S(1)} %bitcast.22, ...), custom_call_target="tpu_custom_call" | custom-call | tf_op jit(solution)/shard_map/hot_pages/pallas_call | solution.py:260
  19.3 1.3 %collective-permute-start.5 = (bf16[528,128]{1,0:T(8,128)(2,1)S(1)}, bf16[528,128]{1,0:T(8,128)(2,1)S(1)}, u32[]{:S(2)}, u32[]{:S(2)}) collective-permute-start(bf16[528,128]{1,0:T(8,128)(2,1)S(1)} %get-tuple-element.41), channel_id=1, source_target_pairs={{8,0},{12,4},{0,8},{4,12},{24,16},{28,20},{16,24},{20,28},{9,1},{1... | collective-permute-start | bytes 405512 | tf_op jit(solution)/shard_map/ppermute | solution.py:397
  20.6 0.8 %collective-permute-start.6 = (bf16[528,128]{1,0:T(8,128)(2,1)S(1)}, bf16[528,128]{1,0:T(8,128)(2,1)S(1)}, u32[]{:S(2)}, u32[]{:S(2)}) collective-permute-start(bf16[528,128]{1,0:T(8,128)(2,1)S(1)} %get-tuple-element.42), channel_id=1, source_target_pairs={{16,0},{20,4},{24,8},{28,12},{0,16},{4,20},{8,24},{12,28},{17,1},{... | collective-permute-start | bytes 405512 | tf_op jit(solution)/shard_map/ppermute | solution.py:397
  21.4 1.4 %collective-permute-start.7 = (bf16[528,128]{1,0:T(8,128)(2,1)S(1)}, bf16[528,128]{1,0:T(8,128)(2,1)S(1)}, u32[]{:S(2)}, u32[]{:S(2)}) collective-permute-start(bf16[528,128]{1,0:T(8,128)(2,1)S(1)} %get-tuple-element.43), channel_id=1, source_target_pairs={{24,0},{28,4},{16,8},{20,12},{8,16},{12,20},{0,24},{4,28},{25,1},{... | collective-permute-start | bytes 405512 | tf_op jit(solution)/shard_map/ppermute | solution.py:397
  22.9 0.0 copy-done.5
  22.9 0.0 slice-start.2
  22.9 6.3 %own_pages.1 = (f32[512,128]{1,0:T(8,128)S(1)}, f32[512,128]{1,0:T(8,128)S(1)}) custom-call(s32[64]{0:T(128)S(1)} %bitcast.20, s32[64]{0:T(128)S(1)} %copy-done.5, bf16[512,128]{1,0:T(8,128)(2,1)S(1)} %bitcast.12, bf16[48,4,128,128]{3,2,1,0:T(8,128)(2,1)S(1)} %get-tuple-element.48.first_k, bf16[16,4,128,128]{3,2,1,0:T(8,128)(2,1)S(1)} %get-tuple-element.49.last_k, ...), custom_call_target="tpu_custom_call" | custom-call | tf_op jit(solution)/shard_map/own_pages/pallas_call | solution.py:123
  29.2 0.0 copy-start.6
  29.2 0.0 copy-start.1
  29.2 0.0 collective-permute-done.5.refs_0_
  29.2 0.0 collective-permute-done.6.refs_1_
  29.2 0.0 collective-permute-done.7.refs_2_
  29.3 0.0 slice-done
  29.3 0.0 slice-done.1
  29.3 0.0 slice-done.2
  29.3 2.0 %project.1 = (f32[16,4608]{1,0:T(8,128)S(1)}, bf16[16,4608]{1,0:T(8,128)(2,1)S(1)}, bf16[16,4608]{1,0:T(8,128)(2,1)S(1)}, bf16[16,4608]{1,0:T(8,128)(2,1)S(1)}) custom-call(bf16[528,128]{1,0:T(8,128)(2,1)S(1)} %collective-permute-done.5.refs_0_, bf16[528,128]{1,0:T(8,128)(2,1)S(1)} %collective-permute-done.6.refs_1_, ...), custom_call_target="tpu_custom_call" | custom-call | tf_op jit(solution)/shard_map/project/pallas_call | solution.py:327
  31.3 3.7 %collective-permute-start.10 = (bf16[16,4608]{1,0:T(8,128)(2,1)S(1)}, bf16[16,4608]{1,0:T(8,128)(2,1)S(1)}, u32[]{:S(2)}, u32[]{:S(2)}) collective-permute-start(bf16[16,4608]{1,0:T(8,128)(2,1)S(1)} %get-tuple-element.58), channel_id=1, source_target_pairs={{0,3},{1,2},{2,1},{3,0},{4,7},{5,6},{6,5},{7,4},{8,11},{9,10},{10,... | collective-permute-start | bytes 442376 | tf_op jit(solution)/shard_map/ppermute | solution.py:406
  35.0 0.0 collective-permute-start.8
  35.0 0.8 %collective-permute-start.9 = (bf16[16,4608]{1,0:T(8,128)(2,1)S(1)}, bf16[16,4608]{1,0:T(8,128)(2,1)S(1)}, u32[]{:S(2)}, u32[]{:S(2)}) collective-permute-start(bf16[16,4608]{1,0:T(8,128)(2,1)S(1)} %get-tuple-element.57), channel_id=1, source_target_pairs={{0,1},{1,0},{2,3},{3,2},{4,5},{5,4},{6,7},{7,6},{8,9},{9,8},{10,11... | collective-permute-start | bytes 442376 | tf_op jit(solution)/shard_map/ppermute | solution.py:406
  35.8 0.0 copy-done.6
  35.8 4.1 %collective-permute-done.10.refs_3_ = bf16[16,4608]{1,0:T(8,128)(2,1)S(1)} collective-permute-done((bf16[16,4608]{1,0:T(8,128)(2,1)S(1)}, bf16[16,4608]{1,0:T(8,128)(2,1)S(1)}, u32[]{:S(2)}, u32[]{:S(2)}) %collective-permute-start.10) | collective-permute-done | bytes 147488 | tf_op jit(solution)/shard_map/ppermute | solution.py:406
  39.9 5.8 %collective-permute-done.8.refs_1_ = bf16[16,4608]{1,0:T(8,128)(2,1)S(1)} collective-permute-done((bf16[16,4608]{1,0:T(8,128)(2,1)S(1)}, bf16[16,4608]{1,0:T(8,128)(2,1)S(1)}, u32[]{:S(2)}, u32[]{:S(2)}) %collective-permute-start.8) | collective-permute-done | bytes 147488 | tf_op jit(solution)/shard_map/ppermute | solution.py:406
  45.6 0.0 collective-permute-done.9.refs_2_
  45.6 0.0 copy-done.1
  45.6 0.9 %finish.1 = bf16[16,4608]{1,0:T(8,128)(2,1)} custom-call(f32[16,4608]{1,0:T(8,128)S(1)} %get-tuple-element.55.refs_0_, bf16[16,4608]{1,0:T(8,128)(2,1)S(1)} %collective-permute-done.8.refs_1_, bf16[16,4608]{1,0:T(8,128)(2,1)S(1)} %collective-permute-done.9.refs_2_, bf16[16,4608]{1,0:T(8,128)(2,1)S(1)} %collective-permute-done.10.refs_3_, ...), custom_call_target="tpu_custom_call" | custom-call | tf_op jit(solution)/shard_map/finish/pallas_call | solution.py:349
  (2 shorter events, 0.0 us)
Async XLA Ops:
  0.0 2.3 %copy-start = (bf16[64,8,128]{2,1,0:T(8,128)(2,1)S(1)}, bf16[64,8,128]{2,1,0:T(8,128)(2,1)}, u32[]{:S(2)}) copy-start(bf16[64,8,128]{2,1,0:T(8,128)(2,1)} %param.10) | copy-start | bytes 393220
  0.0 6.7 %copy-start.3 = (s32[64,1]{0,1:T(1,128)S(1)}, s32[64,1]{0,1:T(1,128)}, u32[]{:S(2)}) copy-start(s32[64,1]{0,1:T(1,128)} %param.15) | copy-start | bytes 772
  0.0 6.7 %copy-start.4 = (s32[64]{0:T(128)S(1)}, s32[64]{0:T(128)}, u32[]{:S(2)}) copy-start(s32[64]{0:T(128)} %param.13) | copy-start | bytes 772
  0.0 6.7 %copy-start.2 = (s32[512]{0:T(512)S(1)}, s32[512]{0:T(512)}, u32[]{:S(2)}) copy-start(s32[512]{0:T(512)} %param.14) | copy-start | bytes 6148
  1.6 11.6 %collective-permute-start.3 = (bf16[8,4,128,128]{3,2,1,0:T(8,128)(2,1)S(1)}, bf16[8,4,128,128]{3,2,1,0:T(8,128)(2,1)S(1)}, u32[]{:S(2)}, u32[]{:S(2)}) collective-permute-start(bf16[8,4,128,128]{3,2,1,0:T(8,128)(2,1)S(1)} %get-tuple-element.32.refs_3_.refs_7_), channel_id=1, source_target_pairs={{0,4},{4,0},{8,12},{12,8},{16,20},{20,16},{24,28},{28,24},{1,5},{5... | collective-permute-start | bytes 3145736 | tf_op jit(solution)/shard_map/ppermute | solution.py:375
  2.2 11.0 %collective-permute-start.4 = (bf16[8,4,128,128]{3,2,1,0:T(8,128)(2,1)S(1)}, bf16[8,4,128,128]{3,2,1,0:T(8,128)(2,1)S(1)}, u32[]{:S(2)}, u32[]{:S(2)}) collective-permute-start(bf16[8,4,128,128]{3,2,1,0:T(8,128)(2,1)S(1)} %get-tuple-element.33.refs_4_.refs_8_), channel_id=1, source_target_pairs={{0,4},{4,0},{8,12},{12,8},{16,20},{20,16},{24,28},{28,24},{1,5},{5... | collective-permute-start | bytes 3145736 | tf_op jit(solution)/shard_map/ppermute | solution.py:375
  2.3 8.3 %collective-permute-start = (bf16[64,8,128]{2,1,0:T(8,128)(2,1)S(1)}, bf16[64,8,128]{2,1,0:T(8,128)(2,1)S(1)}, u32[]{:S(2)}, u32[]{:S(2)}) collective-permute-start(bf16[64,8,128]{2,1,0:T(8,128)(2,1)S(1)} %copy-done), channel_id=1, source_target_pairs={{0,8},{4,12},{8,0},{12,4},{16,24},{20,28},{24,16},{28,20},{1,9},{5... | collective-permute-start | bytes 393224 | tf_op jit(solution)/shard_map/ppermute | solution.py:373
  5.2 8.0 %collective-permute-start.1 = (bf16[64,8,128]{2,1,0:T(8,128)(2,1)S(1)}, bf16[64,8,128]{2,1,0:T(8,128)(2,1)S(1)}, u32[]{:S(2)}, u32[]{:S(2)}) collective-permute-start(bf16[64,8,128]{2,1,0:T(8,128)(2,1)S(1)} %copy-done), channel_id=1, source_target_pairs={{0,16},{4,20},{8,24},{12,28},{16,0},{20,4},{24,8},{28,12},{1,17},{... | collective-permute-start | bytes 393224 | tf_op jit(solution)/shard_map/ppermute | solution.py:373
  6.7 6.5 %collective-permute-start.2 = (bf16[64,8,128]{2,1,0:T(8,128)(2,1)S(1)}, bf16[64,8,128]{2,1,0:T(8,128)(2,1)S(1)}, u32[]{:S(2)}, u32[]{:S(2)}) collective-permute-start(bf16[64,8,128]{2,1,0:T(8,128)(2,1)S(1)} %copy-done), channel_id=1, source_target_pairs={{0,24},{4,28},{8,16},{12,20},{16,8},{20,12},{24,0},{28,4},{1,25},{... | collective-permute-start | bytes 393224 | tf_op jit(solution)/shard_map/ppermute | solution.py:373
  13.2 9.7 %copy-start.5 = (s32[64]{0:T(128)S(1)}, s32[64]{0:T(128)}, u32[]{:S(2)}) copy-start(s32[64]{0:T(128)} %lengths_ref.1) | copy-start | bytes 772
  13.2 16.1 %slice-start = ((s8[9437184]{0:T(1024)(128)(4,1)}), s8[1048576]{0:T(1024)(128)(4,1)S(1)}, s32[]{:S(2)}) async-start(s8[9437184]{0:T(1024)(128)(4,1)} %bitcast.8), calls=%async_computation | async-start | bytes 2097152
  13.2 16.0 %slice-start.1 = ((s8[9437184]{0:T(1024)(128)(4,1)}), s8[4194304]{0:T(1024)(128)(4,1)S(1)}, s32[]{:S(2)}) async-start(s8[9437184]{0:T(1024)(128)(4,1)} %bitcast.8), calls=%async_computation.1 | async-start | bytes 8388608
  19.3 9.9 %collective-permute-start.5 = (bf16[528,128]{1,0:T(8,128)(2,1)S(1)}, bf16[528,128]{1,0:T(8,128)(2,1)S(1)}, u32[]{:S(2)}, u32[]{:S(2)}) collective-permute-start(bf16[528,128]{1,0:T(8,128)(2,1)S(1)} %get-tuple-element.41), channel_id=1, source_target_pairs={{8,0},{12,4},{0,8},{4,12},{24,16},{28,20},{16,24},{20,28},{9,1},{1... | collective-permute-start | bytes 405512 | tf_op jit(solution)/shard_map/ppermute | solution.py:397
  20.6 8.6 %collective-permute-start.6 = (bf16[528,128]{1,0:T(8,128)(2,1)S(1)}, bf16[528,128]{1,0:T(8,128)(2,1)S(1)}, u32[]{:S(2)}, u32[]{:S(2)}) collective-permute-start(bf16[528,128]{1,0:T(8,128)(2,1)S(1)} %get-tuple-element.42), channel_id=1, source_target_pairs={{16,0},{20,4},{24,8},{28,12},{0,16},{4,20},{8,24},{12,28},{17,1},{... | collective-permute-start | bytes 405512 | tf_op jit(solution)/shard_map/ppermute | solution.py:397
  21.4 7.8 %collective-permute-start.7 = (bf16[528,128]{1,0:T(8,128)(2,1)S(1)}, bf16[528,128]{1,0:T(8,128)(2,1)S(1)}, u32[]{:S(2)}, u32[]{:S(2)}) collective-permute-start(bf16[528,128]{1,0:T(8,128)(2,1)S(1)} %get-tuple-element.43), channel_id=1, source_target_pairs={{24,0},{28,4},{16,8},{20,12},{8,16},{12,20},{0,24},{4,28},{25,1},{... | collective-permute-start | bytes 405512 | tf_op jit(solution)/shard_map/ppermute | solution.py:397
  22.9 6.4 %slice-start.2 = ((s8[9437184]{0:T(1024)(128)(4,1)}), s8[4194304]{0:T(1024)(128)(4,1)S(1)}, s32[]{:S(2)}) async-start(s8[9437184]{0:T(1024)(128)(4,1)} %bitcast.8), calls=%async_computation.2 | async-start | bytes 8388608
  29.2 6.6 %copy-start.6 = (f32[4608]{0:T(1024)S(1)}, f32[4608]{0:T(1024)}, u32[]{:S(2)}) copy-start(f32[4608]{0:T(1024)} %param.19) | copy-start | bytes 55300
  29.2 16.4 %copy-start.1 = (bf16[16,4608]{1,0:T(8,128)(2,1)S(1)}, bf16[16,4608]{1,0:T(8,128)(2,1)}, u32[]{:S(2)}) copy-start(bf16[16,4608]{1,0:T(8,128)(2,1)} %refs_4_.1) | copy-start | bytes 442372
  31.3 8.6 %collective-permute-start.10 = (bf16[16,4608]{1,0:T(8,128)(2,1)S(1)}, bf16[16,4608]{1,0:T(8,128)(2,1)S(1)}, u32[]{:S(2)}, u32[]{:S(2)}) collective-permute-start(bf16[16,4608]{1,0:T(8,128)(2,1)S(1)} %get-tuple-element.58), channel_id=1, source_target_pairs={{0,3},{1,2},{2,1},{3,0},{4,7},{5,6},{6,5},{7,4},{8,11},{9,10},{10,... | collective-permute-start | bytes 442376 | tf_op jit(solution)/shard_map/ppermute | solution.py:406
  35.0 10.7 %collective-permute-start.8 = (bf16[16,4608]{1,0:T(8,128)(2,1)S(1)}, bf16[16,4608]{1,0:T(8,128)(2,1)S(1)}, u32[]{:S(2)}, u32[]{:S(2)}) collective-permute-start(bf16[16,4608]{1,0:T(8,128)(2,1)S(1)} %get-tuple-element.56), channel_id=1, source_target_pairs={{0,2},{1,3},{2,0},{3,1},{4,6},{5,7},{6,4},{7,5},{8,10},{9,11},{10,... | collective-permute-start | bytes 442376 | tf_op jit(solution)/shard_map/ppermute | solution.py:406
  35.0 10.7 %collective-permute-start.9 = (bf16[16,4608]{1,0:T(8,128)(2,1)S(1)}, bf16[16,4608]{1,0:T(8,128)(2,1)S(1)}, u32[]{:S(2)}, u32[]{:S(2)}) collective-permute-start(bf16[16,4608]{1,0:T(8,128)(2,1)S(1)} %get-tuple-element.57), channel_id=1, source_target_pairs={{0,1},{1,0},{2,3},{3,2},{4,5},{5,4},{6,7},{7,6},{8,9},{9,8},{10,11... | collective-permute-start | bytes 442376 | tf_op jit(solution)/shard_map/ppermute | solution.py:406
